TPU v7x, 32 devices: a whole 2x2x4 slice. The times are simulated.
32 devices in a mesh: seq: 8 (over y, x, core), head: 4 (over z).
Axes of the slice: x: 2, y: 2, z: 4, core: 2. Of those that a mesh axis runs over, the one named last changes fastest.
Arguments:
- queries: bfloat16 [4096, 1024], P('seq', 'head'), may hold values from -16 to 16
- keys: bfloat16 [4096, 1024], P('seq', 'head'), may hold values from -16 to 16
- values: bfloat16 [4096, 1024], P('seq', 'head'), may hold values from -6 to 6
- segment_ids: int32 [4096], P('seq'), may hold values from 0 to 4, never falling along the last dimension, each value on 1 to 1024 neighbouring positions
- out_weight: bfloat16 [1024, 5120], P('head'), may hold values from -0.25 to 0.25
Outputs:
- mixed: bfloat16 [4096, 5120], P('seq', 'head')
Inputs may be any that keep to these rules, and one draw needn't show every extreme that they name: `segment_ids`: segment numbers never fall along the sequence; a segment holds at most 1024 tokens.
All inputs are finite; a program needn't handle non-finite values.
Results may differ from a plain program's by a relative error of at most 0.02.
Values may be sent and summed in bfloat16 or wider, within the bound.
No kernel may reach another device: no remote copies, remote signals or barrier semaphores. Data moves between devices by JAX's collectives and lax.ppermute only.
A program may use at most 64 MiB of HBM per device.

v0:
```python
import jax
import jax.numpy as jnp
from jax import lax
from jax.sharding import PartitionSpec as P

HEAD_DEV = 2
SPAN = 2


def shifted(block, axis, distance):
    devices = range(lax.axis_size(axis))
    route = [(i - distance, i) for i in devices if i - distance in devices]
    return lax.ppermute(block, axis, route)


def attend(query, query_marks, key_rows, value_rows, key_marks):
    rows = query.shape[0]
    head_size = query.shape[1] // HEAD_DEV
    query_heads = query.reshape(rows, HEAD_DEV, head_size)
    key_heads = key_rows.reshape(key_rows.shape[0], HEAD_DEV, head_size)
    value_heads = value_rows.reshape(value_rows.shape[0], HEAD_DEV, head_size)
    allowed = (query_marks[:, None] == key_marks[None, :])[None]
    scores = jnp.einsum(
        "qhd,khd->hqk", query_heads, key_heads, preferred_element_type=jnp.float32
    ) * head_size ** (-0.5)
    scores = jnp.where(allowed, scores, -1e30)
    peak = jnp.max(scores, axis=2)
    weights = jnp.where(allowed, jnp.exp(scores - peak[:, :, None]), 0.0)
    total = jnp.sum(weights, axis=2)
    summed = jnp.einsum(
        "hqk,khd->qhd",
        weights.astype(jnp.bfloat16),
        value_heads,
        preferred_element_type=jnp.float32,
    )
    return (summed, peak, total)


def attend_block(query, query_marks, key_rows, value_rows, key_marks):
    return attend(query, query_marks, key_rows, value_rows, key_marks)


def combine(first, second):
    peak = jnp.maximum(first[1], second[1])
    scale_one = jnp.exp(first[1] - peak)
    scale_two = jnp.exp(second[1] - peak)
    summed = (
        first[0] * jnp.transpose(scale_one)[:, :, None]
        + second[0] * jnp.transpose(scale_two)[:, :, None]
    )
    return (summed, peak, first[2] * scale_one + second[2] * scale_two)


def pull_keys(query, marks, key_rows, value_rows, offset):
    far_keys, far_values, far_marks = shifted((key_rows, value_rows, marks), "seq", offset)
    return attend_block(query, marks, far_keys, far_values, far_marks)


def shards(queries, keys, values, segment_ids, out_weight):
    marks = segment_ids + 1
    state = attend_block(queries, marks, keys, values, marks)
    for distance in range(1, SPAN + 1):
        for sign in (1, -1):
            state = combine(state, pull_keys(queries, marks, keys, values, sign * distance))
    summed, peak, total = state
    attended = (
        (summed / jnp.transpose(total)[:, :, None])
        .reshape(queries.shape[0], queries.shape[1])
        .astype(jnp.bfloat16)
    )
    term = jnp.dot(attended, out_weight, preferred_element_type=jnp.float32)
    mixed = lax.psum_scatter(term.astype(jnp.bfloat16), "head", scatter_dimension=1, tiled=True)
    return mixed


def solution(mesh):
    placed = (P("seq", "head"), P("seq", "head"), P("seq", "head"), P("seq"), P("head", None))
    return jax.shard_map(
        shards, mesh=mesh, in_specs=placed, out_specs=P("seq", "head"), check_vma=False
    )
```

profile of v0, /device:TPU:6, one launch (start us, length us, event | category | flops | bytes accessed | tf_op | source)
XLA Modules:
  0.0 185.0 jit_solution(15955651120348622342)
XLA Ops:
  6.5 0.8 broadcast_add_fusion
  7.4 1.9 %collective-permute-start = (s32[512]{0:T(512)S(1)}, s32[512]{0:T(512)S(1)}, u32[]{:S(2)}, u32[]{:S(2)}) collective-permute-start(s32[512]{0:T(512)S(1)} %broadcast_add_fusion), channel_id=1, source_target_pairs={{0,4},{4,8},{8,12},{12,16},{16,20},{20,24},{24,28},{1,5},{5,9},{9,... | collective-permute-start | bytes 6152 | tf_op jit(solution)/shard_map/ppermute | solution.py:13
  9.3 3.6 %collective-permute-start.3 = (s32[512]{0:T(512)S(1)}, s32[512]{0:T(512)S(1)}, u32[]{:S(2)}, u32[]{:S(2)}) collective-permute-start(s32[512]{0:T(512)S(1)} %broadcast_add_fusion), channel_id=1, source_target_pairs={{4,0},{8,4},{12,8},{16,12},{20,16},{24,20},{28,24},{5,1},{9,5},{13... | collective-permute-start | bytes 6152 | tf_op jit(solution)/shard_map/ppermute | solution.py:13
  12.9 1.3 collective-permute-start.6
  14.2 4.5 %collective-permute-start.9 = (s32[512]{0:T(512)S(1)}, s32[512]{0:T(512)S(1)}, u32[]{:S(2)}, u32[]{:S(2)}) collective-permute-start(s32[512]{0:T(512)S(1)} %broadcast_add_fusion), channel_id=1, source_target_pairs={{8,0},{12,4},{16,8},{20,12},{24,16},{28,20},{9,1},{13,5},{17,9},{2... | collective-permute-start | bytes 6152 | tf_op jit(solution)/shard_map/ppermute | solution.py:13
  18.8 1.8 copy.26
  20.6 1.9 %collective-permute-start.1 = (bf16[512,256]{0,1:T(8,128)(2,1)}, bf16[512,256]{0,1:T(8,128)(2,1)}, u32[]{:S(2)}, u32[]{:S(2)}) collective-permute-start(bf16[512,256]{0,1:T(8,128)(2,1)} %copy.26), channel_id=1, source_target_pairs={{0,4},{4,8},{8,12},{12,16},{16,20},{20,24},{24,28},{1,5},{5,9},{9,... | collective-permute-start | bytes 786440 | tf_op jit(solution)/shard_map/ppermute | solution.py:13
  22.5 1.8 copy.55
  24.3 0.0 collective-permute-done
  24.3 1.4 collective-permute-start.7
  25.8 0.0 collective-permute-done.3
  25.8 4.3 %collective-permute-start.4 = (bf16[512,256]{0,1:T(8,128)(2,1)}, bf16[512,256]{0,1:T(8,128)(2,1)S(1)}, u32[]{:S(2)}, u32[]{:S(2)}) collective-permute-start(bf16[512,256]{0,1:T(8,128)(2,1)} %copy.26), channel_id=1, source_target_pairs={{4,0},{8,4},{12,8},{16,12},{20,16},{24,20},{28,24},{5,1},{9,5},{13... | collective-permute-start | bytes 786440 | tf_op jit(solution)/shard_map/ppermute | solution.py:13
  30.0 0.0 collective-permute-done.6
  30.1 5.2 %collective-permute-start.10 = (bf16[512,256]{0,1:T(8,128)(2,1)}, bf16[512,256]{0,1:T(8,128)(2,1)S(1)}, u32[]{:S(2)}, u32[]{:S(2)}) collective-permute-start(bf16[512,256]{0,1:T(8,128)(2,1)} %copy.26), channel_id=1, source_target_pairs={{8,0},{12,4},{16,8},{20,12},{24,16},{28,20},{9,1},{13,5},{17,9},{2... | collective-permute-start | bytes 786440 | tf_op jit(solution)/shard_map/ppermute | solution.py:13
  35.2 0.0 collective-permute-done.9
  35.2 1.9 %collective-permute-start.2 = (bf16[512,256]{1,0:T(8,128)(2,1)}, bf16[512,256]{1,0:T(8,128)(2,1)}, u32[]{:S(2)}, u32[]{:S(2)}) collective-permute-start(bf16[512,256]{1,0:T(8,128)(2,1)} %param.7), channel_id=1, source_target_pairs={{0,4},{4,8},{8,12},{12,16},{16,20},{20,24},{24,28},{1,5},{5,9},{9,... | collective-permute-start | bytes 786440 | tf_op jit(solution)/shard_map/ppermute | solution.py:13
  37.2 0.9 broadcast_compare_fusion.3
  38.1 1.7 fusion
  39.7 0.0 collective-permute-done.1
  39.7 3.6 %collective-permute-start.5 = (bf16[512,256]{1,0:T(8,128)(2,1)}, bf16[512,256]{1,0:T(8,128)(2,1)}, u32[]{:S(2)}, u32[]{:S(2)}) collective-permute-start(bf16[512,256]{1,0:T(8,128)(2,1)} %param.7), channel_id=1, source_target_pairs={{4,0},{8,4},{12,8},{16,12},{20,16},{24,20},{28,24},{5,1},{9,5},{13... | collective-permute-start | bytes 786440 | tf_op jit(solution)/shard_map/ppermute | solution.py:13
  43.4 1.6 fusion.1
  45.0 0.0 collective-permute-done.7
  45.0 1.3 collective-permute-start.8
  46.3 0.6 fusion.3
  47.0 0.0 collective-permute-done.4
  47.0 5.9 %collective-permute-start.11 = (bf16[512,256]{1,0:T(8,128)(2,1)}, bf16[512,256]{1,0:T(8,128)(2,1)}, u32[]{:S(2)}, u32[]{:S(2)}) collective-permute-start(bf16[512,256]{1,0:T(8,128)(2,1)} %param.7), channel_id=1, source_target_pairs={{8,0},{12,4},{16,8},{20,12},{24,16},{28,20},{9,1},{13,5},{17,9},{2... | collective-permute-start | bytes 786440 | tf_op jit(solution)/shard_map/ppermute | solution.py:13
  52.9 0.6 fusion.2
  53.5 0.0 collective-permute-done.10
  53.5 0.6 fusion.4
  54.2 1.3 copy-done.1
  55.5 0.6 fusion.13
  56.1 1.1 fusion.5
  57.2 0.0 copy-start.6
  57.2 1.1 fusion.9
  58.4 1.6 fusion.23
  60.0 1.8 copy.29
  61.8 3.4 %fusion.24 = f32[512,2,128]{0,2,1:T(8,128)} fusion(f32[512,2,128]{0,2,1:T(8,128)} %fusion.23, bf16[512,2,128]{0,2,1:T(8,128)(2,1)} %bitcast.200, f32[2,512,512]{1,2,0:T(8,128)} %copy-done.3, f32[2,512]{1,0:T(2,128)S(1)} %get-tuple-element.27, pred[512,512]{0,1:T(8,128)(4,1)} %copy-done.5, f32[512,2]{0,1:T(2,128)S(1)} %get-tuple-element.12, ...), kind=kOutput, calls=%fused_computation.40 | convolution fusion | flops 137232384 | bytes 3682304 | tf_op jit(solution)/shard_map/hqk,khd->qhd/dot_general | solution.py:30
  65.2 0.0 collective-permute-done.5
  65.2 1.8 copy.34
  67.0 3.3 %fusion.25 = f32[512,2,128]{0,2,1:T(8,128)} fusion(f32[512,2,128]{0,2,1:T(8,128)} %fusion.24, bf16[512,2,128]{0,2,1:T(8,128)(2,1)} %bitcast.201, f32[2,512,512]{1,2,0:T(8,128)} %copy-done.4, f32[2,512]{1,0:T(2,128)S(1)} %get-tuple-element.25, pred[512,512]{0,1:T(8,128)(4,1)S(1)} %get-tuple-element.15, f32[512,2]{0,1:T(2,128)S(1)} %get-tuple-element.10, ...), kind=kOutput, calls=%fused_computation.41 | convolution fusion | flops 137232384 | bytes 3682304 | tf_op jit(solution)/shard_map/hqk,khd->qhd/dot_general | solution.py:30
  70.3 0.0 collective-permute-done.8
  70.3 1.1 copy.39
  71.4 3.3 %fusion.26 = f32[512,2,128]{0,2,1:T(8,128)} fusion(f32[512,2,128]{0,2,1:T(8,128)} %fusion.25, bf16[512,2,128]{0,2,1:T(8,128)(2,1)S(1)} %bitcast.202, f32[2,512,512]{1,2,0:T(8,128)} %copy-done.2, f32[2,512]{1,0:T(2,128)S(1)} %get-tuple-element.23, pred[512,512]{0,1:T(8,128)(4,1)S(1)} %get-tuple-element.16, f32[512,2]{0,1:T(2,128)S(1)} %get-tuple-element.8, ...), kind=kOutput, calls=%fused_computation.42 | convolution fusion | flops 137232384 | bytes 3682304 | tf_op jit(solution)/shard_map/hqk,khd->qhd/dot_general | solution.py:30
  74.7 1.1 copy.44
  75.8 2.5 %fusion.28 = bf16[512,2,128]{0,2,1:T(8,128)(2,1)S(1)} fusion(f32[512,2,128]{0,2,1:T(8,128)} %fusion.26, bf16[512,2,128]{0,2,1:T(8,128)(2,1)S(1)} %bitcast.199, f32[2,512,512]{1,2,0:T(8,128)} %copy-done.1, f32[2,512]{1,0:T(2,128)S(1)} %get-tuple-element.21, pred[512,512]{0,1:T(8,128)(4,1)S(1)} %get-tuple-element.17, f32[512,2]{0,1:T(2,128)S(1)} %get-tuple-element.5, ...), kind=kOutput, calls=%fused_computation.44 | convolution fusion | flops 137363456 | bytes 3420160 | tf_op jit(solution)/shard_map/hqk,khd->qhd/dot_general | solution.py:30
  78.2 3.9 %convolution_convert_fusion = bf16[512,5120]{1,0:T(8,128)(2,1)} fusion(bf16[512,256]{0,1:T(8,128)(2,1)S(1)} %bitcast.197, bf16[256,5120]{1,0:T(8,128)(2,1)S(1)} %copy-done), kind=kOutput, calls=%fused_computation | convolution fusion | flops 1344798720 | bytes 8126464 | tf_op jit(solution)/shard_map/dot_general | solution.py:71
  82.1 0.0 reduce-scatter.2.cloned.1.call-update
  82.2 96.0 %reduce-scatter.2.cloned.1.call-done = bf16[512,1280]{1,0:T(8,128)(2,1)} async-done(((bf16[512,5120]{1,0:T(8,128)(2,1)}), bf16[512,1280]{1,0:T(8,128)(2,1)}) %reduce-scatter.2.cloned.1.call-update) | async-done | bytes 1310736 | tf_op jit(solution)/shard_map/reduce_scatter | solution.py:72
  (18 shorter events, 0.1 us)
Async XLA Ops:
  6.5 71.7 %copy-start = (bf16[256,5120]{1,0:T(8,128)(2,1)S(1)}, bf16[256,5120]{1,0:T(8,128)(2,1)}, u32[]{:S(2)}) copy-start(bf16[256,5120]{1,0:T(8,128)(2,1)} %param.9) | copy-start | bytes 7864324
  6.5 171.7 %reduce-scatter.2.cloned.1.call-start = ((), (), s32[]{:S(2)}) async-start(), calls=%async_computation.1 | async-start | bytes 6553600 | tf_op jit(solution)/shard_map/reduce_scatter | solution.py:72
  7.4 17.0 %collective-permute-start = (s32[512]{0:T(512)S(1)}, s32[512]{0:T(512)S(1)}, u32[]{:S(2)}, u32[]{:S(2)}) collective-permute-start(s32[512]{0:T(512)S(1)} %broadcast_add_fusion), channel_id=1, source_target_pairs={{0,4},{4,8},{8,12},{12,16},{16,20},{20,24},{24,28},{1,5},{5,9},{9,... | collective-permute-start | bytes 6152 | tf_op jit(solution)/shard_map/ppermute | solution.py:13
  9.3 16.5 %collective-permute-start.3 = (s32[512]{0:T(512)S(1)}, s32[512]{0:T(512)S(1)}, u32[]{:S(2)}, u32[]{:S(2)}) collective-permute-start(s32[512]{0:T(512)S(1)} %broadcast_add_fusion), channel_id=1, source_target_pairs={{4,0},{8,4},{12,8},{16,12},{20,16},{24,20},{28,24},{5,1},{9,5},{13... | collective-permute-start | bytes 6152 | tf_op jit(solution)/shard_map/ppermute | solution.py:13
  12.9 17.1 %collective-permute-start.6 = (s32[512]{0:T(512)S(1)}, s32[512]{0:T(512)S(1)}, u32[]{:S(2)}, u32[]{:S(2)}) collective-permute-start(s32[512]{0:T(512)S(1)} %broadcast_add_fusion), channel_id=1, source_target_pairs={{0,8},{4,12},{8,16},{12,20},{16,24},{20,28},{1,9},{5,13},{9,17},{1... | collective-permute-start | bytes 6152 | tf_op jit(solution)/shard_map/ppermute | solution.py:13
  14.2 21.0 %collective-permute-start.9 = (s32[512]{0:T(512)S(1)}, s32[512]{0:T(512)S(1)}, u32[]{:S(2)}, u32[]{:S(2)}) collective-permute-start(s32[512]{0:T(512)S(1)} %broadcast_add_fusion), channel_id=1, source_target_pairs={{8,0},{12,4},{16,8},{20,12},{24,16},{28,20},{9,1},{13,5},{17,9},{2... | collective-permute-start | bytes 6152 | tf_op jit(solution)/shard_map/ppermute | solution.py:13
  20.6 19.1 %collective-permute-start.1 = (bf16[512,256]{0,1:T(8,128)(2,1)}, bf16[512,256]{0,1:T(8,128)(2,1)}, u32[]{:S(2)}, u32[]{:S(2)}) collective-permute-start(bf16[512,256]{0,1:T(8,128)(2,1)} %copy.26), channel_id=1, source_target_pairs={{0,4},{4,8},{8,12},{12,16},{16,20},{20,24},{24,28},{1,5},{5,9},{9,... | collective-permute-start | bytes 786440 | tf_op jit(solution)/shard_map/ppermute | solution.py:13
  24.3 19.1 %copy-start.7 = (bf16[512,256]{1,0:T(8,128)(2,1)S(1)}, bf16[512,256]{1,0:T(8,128)(2,1)}, u32[]{:S(2)}) copy-start(bf16[512,256]{1,0:T(8,128)(2,1)} %param.5) | copy-start | bytes 786436
  24.3 20.7 %collective-permute-start.7 = (bf16[512,256]{0,1:T(8,128)(2,1)}, bf16[512,256]{0,1:T(8,128)(2,1)S(1)}, u32[]{:S(2)}, u32[]{:S(2)}) collective-permute-start(bf16[512,256]{0,1:T(8,128)(2,1)} %copy.26), channel_id=1, source_target_pairs={{0,8},{4,12},{8,16},{12,20},{16,24},{20,28},{1,9},{5,13},{9,17},{1... | collective-permute-start | bytes 786440 | tf_op jit(solution)/shard_map/ppermute | solution.py:13
  25.8 21.2 %collective-permute-start.4 = (bf16[512,256]{0,1:T(8,128)(2,1)}, bf16[512,256]{0,1:T(8,128)(2,1)S(1)}, u32[]{:S(2)}, u32[]{:S(2)}) collective-permute-start(bf16[512,256]{0,1:T(8,128)(2,1)} %copy.26), channel_id=1, source_target_pairs={{4,0},{8,4},{12,8},{16,12},{20,16},{24,20},{28,24},{5,1},{9,5},{13... | collective-permute-start | bytes 786440 | tf_op jit(solution)/shard_map/ppermute | solution.py:13
  30.1 23.5 %collective-permute-start.10 = (bf16[512,256]{0,1:T(8,128)(2,1)}, bf16[512,256]{0,1:T(8,128)(2,1)S(1)}, u32[]{:S(2)}, u32[]{:S(2)}) collective-permute-start(bf16[512,256]{0,1:T(8,128)(2,1)} %copy.26), channel_id=1, source_target_pairs={{8,0},{12,4},{16,8},{20,12},{24,16},{28,20},{9,1},{13,5},{17,9},{2... | collective-permute-start | bytes 786440 | tf_op jit(solution)/shard_map/ppermute | solution.py:13
  35.2 24.7 %collective-permute-start.2 = (bf16[512,256]{1,0:T(8,128)(2,1)}, bf16[512,256]{1,0:T(8,128)(2,1)}, u32[]{:S(2)}, u32[]{:S(2)}) collective-permute-start(bf16[512,256]{1,0:T(8,128)(2,1)} %param.7), channel_id=1, source_target_pairs={{0,4},{4,8},{8,12},{12,16},{16,20},{20,24},{24,28},{1,5},{5,9},{9,... | collective-permute-start | bytes 786440 | tf_op jit(solution)/shard_map/ppermute | solution.py:13
  38.0 18.0 %copy-start.5 = (pred[512,512]{0,1:T(8,128)(4,1)}, pred[512,512]{0,1:T(8,128)(4,1)S(1)}, u32[]{:S(2)}) copy-start(pred[512,512]{0,1:T(8,128)(4,1)S(1)} %get-tuple-element.14) | copy-start | bytes 786436
  39.7 25.5 %collective-permute-start.5 = (bf16[512,256]{1,0:T(8,128)(2,1)}, bf16[512,256]{1,0:T(8,128)(2,1)}, u32[]{:S(2)}, u32[]{:S(2)}) collective-permute-start(bf16[512,256]{1,0:T(8,128)(2,1)} %param.7), channel_id=1, source_target_pairs={{4,0},{8,4},{12,8},{16,12},{20,16},{24,20},{28,24},{5,1},{9,5},{13... | collective-permute-start | bytes 786440 | tf_op jit(solution)/shard_map/ppermute | solution.py:13
  45.0 11.1 %copy-start.3 = (f32[2,512,512]{1,2,0:T(8,128)}, f32[2,512,512]{1,2,0:T(8,128)S(1)}, u32[]{:S(2)}) copy-start(f32[2,512,512]{1,2,0:T(8,128)S(1)} %get-tuple-element.28) | copy-start | bytes 6291460
  45.0 25.3 %collective-permute-start.8 = (bf16[512,256]{1,0:T(8,128)(2,1)}, bf16[512,256]{1,0:T(8,128)(2,1)}, u32[]{:S(2)}, u32[]{:S(2)}) collective-permute-start(bf16[512,256]{1,0:T(8,128)(2,1)} %param.7), channel_id=1, source_target_pairs={{0,8},{4,12},{8,16},{12,20},{16,24},{20,28},{1,9},{5,13},{9,17},{1... | collective-permute-start | bytes 786440 | tf_op jit(solution)/shard_map/ppermute | solution.py:13
  47.0 10.2 %copy-start.2 = (f32[2,512,512]{1,2,0:T(8,128)}, f32[2,512,512]{1,2,0:T(8,128)S(1)}, u32[]{:S(2)}) copy-start(f32[2,512,512]{1,2,0:T(8,128)S(1)} %get-tuple-element.24) | copy-start | bytes 6291460
  47.0 27.7 %collective-permute-start.11 = (bf16[512,256]{1,0:T(8,128)(2,1)}, bf16[512,256]{1,0:T(8,128)(2,1)}, u32[]{:S(2)}, u32[]{:S(2)}) collective-permute-start(bf16[512,256]{1,0:T(8,128)(2,1)} %param.7), channel_id=1, source_target_pairs={{8,0},{12,4},{16,8},{20,12},{24,16},{28,20},{9,1},{13,5},{17,9},{2... | collective-permute-start | bytes 786440 | tf_op jit(solution)/shard_map/ppermute | solution.py:13
  53.5 3.7 %copy-start.4 = (f32[2,512,512]{1,2,0:T(8,128)}, f32[2,512,512]{1,2,0:T(8,128)S(1)}, u32[]{:S(2)}) copy-start(f32[2,512,512]{1,2,0:T(8,128)S(1)} %get-tuple-element.26) | copy-start | bytes 6291460
  54.2 1.3 copy-start.1
  57.2 1.2 copy-start.6
Sparse Core Ops, SparseCore 0:
  82.3 95.8 reduce-scatter.1
where the time goes:
time: 187 us; the launch traced here: 185 us
  waiting for transfers between devices  96.1 us (51%)
  starting transfers between devices  36.9 us (20%)
  matrix products  23.1 us (12%)
  between operations  13.7 us (7%)
  local copies, waits for them, and re-layouts  10.7 us (6%)
  other arithmetic  4.55 us (2%)
    reduce_scatter x1, waiting for transfers between devices, shards(): lax.psum_scatter(term.astype(jnp.bfloat16), 'head', scatter_dimension=1,...  96 us
    ppermute x12, starting transfers between devices, shifted(): return lax.ppermute(block, axis, route)  36.9 us
    dot_general x5, matrix products, attend(): jnp.einsum('hqk,khd->qhd', weights.astype(jnp.bfloat16), value_heads, pre...  14.1 us
    ppermute x4, local copies, waits for them, and re-layouts, shifted(): return lax.ppermute(block, axis, route)  5.77 us
    dot_general x5, matrix products, attend(): jnp.einsum('qhd,khd->hqk', query_heads, key_heads, preferred_element_type...  5.17 us
    dot_general x1, matrix products, shards(): term = jnp.dot(attended, out_weight, preferred_element_type=jnp.float32)  3.88 us
  transfers between devices with their start and end apart: 13, of which 1 were waited for; matrix products, arithmetic and copies ran while one was open for 16% of the time, Pallas kernels for 0%

commit v1 on v0

v1 whole, which is shorter than its diff:
```python
import functools
import math

import jax
import jax.numpy as jnp
from jax import lax
from jax.experimental import pallas as pl
from jax.experimental.pallas import tpu as pltpu
from jax.sharding import PartitionSpec as P

HEAD_DEV = 2
QUERY_TILE = 128
PAD_ROWS = 16


def whole(shape):
    return pl.BlockSpec(shape, lambda *_: (0,) * len(shape))


def rotate(block, axis, distance):
    count = lax.axis_size(axis)
    return lax.ppermute(block, axis, [(i, (i + distance) % count) for i in range(count)])


def shifted(block, axis, distance):
    devices = range(lax.axis_size(axis))
    return lax.ppermute(block, axis, [(i - distance, i) for i in devices if i - distance in devices])


def exchanged(block, axis, flip):
    return lax.ppermute(block, axis, [(i, i ^ flip) for i in range(lax.axis_size(axis))])


def pack(keys, values, marks):
    rows, width = keys.shape
    head = width // HEAD_DEV
    mark_rows = marks.shape[0]

    def body(k_ref, v_ref, m_ref, first_ref, *rest):
        for index, ref in enumerate((first_ref, *rest)):
            part = slice(index * head, (index + 1) * head)
            ref[:rows, :head] = k_ref[:, part]
            ref[:rows, head:] = v_ref[:, part]
        tail = jnp.zeros((PAD_ROWS - mark_rows, 2 * head), jnp.float32)
        first_ref[rows:, :] = jnp.concatenate([m_ref[...], tail], axis=0).astype(jnp.bfloat16)

    shapes = [(rows + PAD_ROWS, 2 * head)] + [(rows, 2 * head)] * (HEAD_DEV - 1)
    return pl.pallas_call(
        body,
        name="pack",
        out_shape=[jax.ShapeDtypeStruct(shape, jnp.bfloat16) for shape in shapes],
        cost_estimate=pl.CostEstimate(flops=0, bytes_accessed=8 * rows * width, transcendentals=0),
    )(keys, values, marks)


def attend(query, query_marks, blocks, mark_blocks, index):
    rows = query.shape[0]
    head = query.shape[1] // HEAD_DEV
    count = len(blocks)
    mark_rows = rows // (2 * head)
    span = count * rows
    scale = head ** -0.5 * math.log2(math.e)

    def body(q_ref, qm_ref, *refs):
        block_refs = refs[:count]
        mark_refs = refs[count:2 * count]
        out_ref = refs[2 * count]
        for start in range(0, rows, QUERY_TILE):
            tile = slice(start, start + QUERY_TILE)
            q_tile = q_ref[tile, :]
            q_mark = qm_ref[tile, :]
            q_mark = jnp.concatenate([q_mark] * (2 * head // q_mark.shape[1]), axis=1)
            parts = []
            for block, mark in zip(block_refs, mark_refs):
                for piece in range(mark_rows):
                    lines = slice(piece * 2 * head, (piece + 1) * 2 * head)
                    score = lax.dot_general(
                        q_tile, block[lines, :head], (((1,), (1,)), ((), ())),
                        preferred_element_type=jnp.float32,
                    )
                    row = mark[piece:piece + 1, :].astype(jnp.float32)
                    parts.append(jnp.where(q_mark == row, score, -1e30))
            peak = functools.reduce(jnp.maximum, parts)
            peak = jnp.max(peak, axis=1, keepdims=True)
            weights = [jnp.exp2((part - peak) * scale) for part in parts]
            total = jnp.sum(functools.reduce(jnp.add, weights), axis=1, keepdims=True)
            summed = jnp.zeros((QUERY_TILE, head), jnp.float32)
            step = 0
            for block in block_refs:
                for piece in range(mark_rows):
                    lines = slice(piece * 2 * head, (piece + 1) * 2 * head)
                    summed += jnp.dot(
                        weights[step].astype(jnp.bfloat16), block[lines, head:],
                        preferred_element_type=jnp.float32,
                    )
                    step += 1
            out_ref[tile, :] = (summed / total).astype(jnp.bfloat16)

    return pl.pallas_call(
        body,
        name="attend",
        grid=(1,),
        in_specs=[
            pl.BlockSpec((rows, head), lambda i: (0, index)),
            whole(query_marks.shape),
            *[pl.BlockSpec((rows, 2 * head), lambda i: (0, 0)) for _ in blocks],
            *[pl.BlockSpec((PAD_ROWS, 2 * head), lambda i: (rows // PAD_ROWS, 0)) for _ in mark_blocks],
        ],
        out_specs=whole((rows, head)),
        out_shape=jax.ShapeDtypeStruct((rows, head), jnp.bfloat16),
        cost_estimate=pl.CostEstimate(
            flops=8 * rows * span * head, bytes_accessed=4 * span * head, transcendentals=rows * span
        ),
    )(query, query_marks, *blocks, *mark_blocks)


def assemble(order, pieces):
    groups, part, columns = pieces[0].shape
    count = len(pieces)

    def body(order_ref, *refs):
        out_ref = refs[-1]
        for index, ref in enumerate(refs[:-1]):
            place = pl.multiple_of((order_ref[0] ^ index) * part, part)
            out_ref[:, pl.ds(place, part), :] = ref[...]

    return pl.pallas_call(
        body,
        name="assemble",
        in_specs=[pl.BlockSpec(memory_space=pltpu.SMEM)] + [pl.BlockSpec(memory_space=pltpu.VMEM)] * count,
        out_shape=jax.ShapeDtypeStruct((groups, part * count, columns), jnp.bfloat16),
        cost_estimate=pl.CostEstimate(
            flops=0, bytes_accessed=4 * groups * part * count * columns, transcendentals=0
        ),
    )(order, *pieces)


def gathered_weight(out_weight, axis):
    groups = lax.axis_size(axis)
    replicas = 4
    rows, width = out_weight.shape
    part, columns = rows // replicas, width // groups
    me = lax.axis_index(axis)
    place = lax.axis_index("seq")
    mine = (place & 1) + 2 * ((place >> 2) & 1)
    received = []
    for distance in range(1, groups):
        target = (me + distance) % groups
        piece = lax.dynamic_slice(out_weight, (mine * part, target * columns), (part, columns))
        received.append(rotate(piece, axis, distance))
    first = jnp.stack(received)
    second = exchanged(first, "seq", 4)
    near = exchanged(jnp.stack([first, second]), "seq", 1)
    others = assemble(mine.astype(jnp.int32)[None], [first, near[0], second, near[1]])
    own = lax.dynamic_slice(out_weight, (0, me * columns), (rows, columns))
    return own, others


def shards(queries, keys, values, segment_ids, out_weight):
    rows, width = queries.shape
    head = width // HEAD_DEV
    groups = lax.axis_size("head")
    marks = (segment_ids + 1).astype(jnp.float32)
    query_marks = jnp.broadcast_to(marks[:, None], (rows, head))
    messages = pack(keys, values, marks.reshape(rows // (2 * head), 2 * head))
    even = lax.axis_index("seq") % 2 == 0

    own_weight, other_weight = gathered_weight(out_weight, "head")

    mark_blocks = None
    sent = []
    for index, message in enumerate(messages):
        left = shifted(message, "seq", 2)
        right = shifted(message, "seq", -2)
        beside = exchanged(message, "seq", 1)
        across = exchanged(jnp.where(even, right, left), "seq", 1)
        blocks = (message, beside, left, right, across)
        if mark_blocks is None:
            mark_blocks = blocks
        done = attend(queries, query_marks, blocks, mark_blocks, index)
        sent.append([done] + [rotate(done, "head", distance) for distance in range(1, groups)])

    mixed = jnp.zeros((rows, own_weight.shape[1]), jnp.float32)
    for distance in range(groups):
        weight = own_weight if distance == 0 else other_weight[distance - 1]
        group = jnp.concatenate([part[distance] for part in sent], axis=1)
        mixed += jnp.dot(group, weight, preferred_element_type=jnp.float32)
    return mixed.astype(jnp.bfloat16)


def solution(mesh):
    placed = (P("seq", "head"), P("seq", "head"), P("seq", "head"), P("seq"), P("head", None))
    return jax.shard_map(
        shards, mesh=mesh, in_specs=placed, out_specs=P("seq", "head"), check_vma=False
    )
```

time: 187 us -> 91.4 us (0.49)
  waiting for transfers between devices: 96.1 us -> 43.9 us
  matrix products: 23.1 us -> 5.31 us
  starting transfers between devices: 36.9 us -> 20.1 us
  Pallas kernels: 0 us -> 14.2 us
  between operations: 13.7 us -> 0.15 us
  local copies, waits for them, and re-layouts: 10.7 us -> 3.95 us
    reduce_scatter x1 -> x0, waiting for transfers between devices: 96 us -> none  [shards(): lax.psum_scatter(term.astype(jnp.bfloat16), 'head', scatter_dimension=1,...]
    ppermute x12 -> x19, waiting for transfers between devices: 0.03 us -> 43.9 us  [the longest x9 20.7 us: rotate(): lax.ppermute(block, axis, [(i, (i + distance) % count) for i in range(cou...]
    dot_general x11 -> x4, matrix products: 23.1 us -> 5.31 us  [shards(): mixed += jnp.dot(group, weight, preferred_element_type=jnp.float32)]
    ppermute x12 -> x19, starting transfers between devices: 36.9 us -> 20.1 us  [the longest x9 11.7 us: rotate(): lax.ppermute(block, axis, [(i, (i + distance) % count) for i in range(cou...]
    pallas_call x0 -> x4, Pallas kernels: none -> 14.2 us  [the longest x2 9.43 us: attend(): pl.pallas_call(body, name='attend', grid=(1,), in_specs=[pl.BlockSpec((ro...]
    ppermute x4 -> x0, local copies, waits for them, and re-layouts: 5.77 us -> none  [shifted(): return lax.ppermute(block, axis, route)]
    reduce_sum x3 -> x0, other arithmetic: 2.81 us -> none  [attend(): total = jnp.sum(weights, axis=2)]
    unnamed x17 -> x14, local copies, waits for them, and re-layouts: 3.14 us -> 0.4 us
  transfers between devices with their start and end apart: 13 -> 19, of which waited for: 1 -> 8; matrix products, arithmetic and copies ran while one was open for 16% -> 9% of each run, Pallas kernels for 0% -> 16%
where the time goes in v1:
time: 91.4 us; the launch traced here: 90.9 us
  waiting for transfers between devices  43.9 us (48%)
  starting transfers between devices  20.1 us (22%)
  Pallas kernels  14.2 us (16%)
  matrix products  5.31 us (6%)
  local copies, waits for them, and re-layouts  3.95 us (4%)
  other arithmetic  3.27 us (4%)
    ppermute x9, waiting for transfers between devices, rotate(): lax.ppermute(block, axis, [(i, (i + distance) % count) for i in range(cou...  20.7 us
    ppermute x4, waiting for transfers between devices, shifted(): lax.ppermute(block, axis, [(i - distance, i) for i in devices if i - dist...  13.7 us
    ppermute x9, starting transfers between devices, rotate(): lax.ppermute(block, axis, [(i, (i + distance) % count) for i in range(cou...  11.7 us
    ppermute x6, waiting for transfers between devices, exchanged(): lax.ppermute(block, axis, [(i, i ^ flip) for i in range(lax.axis_size(axi...  9.51 us
    pallas_call x2, Pallas kernels, attend(): pl.pallas_call(body, name='attend', grid=(1,), in_specs=[pl.BlockSpec((ro...  9.43 us
    ppermute x4, starting transfers between devices, shifted(): lax.ppermute(block, axis, [(i - distance, i) for i in devices if i - dist...  7.02 us
    dot_general x4, matrix products, shards(): mixed += jnp.dot(group, weight, preferred_element_type=jnp.float32)  5.31 us
    pallas_call x1, Pallas kernels, assemble(): pl.pallas_call(body, name='assemble', in_specs=[pl.BlockSpec(memory_space...  2.89 us
  transfers between devices with their start and end apart: 19, of which 8 were waited for; matrix products, arithmetic and copies ran while one was open for 9% of the time, Pallas kernels for 16%

profile of v1, /device:TPU:6, one launch (start us, length us, event | category | flops | bytes accessed | tf_op | source)
XLA Modules:
  0.0 90.9 jit_solution(727835951658350188)
XLA Ops:
  0.0 1.1 %fusion.25 = (bf16[64,1280]{1,0:T(8,128)(2,1)S(1)}, bf16[64,1280]{1,0:T(8,128)(2,1)S(1)}, bf16[64,1280]{1,0:T(8,128)(2,1)S(1)}) fusion(bf16[256,5120]{1,0:T(8,128)(2,1)} %param.9, s32[]{:T(128)S(6)} %select_n.58, s32[]{:T(128)S(6)} %select_n.60, s32[]{:T(128)S(6)} %select_n.64, s32[]{:T(128)S(6)} %select_n.62), kind=kLoop, calls=%fused_computation.36 | loop fusion | bytes 983056 | tf_op jit(solution)/shard_map/dynamic_slice | solution.py:149
  1.1 1.6 %collective-permute-start.10 = (bf16[64,1280]{1,0:T(8,128)(2,1)S(1)}, bf16[64,1280]{1,0:T(8,128)(2,1)S(1)}, u32[]{:S(2)}, u32[]{:S(2)}) collective-permute-start(bf16[64,1280]{1,0:T(8,128)(2,1)S(1)} %get-tuple-element.9), channel_id=1, source_target_pairs={{0,1},{1,2},{2,3},{3,0},{4,5},{5,6},{6,7},{7,4},{8,9},{9,10},{10,1... | collective-permute-start | bytes 491528 | tf_op jit(solution)/shard_map/ppermute | solution.py:22
  2.7 2.2 %collective-permute-start.12 = (bf16[64,1280]{1,0:T(8,128)(2,1)S(1)}, bf16[64,1280]{1,0:T(8,128)(2,1)S(1)}, u32[]{:S(2)}, u32[]{:S(2)}) collective-permute-start(bf16[64,1280]{1,0:T(8,128)(2,1)S(1)} %get-tuple-element.10), channel_id=1, source_target_pairs={{0,3},{1,0},{2,1},{3,2},{4,7},{5,4},{6,5},{7,6},{8,11},{9,8},{10,9... | collective-permute-start | bytes 491528 | tf_op jit(solution)/shard_map/ppermute | solution.py:22
  5.0 0.8 collective-permute-start.11
  5.8 4.3 %collective-permute-done.10 = bf16[64,1280]{1,0:T(8,128)(2,1)S(1)} collective-permute-done((bf16[64,1280]{1,0:T(8,128)(2,1)S(1)}, bf16[64,1280]{1,0:T(8,128)(2,1)S(1)}, u32[]{:S(2)}, u32[]{:S(2)}) %collective-permute-start.10) | collective-permute-done | bytes 163872 | tf_op jit(solution)/shard_map/ppermute | solution.py:22
  10.1 1.8 %collective-permute-done.12 = bf16[64,1280]{1,0:T(8,128)(2,1)S(1)} collective-permute-done((bf16[64,1280]{1,0:T(8,128)(2,1)S(1)}, bf16[64,1280]{1,0:T(8,128)(2,1)S(1)}, u32[]{:S(2)}, u32[]{:S(2)}) %collective-permute-start.12) | collective-permute-done | bytes 163872 | tf_op jit(solution)/shard_map/ppermute | solution.py:22
  11.9 7.6 %collective-permute-done.11 = bf16[64,1280]{1,0:T(8,128)(2,1)S(1)} collective-permute-done((bf16[64,1280]{1,0:T(8,128)(2,1)S(1)}, bf16[64,1280]{1,0:T(8,128)(2,1)S(1)}, u32[]{:S(2)}, u32[]{:S(2)}) %collective-permute-start.11) | collective-permute-done | bytes 163872 | tf_op jit(solution)/shard_map/ppermute | solution.py:22
  19.5 0.1 fusion.24
  19.6 0.0 copy-start.1
  19.6 0.6 collective-permute-start.13
  20.2 0.7 add_convert_fusion
  20.8 0.6 reshape.4.m_ref
  21.4 1.9 %pack.1 = (bf16[528,256]{1,0:T(8,128)(2,1)}, bf16[512,256]{1,0:T(8,128)(2,1)}) custom-call(bf16[512,256]{1,0:T(8,128)(2,1)} %k_ref.1, bf16[512,256]{1,0:T(8,128)(2,1)} %v_ref.1, f32[2,256]{1,0:T(2,128)} %reshape.4.m_ref), custom_call_target="tpu_custom_call" | custom-call | bytes 1048576 | tf_op jit(solution)/shard_map/pack/pallas_call | solution.py:48
  23.4 2.4 %collective-permute-start.2 = (bf16[528,256]{1,0:T(8,128)(2,1)}, bf16[528,256]{1,0:T(8,128)(2,1)S(1)}, u32[]{:S(2)}, u32[]{:S(2)}) collective-permute-start(bf16[528,256]{1,0:T(8,128)(2,1)} %get-tuple-element.7.refs_0_.refs_5_), channel_id=1, source_target_pairs={{8,0},{12,4},{16,8},{20,12},{24,16},{28,20},{9,1},{13,5},{17,9},{2... | collective-permute-start | bytes 811016 | tf_op jit(solution)/shard_map/ppermute | solution.py:27
  25.8 1.3 %collective-permute-start.1 = (bf16[528,256]{1,0:T(8,128)(2,1)}, bf16[528,256]{1,0:T(8,128)(2,1)S(1)}, u32[]{:S(2)}, u32[]{:S(2)}) collective-permute-start(bf16[528,256]{1,0:T(8,128)(2,1)} %get-tuple-element.7.refs_0_.refs_5_), channel_id=1, source_target_pairs={{0,8},{4,12},{8,16},{12,20},{16,24},{20,28},{1,9},{5,13},{9,17},{1... | collective-permute-start | bytes 811016 | tf_op jit(solution)/shard_map/ppermute | solution.py:27
  27.1 9.5 %collective-permute-done.13.refs_2_ = bf16[3,64,1280]{2,1,0:T(8,128)(2,1)S(1)} collective-permute-done((bf16[3,64,1280]{2,1,0:T(8,128)(2,1)S(1)}, bf16[3,64,1280]{2,1,0:T(8,128)(2,1)S(1)}, u32[]{:S(2)}, u32[]{:S(2)}) %collective-permute-start.13) | collective-permute-done | bytes 491552 | tf_op jit(solution)/shard_map/ppermute | solution.py:31
  36.6 0.1 pad_maximum_fusion
  36.7 0.1 collective-permute-start.14
  36.8 2.0 %collective-permute-start.6 = (bf16[512,256]{1,0:T(8,128)(2,1)}, bf16[512,256]{1,0:T(8,128)(2,1)}, u32[]{:S(2)}, u32[]{:S(2)}) collective-permute-start(bf16[512,256]{1,0:T(8,128)(2,1)} %get-tuple-element.8.refs_0_), channel_id=1, source_target_pairs={{8,0},{12,4},{16,8},{20,12},{24,16},{28,20},{9,1},{13,5},{17,9},{2... | collective-permute-start | bytes 786440 | tf_op jit(solution)/shard_map/ppermute | solution.py:27
  38.8 1.3 %collective-permute-start.5 = (bf16[512,256]{1,0:T(8,128)(2,1)}, bf16[512,256]{1,0:T(8,128)(2,1)}, u32[]{:S(2)}, u32[]{:S(2)}) collective-permute-start(bf16[512,256]{1,0:T(8,128)(2,1)} %get-tuple-element.8.refs_0_), channel_id=1, source_target_pairs={{0,8},{4,12},{8,16},{12,20},{16,24},{20,28},{1,9},{5,13},{9,17},{1... | collective-permute-start | bytes 786440 | tf_op jit(solution)/shard_map/ppermute | solution.py:27
  40.1 0.6 collective-permute-start.4
  40.7 0.0 collective-permute-done.1.refs_2_.refs_7_
  40.7 0.1 collective-permute-start
  40.8 0.7 broadcast_select_fusion
  41.5 3.4 %collective-permute-done.6.refs_3_ = bf16[512,256]{1,0:T(8,128)(2,1)} collective-permute-done((bf16[512,256]{1,0:T(8,128)(2,1)}, bf16[512,256]{1,0:T(8,128)(2,1)}, u32[]{:S(2)}, u32[]{:S(2)}) %collective-permute-start.6) | collective-permute-done | bytes 262176 | tf_op jit(solution)/shard_map/ppermute | solution.py:27
  44.9 10.3 %collective-permute-done.5.refs_2_ = bf16[512,256]{1,0:T(8,128)(2,1)} collective-permute-done((bf16[512,256]{1,0:T(8,128)(2,1)}, bf16[512,256]{1,0:T(8,128)(2,1)}, u32[]{:S(2)}, u32[]{:S(2)}) %collective-permute-start.5) | collective-permute-done | bytes 262176 | tf_op jit(solution)/shard_map/ppermute | solution.py:27
  55.2 1.7 %broadcast_select_fusion.1 = bf16[512,256]{1,0:T(8,128)(2,1)} fusion(bf16[512,256]{1,0:T(8,128)(2,1)} %collective-permute-done.6.refs_3_, bf16[512,256]{1,0:T(8,128)(2,1)} %collective-permute-done.5.refs_2_, pred[]{:T(512)S(6)} %eq.8), kind=kLoop, calls=%fused_computation.28 | loop fusion | flops 131072 | bytes 786433 | tf_op jit(solution)/shard_map/jit(_where)/select_n | solution.py:176
  56.9 0.0 collective-permute-start.7
  56.9 0.0 collective-permute-done.refs_1_.refs_6_
  56.9 0.0 collective-permute-done.3.refs_4_.refs_9_
  56.9 0.8 broadcast_in_dim.4.qm_ref
  57.8 4.7 %attend.2 = bf16[512,128]{1,0:T(8,128)(2,1)} custom-call(bf16[512,256]{1,0:T(8,128)(2,1)} %q_ref.3, f32[512,128]{1,0:T(8,128)} %broadcast_in_dim.4.qm_ref, bf16[528,256]{1,0:T(8,128)(2,1)} %get-tuple-element.7.refs_0_.refs_5_, bf16[528,256]{1,0:T(8,128)(2,1)} %collective-permute-done.refs_1_.refs_6_, bf16[528,256]{1,0:T(8,128)(2,1)} %copy-done.4, ...), custom_call_target="tpu_custom_call" | custom-call | flops 1342177280 | bytes 1310720 | tf_op jit(solution)/shard_map/attend/pallas_call | solution.py:99
  62.5 0.6 collective-permute-start.17
  63.1 0.0 collective-permute-start.15
  63.1 1.4 %collective-permute-start.8 = (bf16[512,128]{1,0:T(8,128)(2,1)}, bf16[512,128]{1,0:T(8,128)(2,1)S(1)}, u32[]{:S(2)}, u32[]{:S(2)}) collective-permute-start(bf16[512,128]{1,0:T(8,128)(2,1)} %attend.2), channel_id=1, source_target_pairs={{0,1},{1,2},{2,3},{3,0},{4,5},{5,6},{6,7},{7,4},{8,9},{9,10},{10,1... | collective-permute-start | bytes 393224 | tf_op jit(solution)/shard_map/ppermute | solution.py:22
  64.6 4.7 %attend.3 = bf16[512,128]{1,0:T(8,128)(2,1)} custom-call(bf16[512,256]{1,0:T(8,128)(2,1)} %q_ref.3, f32[512,128]{1,0:T(8,128)} %broadcast_in_dim.4.qm_ref, bf16[512,256]{1,0:T(8,128)(2,1)} %get-tuple-element.8.refs_0_, bf16[512,256]{1,0:T(8,128)(2,1)} %collective-permute-done.4.refs_1_, bf16[512,256]{1,0:T(8,128)(2,1)} %collective-permute-done.5.refs_2_, ...), custom_call_target="tpu_custom_call" | custom-call | flops 1342177280 | bytes 1310720 | tf_op jit(solution)/shard_map/attend/pallas_call | solution.py:99
  69.3 2.4 %collective-permute-start.18 = (bf16[512,128]{1,0:T(8,128)(2,1)}, bf16[512,128]{1,0:T(8,128)(2,1)S(1)}, u32[]{:S(2)}, u32[]{:S(2)}) collective-permute-start(bf16[512,128]{1,0:T(8,128)(2,1)} %attend.3), channel_id=1, source_target_pairs={{0,3},{1,0},{2,1},{3,2},{4,7},{5,4},{6,5},{7,6},{8,11},{9,8},{10,9... | collective-permute-start | bytes 393224 | tf_op jit(solution)/shard_map/ppermute | solution.py:22
  71.7 1.1 %collective-permute-start.16 = (bf16[512,128]{1,0:T(8,128)(2,1)}, bf16[512,128]{1,0:T(8,128)(2,1)S(1)}, u32[]{:S(2)}, u32[]{:S(2)}) collective-permute-start(bf16[512,128]{1,0:T(8,128)(2,1)} %attend.3), channel_id=1, source_target_pairs={{0,2},{1,3},{2,0},{3,1},{4,6},{5,7},{6,4},{7,5},{8,10},{9,11},{10,... | collective-permute-start | bytes 393224 | tf_op jit(solution)/shard_map/ppermute | solution.py:22
  72.8 1.0 %slice_bitcast_fusion.6 = (bf16[3,64,1280]{2,1,0:T(8,128)(2,1)}, bf16[3,64,1280]{2,1,0:T(8,128)(2,1)}) fusion(bf16[2,3,64,1280]{3,2,1,0:T(8,128)(2,1)S(1)} %collective-permute-done.14), kind=kLoop, calls=%fused_computation.12 | loop fusion | bytes 1966080 | tf_op jit(solution)/shard_map/squeeze | solution.py:154
  73.8 2.9 %assemble.1 = bf16[3,256,1280]{2,1,0:T(8,128)(2,1)} custom-call(s32[1]{0:T(128)} %bitcast.order_ref, bf16[3,64,1280]{2,1,0:T(8,128)(2,1)} %copy-done.1, bf16[3,64,1280]{2,1,0:T(8,128)(2,1)} %get-tuple-element.13.refs_1_, bf16[3,64,1280]{2,1,0:T(8,128)(2,1)} %copy-done.2, bf16[3,64,1280]{2,1,0:T(8,128)(2,1)} %get-tuple-element.12.refs_3_), custom_call_target="tpu_custom_call" | custom-call | bytes 3932160 | tf_op jit(solution)/shard_map/assemble/pallas_call | solution.py:127
  76.7 1.5 %collective-permute-start.9 = (bf16[512,128]{1,0:T(8,128)(2,1)S(1)}, bf16[512,128]{1,0:T(8,128)(2,1)S(1)}, u32[]{:S(2)}, u32[]{:S(2)}) collective-permute-start(bf16[512,128]{1,0:T(8,128)(2,1)S(1)} %copy-done.6), channel_id=1, source_target_pairs={{0,1},{1,2},{2,3},{3,0},{4,5},{5,6},{6,7},{7,4},{8,9},{9,10},{10,1... | collective-permute-start | bytes 393224 | tf_op jit(solution)/shard_map/ppermute | solution.py:22
  78.2 0.1 collective-permute-done.18
  78.3 1.6 %fusion.3 = f32[512,1280]{1,0:T(8,128)S(1)} fusion(bf16[3,256,1280]{2,1,0:T(8,128)(2,1)} %assemble.1, bf16[512,128]{1,0:T(8,128)(2,1)S(1)} %collective-permute-done.18, bf16[512,128]{1,0:T(8,128)(2,1)S(1)} %collective-permute-done.17), kind=kOutput, calls=%fused_computation.6 | convolution fusion | flops 336068608 | bytes 3538944 | tf_op jit(solution)/shard_map/dot_general | solution.py:187
  79.9 6.9 %collective-permute-done.16 = bf16[512,128]{1,0:T(8,128)(2,1)S(1)} collective-permute-done((bf16[512,128]{1,0:T(8,128)(2,1)}, bf16[512,128]{1,0:T(8,128)(2,1)S(1)}, u32[]{:S(2)}, u32[]{:S(2)}) %collective-permute-start.16) | collective-permute-done | bytes 131104 | tf_op jit(solution)/shard_map/ppermute | solution.py:22
  86.8 0.5 fusion.4
  87.3 0.5 fusion.5
  87.8 0.4 copy-done.5
  88.2 2.7 %fusion.2 = bf16[512,1280]{1,0:T(8,128)(2,1)} fusion(f32[512,1280]{1,0:T(8,128)S(1)} %fusion.3, f32[512,1280]{1,0:T(8,128)S(1)} %fusion.4, f32[512,1280]{1,0:T(8,128)S(1)} %fusion.5, bf16[256,5120]{1,0:T(8,128)(2,1)} %param.9, s32[]{:T(128)S(6)} %select_n.57, bf16[512,128]{1,0:T(8,128)(2,1)S(1)} %copy-done.6, bf16[512,128]{1,0:T(8,128)(2,1)S(1)} %copy-done.5), kind=kOutput, calls=%fused_computation.3 | convolution fusion | flops 338690048 | bytes 10092548 | tf_op jit(solution)/shard_map/dot_general | solution.py:187
  (21 shorter events, 0.0 us)
Async XLA Ops:
  1.1 9.0 %collective-permute-start.10 = (bf16[64,1280]{1,0:T(8,128)(2,1)S(1)}, bf16[64,1280]{1,0:T(8,128)(2,1)S(1)}, u32[]{:S(2)}, u32[]{:S(2)}) collective-permute-start(bf16[64,1280]{1,0:T(8,128)(2,1)S(1)} %get-tuple-element.9), channel_id=1, source_target_pairs={{0,1},{1,2},{2,3},{3,0},{4,5},{5,6},{6,7},{7,4},{8,9},{9,10},{10,1... | collective-permute-start | bytes 491528 | tf_op jit(solution)/shard_map/ppermute | solution.py:22
  2.7 9.2 %collective-permute-start.12 = (bf16[64,1280]{1,0:T(8,128)(2,1)S(1)}, bf16[64,1280]{1,0:T(8,128)(2,1)S(1)}, u32[]{:S(2)}, u32[]{:S(2)}) collective-permute-start(bf16[64,1280]{1,0:T(8,128)(2,1)S(1)} %get-tuple-element.10), channel_id=1, source_target_pairs={{0,3},{1,0},{2,1},{3,2},{4,7},{5,4},{6,5},{7,6},{8,11},{9,8},{10,9... | collective-permute-start | bytes 491528 | tf_op jit(solution)/shard_map/ppermute | solution.py:22
  5.0 14.5 %collective-permute-start.11 = (bf16[64,1280]{1,0:T(8,128)(2,1)S(1)}, bf16[64,1280]{1,0:T(8,128)(2,1)S(1)}, u32[]{:S(2)}, u32[]{:S(2)}) collective-permute-start(bf16[64,1280]{1,0:T(8,128)(2,1)S(1)} %get-tuple-element.11), channel_id=1, source_target_pairs={{0,2},{1,3},{2,0},{3,1},{4,6},{5,7},{6,4},{7,5},{8,10},{9,11},{10,... | collective-permute-start | bytes 491528 | tf_op jit(solution)/shard_map/ppermute | solution.py:22
  19.6 42.9 %copy-start.1 = (bf16[3,64,1280]{2,1,0:T(8,128)(2,1)}, bf16[3,64,1280]{2,1,0:T(8,128)(2,1)S(1)}, u32[]{:S(2)}) copy-start(bf16[3,64,1280]{2,1,0:T(8,128)(2,1)S(1)} %get-tuple-element.15.refs_0_) | copy-start | bytes 1474564
  19.6 17.0 %collective-permute-start.13 = (bf16[3,64,1280]{2,1,0:T(8,128)(2,1)S(1)}, bf16[3,64,1280]{2,1,0:T(8,128)(2,1)S(1)}, u32[]{:S(2)}, u32[]{:S(2)}) collective-permute-start(bf16[3,64,1280]{2,1,0:T(8,128)(2,1)S(1)} %get-tuple-element.15.refs_0_), channel_id=1, source_target_pairs={{0,16},{4,20},{8,24},{12,28},{16,0},{20,4},{24,8},{28,12},{1,17},{... | collective-permute-start | bytes 1474568 | tf_op jit(solution)/shard_map/ppermute | solution.py:31
  23.4 16.7 %collective-permute-start.2 = (bf16[528,256]{1,0:T(8,128)(2,1)}, bf16[528,256]{1,0:T(8,128)(2,1)S(1)}, u32[]{:S(2)}, u32[]{:S(2)}) collective-permute-start(bf16[528,256]{1,0:T(8,128)(2,1)} %get-tuple-element.7.refs_0_.refs_5_), channel_id=1, source_target_pairs={{8,0},{12,4},{16,8},{20,12},{24,16},{28,20},{9,1},{13,5},{17,9},{2... | collective-permute-start | bytes 811016 | tf_op jit(solution)/shard_map/ppermute | solution.py:27
  25.8 14.8 %collective-permute-start.1 = (bf16[528,256]{1,0:T(8,128)(2,1)}, bf16[528,256]{1,0:T(8,128)(2,1)S(1)}, u32[]{:S(2)}, u32[]{:S(2)}) collective-permute-start(bf16[528,256]{1,0:T(8,128)(2,1)} %get-tuple-element.7.refs_0_.refs_5_), channel_id=1, source_target_pairs={{0,8},{4,12},{8,16},{12,20},{16,24},{20,28},{1,9},{5,13},{9,17},{1... | collective-permute-start | bytes 811016 | tf_op jit(solution)/shard_map/ppermute | solution.py:27
  36.6 25.9 %copy-start.2 = (bf16[3,64,1280]{2,1,0:T(8,128)(2,1)}, bf16[3,64,1280]{2,1,0:T(8,128)(2,1)S(1)}, u32[]{:S(2)}) copy-start(bf16[3,64,1280]{2,1,0:T(8,128)(2,1)S(1)} %collective-permute-done.13.refs_2_) | copy-start | bytes 1474564
  36.7 35.0 %collective-permute-start.14 = (bf16[2,3,64,1280]{3,2,1,0:T(8,128)(2,1)S(1)}, bf16[2,3,64,1280]{3,2,1,0:T(8,128)(2,1)S(1)}, u32[]{:S(2)}, u32[]{:S(2)}) collective-permute-start(bf16[2,3,64,1280]{3,2,1,0:T(8,128)(2,1)S(1)} %pad_maximum_fusion), channel_id=1, source_target_pairs={{0,4},{4,0},{8,12},{12,8},{16,20},{20,16},{24,28},{28,24},{1,5},{5... | collective-permute-start | bytes 2949128 | tf_op jit(solution)/shard_map/ppermute | solution.py:31
  36.8 8.1 %collective-permute-start.6 = (bf16[512,256]{1,0:T(8,128)(2,1)}, bf16[512,256]{1,0:T(8,128)(2,1)}, u32[]{:S(2)}, u32[]{:S(2)}) collective-permute-start(bf16[512,256]{1,0:T(8,128)(2,1)} %get-tuple-element.8.refs_0_), channel_id=1, source_target_pairs={{8,0},{12,4},{16,8},{20,12},{24,16},{28,20},{9,1},{13,5},{17,9},{2... | collective-permute-start | bytes 786440 | tf_op jit(solution)/shard_map/ppermute | solution.py:27
  38.8 16.4 %collective-permute-start.5 = (bf16[512,256]{1,0:T(8,128)(2,1)}, bf16[512,256]{1,0:T(8,128)(2,1)}, u32[]{:S(2)}, u32[]{:S(2)}) collective-permute-start(bf16[512,256]{1,0:T(8,128)(2,1)} %get-tuple-element.8.refs_0_), channel_id=1, source_target_pairs={{0,8},{4,12},{8,16},{12,20},{16,24},{20,28},{1,9},{5,13},{9,17},{1... | collective-permute-start | bytes 786440 | tf_op jit(solution)/shard_map/ppermute | solution.py:27
  40.1 17.7 %copy-start.3 = (bf16[528,256]{1,0:T(8,128)(2,1)}, bf16[528,256]{1,0:T(8,128)(2,1)S(1)}, u32[]{:S(2)}) copy-start(bf16[528,256]{1,0:T(8,128)(2,1)S(1)} %collective-permute-done.2.refs_3_.refs_8_) | copy-start | bytes 811012
  40.1 23.0 %collective-permute-start.4 = (bf16[512,256]{1,0:T(8,128)(2,1)}, bf16[512,256]{1,0:T(8,128)(2,1)}, u32[]{:S(2)}, u32[]{:S(2)}) collective-permute-start(bf16[512,256]{1,0:T(8,128)(2,1)} %get-tuple-element.8.refs_0_), channel_id=1, source_target_pairs={{0,4},{4,0},{8,12},{12,8},{16,20},{20,16},{24,28},{28,24},{1,5},{5... | collective-permute-start | bytes 786440 | tf_op jit(solution)/shard_map/ppermute | solution.py:31
  40.7 17.1 %copy-start.4 = (bf16[528,256]{1,0:T(8,128)(2,1)}, bf16[528,256]{1,0:T(8,128)(2,1)S(1)}, u32[]{:S(2)}) copy-start(bf16[528,256]{1,0:T(8,128)(2,1)S(1)} %collective-permute-done.1.refs_2_.refs_7_) | copy-start | bytes 811012
  40.7 16.3 %collective-permute-start = (bf16[528,256]{1,0:T(8,128)(2,1)}, bf16[528,256]{1,0:T(8,128)(2,1)}, u32[]{:S(2)}, u32[]{:S(2)}) collective-permute-start(bf16[528,256]{1,0:T(8,128)(2,1)} %get-tuple-element.7.refs_0_.refs_5_), channel_id=1, source_target_pairs={{0,4},{4,0},{8,12},{12,8},{16,20},{20,16},{24,28},{28,24},{1,5},{5... | collective-permute-start | bytes 811016 | tf_op jit(solution)/shard_map/ppermute | solution.py:31
  44.9 12.0 %collective-permute-start.3 = (bf16[528,256]{1,0:T(8,128)(2,1)}, bf16[528,256]{1,0:T(8,128)(2,1)}, u32[]{:S(2)}, u32[]{:S(2)}) collective-permute-start(bf16[528,256]{1,0:T(8,128)(2,1)} %broadcast_select_fusion), channel_id=1, source_target_pairs={{0,4},{4,0},{8,12},{12,8},{16,20},{20,16},{24,28},{28,24},{1,5},{5... | collective-permute-start | bytes 811016 | tf_op jit(solution)/shard_map/ppermute | solution.py:31
  56.9 7.7 %collective-permute-start.7 = (bf16[512,256]{1,0:T(8,128)(2,1)}, bf16[512,256]{1,0:T(8,128)(2,1)}, u32[]{:S(2)}, u32[]{:S(2)}) collective-permute-start(bf16[512,256]{1,0:T(8,128)(2,1)} %broadcast_select_fusion.1), channel_id=1, source_target_pairs={{0,4},{4,0},{8,12},{12,8},{16,20},{20,16},{24,28},{28,24},{1,5},{5... | collective-permute-start | bytes 786440 | tf_op jit(solution)/shard_map/ppermute | solution.py:31
  62.5 14.2 %collective-permute-start.17 = (bf16[512,128]{1,0:T(8,128)(2,1)}, bf16[512,128]{1,0:T(8,128)(2,1)S(1)}, u32[]{:S(2)}, u32[]{:S(2)}) collective-permute-start(bf16[512,128]{1,0:T(8,128)(2,1)} %attend.2), channel_id=1, source_target_pairs={{0,3},{1,0},{2,1},{3,2},{4,7},{5,4},{6,5},{7,6},{8,11},{9,8},{10,9... | collective-permute-start | bytes 393224 | tf_op jit(solution)/shard_map/ppermute | solution.py:22
  63.1 16.8 %collective-permute-start.15 = (bf16[512,128]{1,0:T(8,128)(2,1)}, bf16[512,128]{1,0:T(8,128)(2,1)S(1)}, u32[]{:S(2)}, u32[]{:S(2)}) collective-permute-start(bf16[512,128]{1,0:T(8,128)(2,1)} %attend.2), channel_id=1, source_target_pairs={{0,2},{1,3},{2,0},{3,1},{4,6},{5,7},{6,4},{7,5},{8,10},{9,11},{10,... | collective-permute-start | bytes 393224 | tf_op jit(solution)/shard_map/ppermute | solution.py:22
  63.1 24.1 %collective-permute-start.8 = (bf16[512,128]{1,0:T(8,128)(2,1)}, bf16[512,128]{1,0:T(8,128)(2,1)S(1)}, u32[]{:S(2)}, u32[]{:S(2)}) collective-permute-start(bf16[512,128]{1,0:T(8,128)(2,1)} %attend.2), channel_id=1, source_target_pairs={{0,1},{1,2},{2,3},{3,0},{4,5},{5,6},{6,7},{7,4},{8,9},{9,10},{10,1... | collective-permute-start | bytes 393224 | tf_op jit(solution)/shard_map/ppermute | solution.py:22
  69.3 7.4 %copy-start.6 = (bf16[512,128]{1,0:T(8,128)(2,1)S(1)}, bf16[512,128]{1,0:T(8,128)(2,1)}, u32[]{:S(2)}) copy-start(bf16[512,128]{1,0:T(8,128)(2,1)} %attend.3) | copy-start | bytes 393220
  69.3 9.0 %collective-permute-start.18 = (bf16[512,128]{1,0:T(8,128)(2,1)}, bf16[512,128]{1,0:T(8,128)(2,1)S(1)}, u32[]{:S(2)}, u32[]{:S(2)}) collective-permute-start(bf16[512,128]{1,0:T(8,128)(2,1)} %attend.3), channel_id=1, source_target_pairs={{0,3},{1,0},{2,1},{3,2},{4,7},{5,4},{6,5},{7,6},{8,11},{9,8},{10,9... | collective-permute-start | bytes 393224 | tf_op jit(solution)/shard_map/ppermute | solution.py:22
  71.7 15.1 %collective-permute-start.16 = (bf16[512,128]{1,0:T(8,128)(2,1)}, bf16[512,128]{1,0:T(8,128)(2,1)S(1)}, u32[]{:S(2)}, u32[]{:S(2)}) collective-permute-start(bf16[512,128]{1,0:T(8,128)(2,1)} %attend.3), channel_id=1, source_target_pairs={{0,2},{1,3},{2,0},{3,1},{4,6},{5,7},{6,4},{7,5},{8,10},{9,11},{10,... | collective-permute-start | bytes 393224 | tf_op jit(solution)/shard_map/ppermute | solution.py:22
  76.7 10.0 %copy-start = (bf16[3,256,1280]{2,1,0:T(8,128)(2,1)S(1)}, bf16[3,256,1280]{2,1,0:T(8,128)(2,1)}, u32[]{:S(2)}) copy-start(bf16[3,256,1280]{2,1,0:T(8,128)(2,1)} %assemble.1) | copy-start | bytes 5898244
  76.7 10.6 %collective-permute-start.9 = (bf16[512,128]{1,0:T(8,128)(2,1)S(1)}, bf16[512,128]{1,0:T(8,128)(2,1)S(1)}, u32[]{:S(2)}, u32[]{:S(2)}) collective-permute-start(bf16[512,128]{1,0:T(8,128)(2,1)S(1)} %copy-done.6), channel_id=1, source_target_pairs={{0,1},{1,2},{2,3},{3,0},{4,5},{5,6},{6,7},{7,4},{8,9},{9,10},{10,1... | collective-permute-start | bytes 393224 | tf_op jit(solution)/shard_map/ppermute | solution.py:22
  87.3 0.9 copy-start.5

commit v2 on v0

v2 whole, which is shorter than its diff:
```python
import functools
import math

import jax
import jax.numpy as jnp
from jax import lax
from jax.experimental import pallas as pl
from jax.experimental.pallas import tpu as pltpu
from jax.sharding import PartitionSpec as P

HEAD_DEV = 2
QUERY_TILE = 256
PAD_ROWS = 16
KERNEL_VMEM = 12 * 2**20
IN_VMEM = pl.BlockSpec(memory_space=pltpu.VMEM)


def partner(index, distance, count):
    return index ^ distance if count & (count - 1) == 0 else (index + distance) % count


def to_partner(block, axis, distance):
    count = lax.axis_size(axis)
    return lax.ppermute(block, axis, [(i, partner(i, distance, count)) for i in range(count)])


def relays():
    return ()


def exchanged(block, axis, flip):
    return lax.ppermute(block, axis, [(i, i ^ flip) for i in range(lax.axis_size(axis))])


def from_far(block, axis, toward):
    count = lax.axis_size(axis)
    route = [(i + toward * (2 if i % 2 == 0 else -2), i) for i in range(count)]
    return lax.ppermute(block, axis, [(s, d) for s, d in route if 0 <= s < count])


def pack(keys, values, segment_ids):
    rows, width = keys.shape
    head = width // HEAD_DEV
    wide = 2 * head
    lines = rows // wide

    def body(k_ref, v_ref, s_ref, column_ref, *refs):
        messages, (ids_ref, sems) = refs[:HEAD_DEV], refs[HEAD_DEV:]
        copies = [pltpu.make_async_copy(s_ref, ids_ref, sems.at[0])]
        for index, ref in enumerate(messages):
            for side, source in enumerate((k_ref, v_ref)):
                copies.append(pltpu.make_async_copy(
                    source.at[:, index * head:(index + 1) * head],
                    ref.at[:rows, side * head:(side + 1) * head],
                    sems.at[1 + 2 * index + side],
                ))
        for copy in copies:
            copy.start()
        copies[0].wait()
        marks = (ids_ref[...] + 1).astype(jnp.float32)
        parts = [marks[:, i * wide:(i + 1) * wide] for i in range(lines)]
        parts.append(jnp.zeros((PAD_ROWS - lines, wide), jnp.float32))
        messages[0][rows:, :] = jnp.concatenate(parts, axis=0).astype(jnp.bfloat16)
        column_ref[...] = jnp.transpose(jnp.broadcast_to(marks, (head, rows)))
        for copy in copies[1:]:
            copy.wait()

    shapes = [(rows + PAD_ROWS, wide)] + [(rows, wide)] * (HEAD_DEV - 1)
    return pl.pallas_call(
        body,
        name="pack",
        in_specs=[pl.BlockSpec(memory_space=pltpu.HBM)] * 3,
        out_specs=[IN_VMEM] * (1 + HEAD_DEV),
        out_shape=[jax.ShapeDtypeStruct((rows, head), jnp.float32)]
        + [jax.ShapeDtypeStruct(shape, jnp.bfloat16) for shape in shapes],
        scratch_shapes=[
            pltpu.VMEM((1, rows), jnp.int32), pltpu.SemaphoreType.DMA((1 + 2 * HEAD_DEV,)),
        ],
        compiler_params=pltpu.CompilerParams(vmem_limit_bytes=KERNEL_VMEM),
        cost_estimate=pl.CostEstimate(flops=10**9, bytes_accessed=8 * rows * width, transcendentals=0),
    )(*[pltpu.with_memory_space_constraint(x, pltpu.HBM) for x in (keys, values, segment_ids.reshape(1, rows))])


def attend(query, query_marks, blocks, index, marks=None):
    rows = query.shape[0]
    head = query.shape[1] // HEAD_DEV
    wide = 2 * head
    count = len(blocks)
    lines = rows // wide
    span = count * rows
    scale = head ** -0.5 * math.log2(math.e)
    first = marks is None
    kept = -(-count * lines // 8) * 8

    def body(*refs):
        q_ref, qm_ref = refs[:2]
        block_refs = refs[2:2 + count]
        if first:
            out_ref, marks_ref, score_ref = refs[2 + count:]
            pieces = [ref[rows:rows + lines, :].astype(jnp.float32) for ref in block_refs]
            pieces.append(jnp.zeros((kept - count * lines, wide), jnp.float32))
            marks_ref[...] = jnp.concatenate(pieces, axis=0)
        else:
            marks_ref, out_ref, score_ref = refs[2 + count:]
        for start in range(0, rows, QUERY_TILE):
            tile = slice(start, start + QUERY_TILE)
            q_tile = q_ref[tile, index * head:(index + 1) * head]
            q_mark = qm_ref[tile, :]
            q_mark = jnp.concatenate([q_mark] * 2, axis=1)
            peak = None
            for piece in range(count * lines):
                block, offset = block_refs[piece // lines], piece % lines * wide
                score = lax.dot_general(
                    q_tile, block[offset:offset + wide, :head], (((1,), (1,)), ((), ())),
                    preferred_element_type=jnp.float32,
                )
                score = jnp.where(q_mark == marks_ref[piece:piece + 1, :], score, -1e30)
                score_ref[:, piece * wide:(piece + 1) * wide] = score
                largest = jnp.maximum(score[:, :head], score[:, head:])
                peak = largest if peak is None else jnp.maximum(peak, largest)
            peak = jnp.max(peak, axis=1, keepdims=True)
            summed, total = None, None
            for piece in range(count * lines):
                block, offset = block_refs[piece // lines], piece % lines * wide
                weight = jnp.exp2((score_ref[:, piece * wide:(piece + 1) * wide] - peak) * scale)
                folded = weight[:, :head] + weight[:, head:]
                term = jnp.dot(
                    weight.astype(jnp.bfloat16), block[offset:offset + wide, head:],
                    preferred_element_type=jnp.float32,
                )
                total = folded if total is None else total + folded
                summed = term if summed is None else summed + term
            total = jnp.sum(total, axis=1, keepdims=True)
            out_ref[tile, :] = (summed / total).astype(jnp.bfloat16)

    outs = [jax.ShapeDtypeStruct((rows, head), jnp.bfloat16)]
    if first:
        outs.append(jax.ShapeDtypeStruct((kept, wide), jnp.float32))
    result = pl.pallas_call(
        body,
        name="attend",
        in_specs=[IN_VMEM] * (2 + count + (not first)),
        out_specs=[IN_VMEM] * len(outs),
        out_shape=outs,
        scratch_shapes=[pltpu.VMEM((QUERY_TILE, span), jnp.float32)],
        compiler_params=pltpu.CompilerParams(vmem_limit_bytes=KERNEL_VMEM),
        cost_estimate=pl.CostEstimate(
            flops=8 * rows * span * head, bytes_accessed=4 * span * head, transcendentals=rows * span
        ),
    )(query, query_marks, *blocks, *([] if first else [marks]))
    return result if first else (result[0], marks)


def assemble(order, own, pieces):
    groups, part, columns = pieces[0].shape
    count = len(pieces)

    def body(order_ref, own_ref, *refs):
        out_ref = refs[-1]
        out_ref[0] = own_ref[...]
        for index, ref in enumerate(refs[:-1]):
            place = pl.multiple_of((order_ref[0] ^ index) * part, part)
            out_ref[1:, pl.ds(place, part), :] = ref[...]

    return pl.pallas_call(
        body,
        name="assemble",
        in_specs=[pl.BlockSpec(memory_space=pltpu.SMEM)] + [IN_VMEM] * (count + 1),
        out_specs=IN_VMEM,
        out_shape=jax.ShapeDtypeStruct((groups + 1, part * count, columns), jnp.bfloat16),
        compiler_params=pltpu.CompilerParams(vmem_limit_bytes=KERNEL_VMEM),
        cost_estimate=pl.CostEstimate(
            flops=10**9, bytes_accessed=4 * groups * part * count * columns, transcendentals=0
        ),
    )(order, own, *pieces)


def tiles(columns):
    tile = 256 if columns % 256 == 0 else columns
    return [slice(start, start + tile) for start in range(0, columns, tile)]


def placed(left_ref, refs, parts):
    place = 0
    refs = iter(refs)
    for arrays in parts:
        value = functools.reduce(jnp.add, [next(refs)[...] for _ in arrays])
        left_ref[:, place:place + value.shape[1]] = value
        place += value.shape[1]


def project_first(weight, own, others):
    groups, depth, columns = weight.shape
    rows, head = own[0].shape
    parts = [[array] for array in own] + others
    flat = [array for arrays in parts for array in arrays]

    def body(w_ref, *refs):
        ins, out_ref, left_ref = refs[:len(flat)], refs[-2], refs[-1]
        placed(left_ref, ins, parts)
        for tile in tiles(columns):
            out = jnp.dot(left_ref[:, :depth], w_ref[0, :, tile], preferred_element_type=jnp.float32)
            for g in range(1, groups):
                place = depth + (g - 1) * head
                out += jnp.dot(
                    left_ref[:, place:place + head], w_ref[g, :head, tile],
                    preferred_element_type=jnp.float32,
                )
            out_ref[:, tile] = out

    return pl.pallas_call(
        body,
        name="project_first",
        in_specs=[IN_VMEM] * (1 + len(flat)),
        out_specs=IN_VMEM,
        out_shape=jax.ShapeDtypeStruct((rows, columns), jnp.float32),
        scratch_shapes=[pltpu.VMEM((rows, depth + (groups - 1) * head), jnp.bfloat16)],
        compiler_params=pltpu.CompilerParams(vmem_limit_bytes=KERNEL_VMEM),
        cost_estimate=pl.CostEstimate(
            flops=rows * groups * depth * columns, bytes_accessed=4 * columns * rows, transcendentals=0
        ),
    )(weight, *flat)


def project_last(weight, partial, others):
    groups, depth, columns = weight.shape
    rows, head = others[0][0].shape
    flat = [array for arrays in others for array in arrays]
    span = (groups - 1) * (depth - head)
    cuts = tiles(columns)

    def body(w_ref, p_ref, *refs):
        ins, (out_ref, left_ref, right_ref, done_ref, sems) = refs[:len(flat)], refs[len(flat):]
        placed(left_ref, ins, others)
        for g in range(1, groups):
            place = (g - 1) * (depth - head)
            right_ref[place:place + depth - head, :] = w_ref[g, head:, :]
        copies = []
        for number, tile in enumerate(cuts):
            out = p_ref[:, tile] + jnp.dot(
                left_ref[...], right_ref[:, tile], preferred_element_type=jnp.float32
            )
            done_ref[:, tile] = out.astype(jnp.bfloat16)
            copies.append(pltpu.make_async_copy(done_ref.at[:, tile], out_ref.at[:, tile], sems.at[number]))
            copies[-1].start()
        for copy in copies:
            copy.wait()

    return pl.pallas_call(
        body,
        name="project_last",
        in_specs=[IN_VMEM] * (2 + len(flat)),
        out_specs=pl.BlockSpec(memory_space=pltpu.HBM),
        out_shape=jax.ShapeDtypeStruct((rows, columns), jnp.bfloat16),
        scratch_shapes=[
            pltpu.VMEM((rows, span), jnp.bfloat16),
            pltpu.VMEM((span, columns), jnp.bfloat16),
            pltpu.VMEM((rows, columns), jnp.bfloat16),
            pltpu.SemaphoreType.DMA((len(cuts),)),
        ],
        compiler_params=pltpu.CompilerParams(vmem_limit_bytes=2 * KERNEL_VMEM),
        cost_estimate=pl.CostEstimate(
            flops=rows * groups * depth * columns, bytes_accessed=4 * columns * rows, transcendentals=0
        ),
    )(weight, partial, *flat)


def shards(queries, keys, values, segment_ids, out_weight):
    groups = lax.axis_size("head")
    me = lax.axis_index("head")
    place = lax.axis_index("seq")
    replicas = 4
    mine = (place & 1) + 2 * ((place >> 2) & 1)
    part, columns = out_weight.shape[0] // replicas, out_weight.shape[1] // groups

    query_marks, *messages = pack(keys, values, segment_ids)

    near, far, beside = [], [], []
    for message in messages:
        near.append(from_far(message, "seq", 1))
        far.append(from_far(message, "seq", -1))
        beside.append(exchanged(message, "seq", 1))

    received = []
    for distance in range(1, groups):
        target = partner(me, distance, groups)
        piece = lax.dynamic_slice(out_weight, (mine * part, target * columns), (part, columns))
        received.append(to_partner(piece, "head", distance))
    first = jnp.stack(received)
    second = exchanged(first, "seq", 4)
    third = exchanged(first, "seq", 1)
    fourth = exchanged(second, "seq", 1)
    own = lax.dynamic_slice(out_weight, (0, me * columns), (out_weight.shape[0], columns))
    weight = assemble(mine.astype(jnp.int32)[None], own, [first, third, second, fourth])

    own, others, marks = [], [], None
    for index, message in enumerate(messages):
        across = exchanged(near[index], "seq", 1)
        blocks = (message, beside[index], near[index], far[index], across)
        done, marks = attend(queries, query_marks, blocks, index, marks)
        own.append(done)
        if index in relays():
            two = lax.ppermute(done, "head", [(0, 2), (2, 0), (1, 3), (3, 1)])
            one = lax.ppermute(done, "head", [(0, 1), (1, 0), (2, 3), (3, 2)])
            inner = lax.ppermute(done, "head", [(1, 2), (2, 1)])
            outer = lax.ppermute(two, "head", [(1, 0), (2, 3)])
            others.append([[one], [two], [inner, outer]])
        else:
            line = []
            for distance in range(1, groups):
                line.append([to_partner(done, "head", distance)])
            others.append(line)

    partial = project_first(weight, own, others[0])
    rest = [line[distance] for distance in range(groups - 1) for line in others[1:]]
    return project_last(weight, partial, rest)


def solution(mesh):
    placed = (P("seq", "head"), P("seq", "head"), P("seq", "head"), P("seq"), P("head", None))
    return jax.shard_map(shards, mesh=mesh, in_specs=placed, out_specs=P("seq", "head"), check_vma=False)
```

time: 187 us -> 71 us (0.38)
  the two profiles are of different devices: /device:TPU:6 before, /device:TPU:3 now
where the time goes in v2:
time: 71 us; the launch traced here: 70.7 us
  starting transfers between devices  33.6 us (47%)
  waiting for transfers between devices  23.6 us (33%)
  Pallas kernels  9.34 us (13%)
  local copies, waits for them, and re-layouts  3.93 us (6%)
    ppermute x9, waiting for transfers between devices, to_partner(): lax.ppermute(block, axis, [(i, partner(i, distance, count)) for i in rang...  21 us
    ppermute x7, starting transfers between devices, exchanged(): lax.ppermute(block, axis, [(i, i ^ flip) for i in range(lax.axis_size(axi...  12.3 us
    ppermute x9, starting transfers between devices, to_partner(): lax.ppermute(block, axis, [(i, partner(i, distance, count)) for i in rang...  10.9 us
    ppermute x4, starting transfers between devices, from_far(): lax.ppermute(block, axis, [(s, d) for s, d in route if 0 <= s < count])  10.3 us
    pallas_call x2, Pallas kernels, attend(): pl.pallas_call(body, name='attend', in_specs=[IN_VMEM] * (2 + count + (no...  4.81 us
    ppermute x4, waiting for transfers between devices, from_far(): lax.ppermute(block, axis, [(s, d) for s, d in route if 0 <= s < count])  2.66 us
    pallas_call x1, Pallas kernels, project_last(): pl.pallas_call(body, name='project_last', in_specs=[IN_VMEM] * (2 + len(f...  1.69 us
    unnamed x8, local copies, waits for them, and re-layouts  1.65 us
  transfers between devices with their start and end apart: 20, of which 6 were waited for; matrix products, arithmetic and copies ran while one was open for 2% of the time, Pallas kernels for 11%

profile of v2, /device:TPU:3, one launch (start us, length us, event | category | flops | bytes accessed | tf_op | source)
XLA Modules:
  0.0 70.7 jit_solution(16702727035627877796)
XLA Ops:
  0.0 1.1 %fusion = (bf16[64,1280]{1,0:T(8,128)(2,1)S(1)}, bf16[64,1280]{1,0:T(8,128)(2,1)S(1)}, bf16[64,1280]{1,0:T(8,128)(2,1)S(1)}) fusion(bf16[256,5120]{1,0:T(8,128)(2,1)} %param.9, s32[]{:T(128)S(6)} %select_n.18, s32[]{:T(128)S(6)} %select_n.19, s32[]{:T(128)S(6)} %select_n.21, s32[]{:T(128)S(6)} %select_n.20), kind=kLoop, calls=%fused_computation.2 | loop fusion | bytes 983056 | tf_op jit(solution)/shard_map/dynamic_slice | solution.py:287
  1.2 1.4 %collective-permute-start = (bf16[64,1280]{1,0:T(8,128)(2,1)S(1)}, bf16[64,1280]{1,0:T(8,128)(2,1)S(1)}, u32[]{:S(2)}, u32[]{:S(2)}) collective-permute-start(bf16[64,1280]{1,0:T(8,128)(2,1)S(1)} %get-tuple-element.15), channel_id=1, source_target_pairs={{0,1},{1,0},{2,3},{3,2},{4,5},{5,4},{6,7},{7,6},{8,9},{9,8},{10,11... | collective-permute-start | bytes 491528 | tf_op jit(solution)/shard_map/ppermute | solution.py:24
  2.5 2.2 %collective-permute-start.2 = (bf16[64,1280]{1,0:T(8,128)(2,1)S(1)}, bf16[64,1280]{1,0:T(8,128)(2,1)S(1)}, u32[]{:S(2)}, u32[]{:S(2)}) collective-permute-start(bf16[64,1280]{1,0:T(8,128)(2,1)S(1)} %get-tuple-element.16), channel_id=1, source_target_pairs={{0,3},{1,2},{2,1},{3,0},{4,7},{5,6},{6,5},{7,4},{8,11},{9,10},{10,... | collective-permute-start | bytes 491528 | tf_op jit(solution)/shard_map/ppermute | solution.py:24
  4.7 0.1 collective-permute-start.1
  4.8 1.2 %pack.1 = (f32[512,128]{1,0:T(8,128)S(1)}, bf16[528,256]{1,0:T(8,128)(2,1)S(1)}, bf16[512,256]{1,0:T(8,128)(2,1)S(1)}) custom-call(bf16[512,256]{1,0:T(8,128)(2,1)} %k_ref.1, bf16[512,256]{1,0:T(8,128)(2,1)} %v_ref.1, s32[1,512]{1,0:T(1,128)} %bitcast.8), custom_call_target="tpu_custom_call" | custom-call | flops 1000000000 | bytes 1048576 | tf_op jit(solution)/shard_map/pack/pallas_call | solution.py:69
  6.0 0.0 copy-start.1
  6.0 0.7 copy-done.1
  6.7 3.1 %collective-permute-start.7 = (bf16[528,256]{1,0:T(8,128)(2,1)S(1)}, bf16[528,256]{1,0:T(8,128)(2,1)S(1)}, u32[]{:S(2)}, u32[]{:S(2)}) collective-permute-start(bf16[528,256]{1,0:T(8,128)(2,1)S(1)} %get-tuple-element.11.refs_2_), channel_id=1, source_target_pairs={{8,0},{16,8},{4,12},{24,16},{12,20},{20,28},{9,1},{17,9},{5,13},{2... | collective-permute-start | bytes 811016 | tf_op jit(solution)/shard_map/ppermute | solution.py:38
  9.8 0.0 collective-permute-done
  9.8 2.1 %collective-permute-done.2 = bf16[64,1280]{1,0:T(8,128)(2,1)S(1)} collective-permute-done((bf16[64,1280]{1,0:T(8,128)(2,1)S(1)}, bf16[64,1280]{1,0:T(8,128)(2,1)S(1)}, u32[]{:S(2)}, u32[]{:S(2)}) %collective-permute-start.2) | collective-permute-done | bytes 163872 | tf_op jit(solution)/shard_map/ppermute | solution.py:24
  11.9 7.1 %collective-permute-done.1 = bf16[64,1280]{1,0:T(8,128)(2,1)S(1)} collective-permute-done((bf16[64,1280]{1,0:T(8,128)(2,1)S(1)}, bf16[64,1280]{1,0:T(8,128)(2,1)S(1)}, u32[]{:S(2)}, u32[]{:S(2)}) %collective-permute-start.1) | collective-permute-done | bytes 163872 | tf_op jit(solution)/shard_map/ppermute | solution.py:24
  19.0 0.1 pad_maximum_fusion.refs_0_
  19.0 1.3 %collective-permute-start.4 = (bf16[3,64,1280]{2,1,0:T(8,128)(2,1)S(1)}, bf16[3,64,1280]{2,1,0:T(8,128)(2,1)S(1)}, u32[]{:S(2)}, u32[]{:S(2)}) collective-permute-start(bf16[3,64,1280]{2,1,0:T(8,128)(2,1)S(1)} %pad_maximum_fusion.refs_0_), channel_id=1, source_target_pairs={{0,16},{4,20},{8,24},{12,28},{16,0},{20,4},{24,8},{28,12},{1,17},{... | collective-permute-start | bytes 1474568 | tf_op jit(solution)/shard_map/ppermute | solution.py:32
  20.3 2.1 %collective-permute-start.11 = (bf16[512,256]{1,0:T(8,128)(2,1)S(1)}, bf16[512,256]{1,0:T(8,128)(2,1)S(1)}, u32[]{:S(2)}, u32[]{:S(2)}) collective-permute-start(bf16[512,256]{1,0:T(8,128)(2,1)S(1)} %get-tuple-element.13.refs_2_), channel_id=1, source_target_pairs={{8,0},{16,8},{4,12},{24,16},{12,20},{20,28},{9,1},{17,9},{5,13},{2... | collective-permute-start | bytes 786440 | tf_op jit(solution)/shard_map/ppermute | solution.py:38
  22.4 3.2 %collective-permute-start.8 = (bf16[528,256]{1,0:T(8,128)(2,1)S(1)}, bf16[528,256]{1,0:T(8,128)(2,1)S(1)}, u32[]{:S(2)}, u32[]{:S(2)}) collective-permute-start(bf16[528,256]{1,0:T(8,128)(2,1)S(1)} %get-tuple-element.11.refs_2_), channel_id=1, source_target_pairs={{12,4},{0,8},{20,12},{8,16},{28,20},{16,24},{13,5},{1,9},{21,13},{... | collective-permute-start | bytes 811016 | tf_op jit(solution)/shard_map/ppermute | solution.py:38
  25.6 3.3 %collective-permute-start.6 = (bf16[528,256]{1,0:T(8,128)(2,1)S(1)}, bf16[528,256]{1,0:T(8,128)(2,1)S(1)}, u32[]{:S(2)}, u32[]{:S(2)}) collective-permute-start(bf16[528,256]{1,0:T(8,128)(2,1)S(1)} %get-tuple-element.11.refs_2_), channel_id=1, source_target_pairs={{0,4},{4,0},{8,12},{12,8},{16,20},{20,16},{24,28},{28,24},{1,5},{5... | collective-permute-start | bytes 811016 | tf_op jit(solution)/shard_map/ppermute | solution.py:32
  29.0 0.0 collective-permute-done.7.refs_4_
  29.0 0.1 collective-permute-start.9
  29.1 0.0 collective-permute-done.11.refs_4_
  29.1 1.9 %collective-permute-start.12 = (bf16[512,256]{1,0:T(8,128)(2,1)S(1)}, bf16[512,256]{1,0:T(8,128)(2,1)S(1)}, u32[]{:S(2)}, u32[]{:S(2)}) collective-permute-start(bf16[512,256]{1,0:T(8,128)(2,1)S(1)} %get-tuple-element.13.refs_2_), channel_id=1, source_target_pairs={{12,4},{0,8},{20,12},{8,16},{28,20},{16,24},{13,5},{1,9},{21,13},{... | collective-permute-start | bytes 786440 | tf_op jit(solution)/shard_map/ppermute | solution.py:38
  31.0 2.7 %collective-permute-done.8.refs_5_ = bf16[528,256]{1,0:T(8,128)(2,1)S(1)} collective-permute-done((bf16[528,256]{1,0:T(8,128)(2,1)S(1)}, bf16[528,256]{1,0:T(8,128)(2,1)S(1)}, u32[]{:S(2)}, u32[]{:S(2)}) %collective-permute-start.8) | collective-permute-done | bytes 270368 | tf_op jit(solution)/shard_map/ppermute | solution.py:38
  33.6 3.4 %collective-permute-start.10 = (bf16[512,256]{1,0:T(8,128)(2,1)S(1)}, bf16[512,256]{1,0:T(8,128)(2,1)S(1)}, u32[]{:S(2)}, u32[]{:S(2)}) collective-permute-start(bf16[512,256]{1,0:T(8,128)(2,1)S(1)} %get-tuple-element.13.refs_2_), channel_id=1, source_target_pairs={{0,4},{4,0},{8,12},{12,8},{16,20},{20,16},{24,28},{28,24},{1,5},{5... | collective-permute-start | bytes 786440 | tf_op jit(solution)/shard_map/ppermute | solution.py:32
  37.1 0.0 collective-permute-done.6.refs_3_
  37.1 0.0 collective-permute-start.3
  37.1 0.0 collective-permute-done.9.refs_6_
  37.1 0.5 collective-permute-start.13
  37.6 0.0 collective-permute-done.4.refs_2_
  37.6 3.7 %collective-permute-start.5 = (bf16[3,64,1280]{2,1,0:T(8,128)(2,1)S(1)}, bf16[3,64,1280]{2,1,0:T(8,128)(2,1)S(1)}, u32[]{:S(2)}, u32[]{:S(2)}) collective-permute-start(bf16[3,64,1280]{2,1,0:T(8,128)(2,1)S(1)} %collective-permute-done.4.refs_2_), channel_id=1, source_target_pairs={{0,4},{4,0},{8,12},{12,8},{16,20},{20,16},{24,28},{28,24},{1,5},{5... | collective-permute-start | bytes 1474568 | tf_op jit(solution)/shard_map/ppermute | solution.py:32
  41.3 0.9 %copy-done.2 = f32[512,128]{1,0:T(8,128)S(1)} copy-done((f32[512,128]{1,0:T(8,128)S(1)}, f32[512,128]{1,0:T(8,128)}, u32[]{:S(2)}) %copy-start.2) | copy-done | bytes 262168
  42.2 2.4 %attend.2 = (bf16[512,128]{1,0:T(8,128)(2,1)S(1)}, f32[16,256]{1,0:T(8,128)S(1)}) custom-call(bf16[512,256]{1,0:T(8,128)(2,1)S(1)} %copy-done, f32[512,128]{1,0:T(8,128)S(1)} %copy-done.2, bf16[528,256]{1,0:T(8,128)(2,1)S(1)} %get-tuple-element.11.refs_2_, bf16[528,256]{1,0:T(8,128)(2,1)S(1)} %collective-permute-done.6.refs_3_, ...), custom_call_target="tpu_custom_call" | custom-call | flops 1342177280 | bytes 1310720 | tf_op jit(solution)/shard_map/attend/pallas_call | solution.py:139
  44.6 0.0 collective-permute-done.12.refs_5_
  44.6 2.4 %collective-permute-start.16 = (bf16[512,128]{1,0:T(8,128)(2,1)S(1)}, bf16[512,128]{1,0:T(8,128)(2,1)S(1)}, u32[]{:S(2)}, u32[]{:S(2)}) collective-permute-start(bf16[512,128]{1,0:T(8,128)(2,1)S(1)} %get-tuple-element.12.refs_0_), channel_id=1, source_target_pairs={{0,3},{1,2},{2,1},{3,0},{4,7},{5,6},{6,5},{7,4},{8,11},{9,10},{10,... | collective-permute-start | bytes 393224 | tf_op jit(solution)/shard_map/ppermute | solution.py:24
  47.0 1.1 %constant_dynamic-slice_fusion.own_ref = bf16[256,1280]{1,0:T(8,128)(2,1)S(1)} fusion(bf16[256,5120]{1,0:T(8,128)(2,1)} %param.9, s32[]{:T(128)S(6)} %select_n.17), kind=kLoop, calls=%fused_computation.1 | loop fusion | bytes 1310724 | tf_op jit(solution)/shard_map/dynamic_slice | solution.py:293
  48.2 0.1 collective-permute-start.15
  48.2 0.0 collective-permute-done.13.refs_6_
  48.2 1.2 %collective-permute-start.14 = (bf16[512,128]{1,0:T(8,128)(2,1)S(1)}, bf16[512,128]{1,0:T(8,128)(2,1)S(1)}, u32[]{:S(2)}, u32[]{:S(2)}) collective-permute-start(bf16[512,128]{1,0:T(8,128)(2,1)S(1)} %get-tuple-element.12.refs_0_), channel_id=1, source_target_pairs={{0,1},{1,0},{2,3},{3,2},{4,5},{5,4},{6,7},{7,6},{8,9},{9,8},{10,11... | collective-permute-start | bytes 393224 | tf_op jit(solution)/shard_map/ppermute | solution.py:24
  49.5 2.4 %attend.3.refs_1_ = bf16[512,128]{1,0:T(8,128)(2,1)S(1)} custom-call(bf16[512,256]{1,0:T(8,128)(2,1)S(1)} %copy-done, f32[512,128]{1,0:T(8,128)S(1)} %copy-done.3, bf16[512,256]{1,0:T(8,128)(2,1)S(1)} %get-tuple-element.13.refs_2_, bf16[512,256]{1,0:T(8,128)(2,1)S(1)} %collective-permute-done.10.refs_3_, ...), custom_call_target="tpu_custom_call" | custom-call | flops 1342177280 | bytes 1310720 | tf_op jit(solution)/shard_map/attend/pallas_call | solution.py:139
  51.9 2.4 %collective-permute-start.19 = (bf16[512,128]{1,0:T(8,128)(2,1)S(1)}, bf16[512,128]{1,0:T(8,128)(2,1)S(1)}, u32[]{:S(2)}, u32[]{:S(2)}) collective-permute-start(bf16[512,128]{1,0:T(8,128)(2,1)S(1)} %attend.3.refs_1_), channel_id=1, source_target_pairs={{0,3},{1,2},{2,1},{3,0},{4,7},{5,6},{6,5},{7,4},{8,11},{9,10},{10,... | collective-permute-start | bytes 393224 | tf_op jit(solution)/shard_map/ppermute | solution.py:24
  54.3 0.0 collective-permute-start.18
  54.3 0.0 collective-permute-done.5.refs_3_
  54.3 1.2 %collective-permute-start.17 = (bf16[512,128]{1,0:T(8,128)(2,1)S(1)}, bf16[512,128]{1,0:T(8,128)(2,1)S(1)}, u32[]{:S(2)}, u32[]{:S(2)}) collective-permute-start(bf16[512,128]{1,0:T(8,128)(2,1)S(1)} %attend.3.refs_1_), channel_id=1, source_target_pairs={{0,1},{1,0},{2,3},{3,2},{4,5},{5,4},{6,7},{7,6},{8,9},{9,8},{10,11... | collective-permute-start | bytes 393224 | tf_op jit(solution)/shard_map/ppermute | solution.py:24
  55.5 0.2 assemble.1.w_ref
  55.7 2.5 %collective-permute-done.15.refs_3_ = bf16[512,128]{1,0:T(8,128)(2,1)S(1)} collective-permute-done((bf16[512,128]{1,0:T(8,128)(2,1)S(1)}, bf16[512,128]{1,0:T(8,128)(2,1)S(1)}, u32[]{:S(2)}, u32[]{:S(2)}) %collective-permute-start.15) | collective-permute-done | bytes 131104 | tf_op jit(solution)/shard_map/ppermute | solution.py:24
  58.2 1.5 %project_first.1.p_ref = f32[512,1280]{1,0:T(8,128)S(1)} custom-call(bf16[4,256,1280]{2,1,0:T(8,128)(2,1)S(1)} %assemble.1.w_ref, bf16[512,128]{1,0:T(8,128)(2,1)S(1)} %get-tuple-element.12.refs_0_, bf16[512,128]{1,0:T(8,128)(2,1)S(1)} %attend.3.refs_1_, bf16[512,128]{1,0:T(8,128)(2,1)S(1)} %collective-permute-done.14.refs_2_, ...), custom_call_target="tpu_custom_call" | custom-call | flops 671088640 | bytes 2621440 | tf_op jit(solution)/shard_map/project_first/pallas_call | solution.py:211
  59.7 0.4 collective-permute-done.19.refs_2_
  60.1 8.9 %collective-permute-done.18.refs_1_ = bf16[512,128]{1,0:T(8,128)(2,1)S(1)} collective-permute-done((bf16[512,128]{1,0:T(8,128)(2,1)S(1)}, bf16[512,128]{1,0:T(8,128)(2,1)S(1)}, u32[]{:S(2)}, u32[]{:S(2)}) %collective-permute-start.18) | collective-permute-done | bytes 131104 | tf_op jit(solution)/shard_map/ppermute | solution.py:24
  69.0 0.0 collective-permute-done.17.refs_0_
  69.0 1.7 %project_last.1 = bf16[512,1280]{1,0:T(8,128)(2,1)} custom-call(bf16[4,256,1280]{2,1,0:T(8,128)(2,1)S(1)} %assemble.1.w_ref, f32[512,1280]{1,0:T(8,128)S(1)} %project_first.1.p_ref, bf16[512,128]{1,0:T(8,128)(2,1)S(1)} %collective-permute-done.17.refs_0_, bf16[512,128]{1,0:T(8,128)(2,1)S(1)} %collective-permute-done.18.refs_1_, ...), custom_call_target="tpu_custom_call" | custom-call | flops 671088640 | bytes 2621440 | tf_op jit(solution)/shard_map/project_last/pallas_call | solution.py:249
  (9 shorter events, 0.0 us)
Async XLA Ops:
  0.0 41.3 %copy-start = (bf16[512,256]{1,0:T(8,128)(2,1)S(1)}, bf16[512,256]{1,0:T(8,128)(2,1)}, u32[]{:S(2)}) copy-start(bf16[512,256]{1,0:T(8,128)(2,1)} %refs_0_.3) | copy-start | bytes 786436
  1.2 8.7 %collective-permute-start = (bf16[64,1280]{1,0:T(8,128)(2,1)S(1)}, bf16[64,1280]{1,0:T(8,128)(2,1)S(1)}, u32[]{:S(2)}, u32[]{:S(2)}) collective-permute-start(bf16[64,1280]{1,0:T(8,128)(2,1)S(1)} %get-tuple-element.15), channel_id=1, source_target_pairs={{0,1},{1,0},{2,3},{3,2},{4,5},{5,4},{6,7},{7,6},{8,9},{9,8},{10,11... | collective-permute-start | bytes 491528 | tf_op jit(solution)/shard_map/ppermute | solution.py:24
  2.5 9.4 %collective-permute-start.2 = (bf16[64,1280]{1,0:T(8,128)(2,1)S(1)}, bf16[64,1280]{1,0:T(8,128)(2,1)S(1)}, u32[]{:S(2)}, u32[]{:S(2)}) collective-permute-start(bf16[64,1280]{1,0:T(8,128)(2,1)S(1)} %get-tuple-element.16), channel_id=1, source_target_pairs={{0,3},{1,2},{2,1},{3,0},{4,7},{5,6},{6,5},{7,4},{8,11},{9,10},{10,... | collective-permute-start | bytes 491528 | tf_op jit(solution)/shard_map/ppermute | solution.py:24
  4.7 14.3 %collective-permute-start.1 = (bf16[64,1280]{1,0:T(8,128)(2,1)S(1)}, bf16[64,1280]{1,0:T(8,128)(2,1)S(1)}, u32[]{:S(2)}, u32[]{:S(2)}) collective-permute-start(bf16[64,1280]{1,0:T(8,128)(2,1)S(1)} %get-tuple-element.17), channel_id=1, source_target_pairs={{0,2},{1,3},{2,0},{3,1},{4,6},{5,7},{6,4},{7,5},{8,10},{9,11},{10,... | collective-permute-start | bytes 491528 | tf_op jit(solution)/shard_map/ppermute | solution.py:24
  6.0 0.7 copy-start.1
  6.7 22.3 %collective-permute-start.7 = (bf16[528,256]{1,0:T(8,128)(2,1)S(1)}, bf16[528,256]{1,0:T(8,128)(2,1)S(1)}, u32[]{:S(2)}, u32[]{:S(2)}) collective-permute-start(bf16[528,256]{1,0:T(8,128)(2,1)S(1)} %get-tuple-element.11.refs_2_), channel_id=1, source_target_pairs={{8,0},{16,8},{4,12},{24,16},{12,20},{20,28},{9,1},{17,9},{5,13},{2... | collective-permute-start | bytes 811016 | tf_op jit(solution)/shard_map/ppermute | solution.py:38
  19.0 18.5 %collective-permute-start.4 = (bf16[3,64,1280]{2,1,0:T(8,128)(2,1)S(1)}, bf16[3,64,1280]{2,1,0:T(8,128)(2,1)S(1)}, u32[]{:S(2)}, u32[]{:S(2)}) collective-permute-start(bf16[3,64,1280]{2,1,0:T(8,128)(2,1)S(1)} %pad_maximum_fusion.refs_0_), channel_id=1, source_target_pairs={{0,16},{4,20},{8,24},{12,28},{16,0},{20,4},{24,8},{28,12},{1,17},{... | collective-permute-start | bytes 1474568 | tf_op jit(solution)/shard_map/ppermute | solution.py:32
  20.3 8.7 %collective-permute-start.11 = (bf16[512,256]{1,0:T(8,128)(2,1)S(1)}, bf16[512,256]{1,0:T(8,128)(2,1)S(1)}, u32[]{:S(2)}, u32[]{:S(2)}) collective-permute-start(bf16[512,256]{1,0:T(8,128)(2,1)S(1)} %get-tuple-element.13.refs_2_), channel_id=1, source_target_pairs={{8,0},{16,8},{4,12},{24,16},{12,20},{20,28},{9,1},{17,9},{5,13},{2... | collective-permute-start | bytes 786440 | tf_op jit(solution)/shard_map/ppermute | solution.py:38
  22.4 11.2 %collective-permute-start.8 = (bf16[528,256]{1,0:T(8,128)(2,1)S(1)}, bf16[528,256]{1,0:T(8,128)(2,1)S(1)}, u32[]{:S(2)}, u32[]{:S(2)}) collective-permute-start(bf16[528,256]{1,0:T(8,128)(2,1)S(1)} %get-tuple-element.11.refs_2_), channel_id=1, source_target_pairs={{12,4},{0,8},{20,12},{8,16},{28,20},{16,24},{13,5},{1,9},{21,13},{... | collective-permute-start | bytes 811016 | tf_op jit(solution)/shard_map/ppermute | solution.py:38
  25.6 11.4 %collective-permute-start.6 = (bf16[528,256]{1,0:T(8,128)(2,1)S(1)}, bf16[528,256]{1,0:T(8,128)(2,1)S(1)}, u32[]{:S(2)}, u32[]{:S(2)}) collective-permute-start(bf16[528,256]{1,0:T(8,128)(2,1)S(1)} %get-tuple-element.11.refs_2_), channel_id=1, source_target_pairs={{0,4},{4,0},{8,12},{12,8},{16,20},{20,16},{24,28},{28,24},{1,5},{5... | collective-permute-start | bytes 811016 | tf_op jit(solution)/shard_map/ppermute | solution.py:32
  29.0 8.1 %collective-permute-start.9 = (bf16[528,256]{1,0:T(8,128)(2,1)S(1)}, bf16[528,256]{1,0:T(8,128)(2,1)S(1)}, u32[]{:S(2)}, u32[]{:S(2)}) collective-permute-start(bf16[528,256]{1,0:T(8,128)(2,1)S(1)} %collective-permute-done.7.refs_4_), channel_id=1, source_target_pairs={{0,4},{4,0},{8,12},{12,8},{16,20},{20,16},{24,28},{28,24},{1,5},{5... | collective-permute-start | bytes 811016 | tf_op jit(solution)/shard_map/ppermute | solution.py:32
  29.1 15.6 %collective-permute-start.12 = (bf16[512,256]{1,0:T(8,128)(2,1)S(1)}, bf16[512,256]{1,0:T(8,128)(2,1)S(1)}, u32[]{:S(2)}, u32[]{:S(2)}) collective-permute-start(bf16[512,256]{1,0:T(8,128)(2,1)S(1)} %get-tuple-element.13.refs_2_), channel_id=1, source_target_pairs={{12,4},{0,8},{20,12},{8,16},{28,20},{16,24},{13,5},{1,9},{21,13},{... | collective-permute-start | bytes 786440 | tf_op jit(solution)/shard_map/ppermute | solution.py:38
  33.6 14.5 %collective-permute-start.10 = (bf16[512,256]{1,0:T(8,128)(2,1)S(1)}, bf16[512,256]{1,0:T(8,128)(2,1)S(1)}, u32[]{:S(2)}, u32[]{:S(2)}) collective-permute-start(bf16[512,256]{1,0:T(8,128)(2,1)S(1)} %get-tuple-element.13.refs_2_), channel_id=1, source_target_pairs={{0,4},{4,0},{8,12},{12,8},{16,20},{20,16},{24,28},{28,24},{1,5},{5... | collective-permute-start | bytes 786440 | tf_op jit(solution)/shard_map/ppermute | solution.py:32
  37.1 14.8 %collective-permute-start.3 = (bf16[3,64,1280]{2,1,0:T(8,128)(2,1)S(1)}, bf16[3,64,1280]{2,1,0:T(8,128)(2,1)S(1)}, u32[]{:S(2)}, u32[]{:S(2)}) collective-permute-start(bf16[3,64,1280]{2,1,0:T(8,128)(2,1)S(1)} %pad_maximum_fusion.refs_0_), channel_id=1, source_target_pairs={{0,4},{4,0},{8,12},{12,8},{16,20},{20,16},{24,28},{28,24},{1,5},{5... | collective-permute-start | bytes 1474568 | tf_op jit(solution)/shard_map/ppermute | solution.py:32
  37.1 11.2 %collective-permute-start.13 = (bf16[512,256]{1,0:T(8,128)(2,1)S(1)}, bf16[512,256]{1,0:T(8,128)(2,1)S(1)}, u32[]{:S(2)}, u32[]{:S(2)}) collective-permute-start(bf16[512,256]{1,0:T(8,128)(2,1)S(1)} %collective-permute-done.11.refs_4_), channel_id=1, source_target_pairs={{0,4},{4,0},{8,12},{12,8},{16,20},{20,16},{24,28},{28,24},{1,5},{5... | collective-permute-start | bytes 786440 | tf_op jit(solution)/shard_map/ppermute | solution.py:32
  37.6 16.7 %collective-permute-start.5 = (bf16[3,64,1280]{2,1,0:T(8,128)(2,1)S(1)}, bf16[3,64,1280]{2,1,0:T(8,128)(2,1)S(1)}, u32[]{:S(2)}, u32[]{:S(2)}) collective-permute-start(bf16[3,64,1280]{2,1,0:T(8,128)(2,1)S(1)} %collective-permute-done.4.refs_2_), channel_id=1, source_target_pairs={{0,4},{4,0},{8,12},{12,8},{16,20},{20,16},{24,28},{28,24},{1,5},{5... | collective-permute-start | bytes 1474568 | tf_op jit(solution)/shard_map/ppermute | solution.py:32
  41.3 1.0 %copy-start.2 = (f32[512,128]{1,0:T(8,128)S(1)}, f32[512,128]{1,0:T(8,128)}, u32[]{:S(2)}) copy-start(f32[512,128]{1,0:T(8,128)} %copy-done.1) | copy-start | bytes 786436
  42.2 7.3 %copy-start.3 = (f32[512,128]{1,0:T(8,128)S(1)}, f32[512,128]{1,0:T(8,128)}, u32[]{:S(2)}) copy-start(f32[512,128]{1,0:T(8,128)} %copy-done.1) | copy-start | bytes 786436
  44.6 9.6 %collective-permute-start.16 = (bf16[512,128]{1,0:T(8,128)(2,1)S(1)}, bf16[512,128]{1,0:T(8,128)(2,1)S(1)}, u32[]{:S(2)}, u32[]{:S(2)}) collective-permute-start(bf16[512,128]{1,0:T(8,128)(2,1)S(1)} %get-tuple-element.12.refs_0_), channel_id=1, source_target_pairs={{0,3},{1,2},{2,1},{3,0},{4,7},{5,6},{6,5},{7,4},{8,11},{9,10},{10,... | collective-permute-start | bytes 393224 | tf_op jit(solution)/shard_map/ppermute | solution.py:24
  48.2 10.1 %collective-permute-start.15 = (bf16[512,128]{1,0:T(8,128)(2,1)S(1)}, bf16[512,128]{1,0:T(8,128)(2,1)S(1)}, u32[]{:S(2)}, u32[]{:S(2)}) collective-permute-start(bf16[512,128]{1,0:T(8,128)(2,1)S(1)} %get-tuple-element.12.refs_0_), channel_id=1, source_target_pairs={{0,2},{1,3},{2,0},{3,1},{4,6},{5,7},{6,4},{7,5},{8,10},{9,11},{10,... | collective-permute-start | bytes 393224 | tf_op jit(solution)/shard_map/ppermute | solution.py:24
  48.2 10.0 %collective-permute-start.14 = (bf16[512,128]{1,0:T(8,128)(2,1)S(1)}, bf16[512,128]{1,0:T(8,128)(2,1)S(1)}, u32[]{:S(2)}, u32[]{:S(2)}) collective-permute-start(bf16[512,128]{1,0:T(8,128)(2,1)S(1)} %get-tuple-element.12.refs_0_), channel_id=1, source_target_pairs={{0,1},{1,0},{2,3},{3,2},{4,5},{5,4},{6,7},{7,6},{8,9},{9,8},{10,11... | collective-permute-start | bytes 393224 | tf_op jit(solution)/shard_map/ppermute | solution.py:24
  51.9 8.2 %collective-permute-start.19 = (bf16[512,128]{1,0:T(8,128)(2,1)S(1)}, bf16[512,128]{1,0:T(8,128)(2,1)S(1)}, u32[]{:S(2)}, u32[]{:S(2)}) collective-permute-start(bf16[512,128]{1,0:T(8,128)(2,1)S(1)} %attend.3.refs_1_), channel_id=1, source_target_pairs={{0,3},{1,2},{2,1},{3,0},{4,7},{5,6},{6,5},{7,4},{8,11},{9,10},{10,... | collective-permute-start | bytes 393224 | tf_op jit(solution)/shard_map/ppermute | solution.py:24
  54.3 14.7 %collective-permute-start.18 = (bf16[512,128]{1,0:T(8,128)(2,1)S(1)}, bf16[512,128]{1,0:T(8,128)(2,1)S(1)}, u32[]{:S(2)}, u32[]{:S(2)}) collective-permute-start(bf16[512,128]{1,0:T(8,128)(2,1)S(1)} %attend.3.refs_1_), channel_id=1, source_target_pairs={{0,2},{1,3},{2,0},{3,1},{4,6},{5,7},{6,4},{7,5},{8,10},{9,11},{10,... | collective-permute-start | bytes 393224 | tf_op jit(solution)/shard_map/ppermute | solution.py:24
  54.3 14.7 %collective-permute-start.17 = (bf16[512,128]{1,0:T(8,128)(2,1)S(1)}, bf16[512,128]{1,0:T(8,128)(2,1)S(1)}, u32[]{:S(2)}, u32[]{:S(2)}) collective-permute-start(bf16[512,128]{1,0:T(8,128)(2,1)S(1)} %attend.3.refs_1_), channel_id=1, source_target_pairs={{0,1},{1,0},{2,3},{3,2},{4,5},{5,4},{6,7},{7,6},{8,9},{9,8},{10,11... | collective-permute-start | bytes 393224 | tf_op jit(solution)/shard_map/ppermute | solution.py:24

commit v3 on v2

--- a/solution.py
+++ b/solution.py
@@ -13,6 +13,12 @@
 PAD_ROWS = 16
 KERNEL_VMEM = 12 * 2**20
 IN_VMEM = pl.BlockSpec(memory_space=pltpu.VMEM)
+IN_HBM = pl.BlockSpec(memory_space=pltpu.HBM)
+LANES = 128
+
+
+def in_hbm(array):
+    return pltpu.with_memory_space_constraint(array, pltpu.HBM)
 
 
 def partner(index, distance, count):
@@ -44,7 +50,7 @@
     wide = 2 * head
     lines = rows // wide
 
-    def body(k_ref, v_ref, s_ref, column_ref, *refs):
+    def body(k_ref, v_ref, s_ref, *refs):
         messages, (ids_ref, sems) = refs[:HEAD_DEV], refs[HEAD_DEV:]
         copies = [pltpu.make_async_copy(s_ref, ids_ref, sems.at[0])]
         for index, ref in enumerate(messages):
@@ -61,7 +67,6 @@
         parts = [marks[:, i * wide:(i + 1) * wide] for i in range(lines)]
         parts.append(jnp.zeros((PAD_ROWS - lines, wide), jnp.float32))
         messages[0][rows:, :] = jnp.concatenate(parts, axis=0).astype(jnp.bfloat16)
-        column_ref[...] = jnp.transpose(jnp.broadcast_to(marks, (head, rows)))
         for copy in copies[1:]:
             copy.wait()
 
@@ -69,19 +74,64 @@
     return pl.pallas_call(
         body,
         name="pack",
-        in_specs=[pl.BlockSpec(memory_space=pltpu.HBM)] * 3,
-        out_specs=[IN_VMEM] * (1 + HEAD_DEV),
-        out_shape=[jax.ShapeDtypeStruct((rows, head), jnp.float32)]
-        + [jax.ShapeDtypeStruct(shape, jnp.bfloat16) for shape in shapes],
+        in_specs=[IN_HBM] * 3,
+        out_specs=[IN_VMEM] * HEAD_DEV,
+        out_shape=[jax.ShapeDtypeStruct(shape, jnp.bfloat16) for shape in shapes],
         scratch_shapes=[
             pltpu.VMEM((1, rows), jnp.int32), pltpu.SemaphoreType.DMA((1 + 2 * HEAD_DEV,)),
         ],
         compiler_params=pltpu.CompilerParams(vmem_limit_bytes=KERNEL_VMEM),
         cost_estimate=pl.CostEstimate(flops=10**9, bytes_accessed=8 * rows * width, transcendentals=0),
-    )(*[pltpu.with_memory_space_constraint(x, pltpu.HBM) for x in (keys, values, segment_ids.reshape(1, rows))])
-
-
-def attend(query, query_marks, blocks, index, marks=None):
+    )(*[in_hbm(x) for x in (keys, values, segment_ids.reshape(1, rows))])
+
+
+def cut(array, corners, rows, columns):
+    count = corners.shape[0] // 2
+
+    def body(corner_ref, source_ref, *refs):
+        copies = []
+        for index in range(count):
+            row = pl.multiple_of(corner_ref[2 * index], rows)
+            column = pl.multiple_of(corner_ref[2 * index + 1], columns)
+            copies.append(pltpu.make_async_copy(
+                source_ref.at[pl.ds(row, rows), pl.ds(column, columns)], refs[index], refs[-1].at[index]
+            ))
+        for copy in copies:
+            copy.start()
+        for copy in copies:
+            copy.wait()
+
+    return pl.pallas_call(
+        body,
+        name="cut",
+        in_specs=[pl.BlockSpec(memory_space=pltpu.SMEM), IN_HBM],
+        out_specs=[IN_VMEM] * count,
+        out_shape=[jax.ShapeDtypeStruct((rows, columns), array.dtype)] * count,
+        scratch_shapes=[pltpu.SemaphoreType.DMA((count,))],
+        compiler_params=pltpu.CompilerParams(vmem_limit_bytes=KERNEL_VMEM),
+        cost_estimate=pl.CostEstimate(
+            flops=10**9, bytes_accessed=4 * count * rows * columns, transcendentals=0
+        ),
+    )(corners, in_hbm(array))
+
+
+def stacked(arrays):
+    def body(*refs):
+        for index, ref in enumerate(refs[:-1]):
+            refs[-1][index] = ref[...]
+
+    return pl.pallas_call(
+        body,
+        name="stacked",
+        in_specs=[IN_VMEM] * len(arrays),
+        out_specs=IN_VMEM,
+        out_shape=jax.ShapeDtypeStruct((len(arrays), *arrays[0].shape), arrays[0].dtype),
+        compiler_params=pltpu.CompilerParams(vmem_limit_bytes=KERNEL_VMEM),
+        cost_estimate=pl.CostEstimate(flops=10**8, bytes_accessed=10**6, transcendentals=0),
+    )(*arrays)
+
+
+def attend(query, blocks, index, marks=None):
     rows = query.shape[0]
     head = query.shape[1] // HEAD_DEV
     wide = 2 * head
@@ -93,19 +143,20 @@
     kept = -(-count * lines // 8) * 8
 
     def body(*refs):
-        q_ref, qm_ref = refs[:2]
-        block_refs = refs[2:2 + count]
+        q_ref, block_refs = refs[0], refs[1:1 + count]
         if first:
-            out_ref, marks_ref, score_ref = refs[2 + count:]
+            out_ref, marks_ref, score_ref = refs[1 + count:]
             pieces = [ref[rows:rows + lines, :].astype(jnp.float32) for ref in block_refs]
             pieces.append(jnp.zeros((kept - count * lines, wide), jnp.float32))
             marks_ref[...] = jnp.concatenate(pieces, axis=0)
         else:
-            marks_ref, out_ref, score_ref = refs[2 + count:]
+            marks_ref, out_ref, score_ref = refs[1 + count:]
+        own = [jnp.broadcast_to(marks_ref[i:i + 1, :], (head, wide)) for i in range(lines)]
+        own = jnp.concatenate([jnp.transpose(row) for row in own], axis=0)
         for start in range(0, rows, QUERY_TILE):
             tile = slice(start, start + QUERY_TILE)
             q_tile = q_ref[tile, index * head:(index + 1) * head]
-            q_mark = qm_ref[tile, :]
+            q_mark = own[tile, :]
             q_mark = jnp.concatenate([q_mark] * 2, axis=1)
             peak = None
             for piece in range(count * lines):
@@ -139,7 +190,7 @@
     result = pl.pallas_call(
         body,
         name="attend",
-        in_specs=[IN_VMEM] * (2 + count + (not first)),
+        in_specs=[IN_VMEM] * (1 + count + (not first)),
         out_specs=[IN_VMEM] * len(outs),
         out_shape=outs,
         scratch_shapes=[pltpu.VMEM((QUERY_TILE, span), jnp.float32)],
@@ -147,8 +198,8 @@
         cost_estimate=pl.CostEstimate(
             flops=8 * rows * span * head, bytes_accessed=4 * span * head, transcendentals=rows * span
         ),
-    )(query, query_marks, *blocks, *([] if first else [marks]))
-    return result if first else (result[0], marks)
+    )(query, *blocks, *([] if first else [marks]))
+    return result if first else [result[0], marks]
 
 
 def assemble(order, own, pieces):
@@ -273,7 +324,17 @@
     mine = (place & 1) + 2 * ((place >> 2) & 1)
     part, columns = out_weight.shape[0] // replicas, out_weight.shape[1] // groups
 
-    query_marks, *messages = pack(keys, values, segment_ids)
+    messages = pack(keys, values, segment_ids)
+
+    aligned = columns % LANES == 0
+    corners = [
+        (mine * part, partner(me, distance, groups) * columns) for distance in range(1, groups)
+    ]
+    if aligned:
+        table = jnp.stack([value for corner in corners for value in corner]).astype(jnp.int32)
+        pieces = cut(out_weight, table, part, columns)
+    else:
+        pieces = [lax.dynamic_slice(out_weight, corner, (part, columns)) for corner in corners]
 
     near, far, beside = [], [], []
     for message in messages:
@@ -282,22 +343,17 @@
         beside.append(exchanged(message, "seq", 1))
 
     received = []
-    for distance in range(1, groups):
-        target = partner(me, distance, groups)
-        piece = lax.dynamic_slice(out_weight, (mine * part, target * columns), (part, columns))
+    for distance, piece in enumerate(pieces, 1):
         received.append(to_partner(piece, "head", distance))
-    first = jnp.stack(received)
+    first = stacked(received)
     second = exchanged(first, "seq", 4)
     third = exchanged(first, "seq", 1)
     fourth = exchanged(second, "seq", 1)
-    own = lax.dynamic_slice(out_weight, (0, me * columns), (out_weight.shape[0], columns))
-    weight = assemble(mine.astype(jnp.int32)[None], own, [first, third, second, fourth])
-
     own, others, marks = [], [], None
     for index, message in enumerate(messages):
         across = exchanged(near[index], "seq", 1)
         blocks = (message, beside[index], near[index], far[index], across)
-        done, marks = attend(queries, query_marks, blocks, index, marks)
+        done, marks = attend(queries, blocks, index, marks)
         own.append(done)
         if index in relays():
             two = lax.ppermute(done, "head", [(0, 2), (2, 0), (1, 3), (3, 1)])
@@ -311,6 +367,12 @@
                 line.append([to_partner(done, "head", distance)])
             others.append(line)
 
+    if aligned:
+        table = jnp.stack([jnp.int32(0), (me * columns).astype(jnp.int32)])
+        own_weight = cut(out_weight, table, out_weight.shape[0], columns)[0]
+    else:
+        own_weight = lax.dynamic_slice(out_weight, (0, me * columns), (out_weight.shape[0], columns))
+    weight = assemble(mine.astype(jnp.int32)[None], own_weight, [first, third, second, fourth])
     partial = project_first(weight, own, others[0])
     rest = [line[distance] for distance in range(groups - 1) for line in others[1:]]
     return project_last(weight, partial, rest)

time: 71 us -> 74.5 us (1.049)
  the two profiles are of different devices: /device:TPU:3 before, /device:TPU:0 now
where the time goes in v3:
time: 74.5 us; the launch traced here: 74.1 us
  starting transfers between devices  31.5 us (42%)
  waiting for transfers between devices  26.4 us (35%)
  Pallas kernels  14.9 us (20%)
  local copies, waits for them, and re-layouts  1.04 us (1%)
    ppermute x9, waiting for transfers between devices, to_partner(): lax.ppermute(block, axis, [(i, partner(i, distance, count)) for i in rang...  19.1 us
    ppermute x9, starting transfers between devices, to_partner(): lax.ppermute(block, axis, [(i, partner(i, distance, count)) for i in rang...  16.7 us
    ppermute x4, starting transfers between devices, from_far(): lax.ppermute(block, axis, [(s, d) for s, d in route if 0 <= s < count])  12.2 us
    pallas_call x2, Pallas kernels, attend(): pl.pallas_call(body, name='attend', in_specs=[IN_VMEM] * (1 + count + (no...  6.38 us
    ppermute x4, waiting for transfers between devices, from_far(): lax.ppermute(block, axis, [(s, d) for s, d in route if 0 <= s < count])  4.84 us
    pallas_call x2, Pallas kernels, cut(): pl.pallas_call(body, name='cut', in_specs=[pl.BlockSpec(memory_space=pltp...  3.29 us
    ppermute x7, starting transfers between devices, exchanged(): lax.ppermute(block, axis, [(i, i ^ flip) for i in range(lax.axis_size(axi...  2.66 us
    ppermute x7, waiting for transfers between devices, exchanged(): lax.ppermute(block, axis, [(i, i ^ flip) for i in range(lax.axis_size(axi...  2.53 us
  transfers between devices with their start and end apart: 20, of which 6 were waited for; matrix products, arithmetic and copies ran while one was open for 0% of the time, Pallas kernels for 16%

profile of v3, /device:TPU:0, one launch (start us, length us, event | category | flops | bytes accessed | tf_op | source)
XLA Modules:
  0.0 74.1 jit_solution(4509880303931936614)
XLA Ops:
  0.0 0.1 stack.29.corner_ref
  0.1 1.6 %cut.3 = (bf16[64,1280]{1,0:T(8,128)(2,1)S(1)}, bf16[64,1280]{1,0:T(8,128)(2,1)S(1)}, bf16[64,1280]{1,0:T(8,128)(2,1)S(1)}) custom-call(s32[6]{0:T(128)S(1)} %stack.29.corner_ref, bf16[256,5120]{1,0:T(8,128)(2,1)} %source_ref.3), custom_call_target="tpu_custom_call" | custom-call | flops 1000000000 | bytes 983040 | tf_op jit(solution)/shard_map/cut/pallas_call | solution.py:104
  1.7 3.1 %collective-permute-start = (bf16[64,1280]{1,0:T(8,128)(2,1)S(1)}, bf16[64,1280]{1,0:T(8,128)(2,1)S(1)}, u32[]{:S(2)}, u32[]{:S(2)}) collective-permute-start(bf16[64,1280]{1,0:T(8,128)(2,1)S(1)} %get-tuple-element.12), channel_id=1, source_target_pairs={{0,1},{1,0},{2,3},{3,2},{4,5},{5,4},{6,7},{7,6},{8,9},{9,8},{10,11... | collective-permute-start | bytes 491528 | tf_op jit(solution)/shard_map/ppermute | solution.py:30
  4.9 2.6 %collective-permute-start.1 = (bf16[64,1280]{1,0:T(8,128)(2,1)S(1)}, bf16[64,1280]{1,0:T(8,128)(2,1)S(1)}, u32[]{:S(2)}, u32[]{:S(2)}) collective-permute-start(bf16[64,1280]{1,0:T(8,128)(2,1)S(1)} %get-tuple-element.13), channel_id=1, source_target_pairs={{0,2},{1,3},{2,0},{3,1},{4,6},{5,7},{6,4},{7,5},{8,10},{9,11},{10,... | collective-permute-start | bytes 491528 | tf_op jit(solution)/shard_map/ppermute | solution.py:30
  7.4 0.0 collective-permute-start.2
  7.4 1.9 %pack.1 = (bf16[528,256]{1,0:T(8,128)(2,1)S(1)}, bf16[512,256]{1,0:T(8,128)(2,1)}) custom-call(bf16[512,256]{1,0:T(8,128)(2,1)} %k_ref.1, bf16[512,256]{1,0:T(8,128)(2,1)} %v_ref.1, s32[1,512]{1,0:T(1,128)} %bitcast.7), custom_call_target="tpu_custom_call" | custom-call | flops 1000000000 | bytes 1048576 | tf_op jit(solution)/shard_map/pack/pallas_call | solution.py:74
  9.3 1.3 %collective-permute-start.7 = (bf16[528,256]{1,0:T(8,128)(2,1)S(1)}, bf16[528,256]{1,0:T(8,128)(2,1)S(1)}, u32[]{:S(2)}, u32[]{:S(2)}) collective-permute-start(bf16[528,256]{1,0:T(8,128)(2,1)S(1)} %get-tuple-element.15.refs_1_), channel_id=1, source_target_pairs={{8,0},{16,8},{4,12},{24,16},{12,20},{20,28},{9,1},{17,9},{5,13},{2... | collective-permute-start | bytes 811016 | tf_op jit(solution)/shard_map/ppermute | solution.py:44
  10.6 1.0 %collective-permute-done.refs_0_ = bf16[64,1280]{1,0:T(8,128)(2,1)S(1)} collective-permute-done((bf16[64,1280]{1,0:T(8,128)(2,1)S(1)}, bf16[64,1280]{1,0:T(8,128)(2,1)S(1)}, u32[]{:S(2)}, u32[]{:S(2)}) %collective-permute-start) | collective-permute-done | bytes 163872 | tf_op jit(solution)/shard_map/ppermute | solution.py:30
  11.6 8.3 %collective-permute-done.1.refs_1_ = bf16[64,1280]{1,0:T(8,128)(2,1)S(1)} collective-permute-done((bf16[64,1280]{1,0:T(8,128)(2,1)S(1)}, bf16[64,1280]{1,0:T(8,128)(2,1)S(1)}, u32[]{:S(2)}, u32[]{:S(2)}) %collective-permute-start.1) | collective-permute-done | bytes 163872 | tf_op jit(solution)/shard_map/ppermute | solution.py:30
  19.9 0.0 collective-permute-done.2.refs_2_
  19.9 1.6 %collective-permute-start.4 = (bf16[3,64,1280]{2,1,0:T(8,128)(2,1)S(1)}, bf16[3,64,1280]{2,1,0:T(8,128)(2,1)S(1)}, u32[]{:S(2)}, u32[]{:S(2)}) collective-permute-start(bf16[3,64,1280]{2,1,0:T(8,128)(2,1)S(1)} %stacked.1.refs_0_), channel_id=1, source_target_pairs={{0,16},{4,20},{8,24},{12,28},{16,0},{20,4},{24,8},{28,12},{1,17},{... | collective-permute-start | bytes 1474568 | tf_op jit(solution)/shard_map/ppermute | solution.py:38
  21.5 1.3 %collective-permute-start.11 = (bf16[512,256]{1,0:T(8,128)(2,1)}, bf16[512,256]{1,0:T(8,128)(2,1)}, u32[]{:S(2)}, u32[]{:S(2)}) collective-permute-start(bf16[512,256]{1,0:T(8,128)(2,1)} %get-tuple-element.17.refs_1_), channel_id=1, source_target_pairs={{8,0},{16,8},{4,12},{24,16},{12,20},{20,28},{9,1},{17,9},{5,13},{2... | collective-permute-start | bytes 786440 | tf_op jit(solution)/shard_map/ppermute | solution.py:44
  22.8 4.6 %collective-permute-start.8 = (bf16[528,256]{1,0:T(8,128)(2,1)S(1)}, bf16[528,256]{1,0:T(8,128)(2,1)S(1)}, u32[]{:S(2)}, u32[]{:S(2)}) collective-permute-start(bf16[528,256]{1,0:T(8,128)(2,1)S(1)} %get-tuple-element.15.refs_1_), channel_id=1, source_target_pairs={{12,4},{0,8},{20,12},{8,16},{28,20},{16,24},{13,5},{1,9},{21,13},{... | collective-permute-start | bytes 811016 | tf_op jit(solution)/shard_map/ppermute | solution.py:44
  27.3 0.1 collective-permute-start.6
  27.4 0.0 collective-permute-done.7.refs_3_
  27.4 0.5 collective-permute-start.9
  27.9 4.8 %collective-permute-done.11.refs_3_ = bf16[512,256]{1,0:T(8,128)(2,1)} collective-permute-done((bf16[512,256]{1,0:T(8,128)(2,1)}, bf16[512,256]{1,0:T(8,128)(2,1)}, u32[]{:S(2)}, u32[]{:S(2)}) %collective-permute-start.11) | collective-permute-done | bytes 262176 | tf_op jit(solution)/shard_map/ppermute | solution.py:44
  32.7 0.0 collective-permute-start.3
  32.8 2.5 %collective-permute-done.4.refs_2_ = bf16[3,64,1280]{2,1,0:T(8,128)(2,1)S(1)} collective-permute-done((bf16[3,64,1280]{2,1,0:T(8,128)(2,1)S(1)}, bf16[3,64,1280]{2,1,0:T(8,128)(2,1)S(1)}, u32[]{:S(2)}, u32[]{:S(2)}) %collective-permute-start.4) | collective-permute-done | bytes 491552 | tf_op jit(solution)/shard_map/ppermute | solution.py:38
  35.3 0.0 collective-permute-start.5
  35.3 0.0 collective-permute-done.8.refs_4_
  35.3 5.1 %collective-permute-start.12 = (bf16[512,256]{1,0:T(8,128)(2,1)}, bf16[512,256]{1,0:T(8,128)(2,1)}, u32[]{:S(2)}, u32[]{:S(2)}) collective-permute-start(bf16[512,256]{1,0:T(8,128)(2,1)} %get-tuple-element.17.refs_1_), channel_id=1, source_target_pairs={{12,4},{0,8},{20,12},{8,16},{28,20},{16,24},{13,5},{1,9},{21,13},{... | collective-permute-start | bytes 786440 | tf_op jit(solution)/shard_map/ppermute | solution.py:44
  40.3 0.0 collective-permute-start.10
  40.3 0.0 collective-permute-done.9.refs_5_
  40.3 0.5 collective-permute-start.13
  40.9 0.1 pad_add_fusion.corner_ref
  40.9 0.9 %copy-done = bf16[512,256]{1,0:T(8,128)(2,1)S(1)} copy-done((bf16[512,256]{1,0:T(8,128)(2,1)S(1)}, bf16[512,256]{1,0:T(8,128)(2,1)}, u32[]{:S(2)}) %copy-start) | copy-done | bytes 262168
  41.9 2.6 %attend.2 = (bf16[512,128]{1,0:T(8,128)(2,1)S(1)}, f32[16,256]{1,0:T(8,128)S(1)}) custom-call(bf16[512,256]{1,0:T(8,128)(2,1)S(1)} %copy-done, bf16[528,256]{1,0:T(8,128)(2,1)S(1)} %get-tuple-element.15.refs_1_, bf16[528,256]{1,0:T(8,128)(2,1)S(1)} %collective-permute-done.6.refs_2_, bf16[528,256]{1,0:T(8,128)(2,1)S(1)} %collective-permute-done.7.refs_3_, ...), custom_call_target="tpu_custom_call" | custom-call | flops 1342177280 | bytes 1310720 | tf_op jit(solution)/shard_map/attend/pallas_call | solution.py:190
  44.5 0.0 copy-start.1
  44.5 0.0 collective-permute-done.12.refs_4_
  44.6 3.4 %collective-permute-start.16 = (bf16[512,128]{1,0:T(8,128)(2,1)S(1)}, bf16[512,128]{1,0:T(8,128)(2,1)S(1)}, u32[]{:S(2)}, u32[]{:S(2)}) collective-permute-start(bf16[512,128]{1,0:T(8,128)(2,1)S(1)} %get-tuple-element.16.refs_0_), channel_id=1, source_target_pairs={{0,3},{1,2},{2,1},{3,0},{4,7},{5,6},{6,5},{7,4},{8,11},{9,10},{10,... | collective-permute-start | bytes 393224 | tf_op jit(solution)/shard_map/ppermute | solution.py:30
  48.0 1.6 %cut.2.own_ref = bf16[256,1280]{1,0:T(8,128)(2,1)S(1)} custom-call(s32[2]{0:T(128)S(1)} %pad_add_fusion.corner_ref, bf16[256,5120]{1,0:T(8,128)(2,1)} %source_ref.3), custom_call_target="tpu_custom_call" | custom-call | flops 1000000000 | bytes 1310720 | tf_op jit(solution)/shard_map/cut/pallas_call | solution.py:104
  49.6 0.0 collective-permute-done.10.refs_2_
  49.7 2.2 %collective-permute-start.15 = (bf16[512,128]{1,0:T(8,128)(2,1)S(1)}, bf16[512,128]{1,0:T(8,128)(2,1)S(1)}, u32[]{:S(2)}, u32[]{:S(2)}) collective-permute-start(bf16[512,128]{1,0:T(8,128)(2,1)S(1)} %get-tuple-element.16.refs_0_), channel_id=1, source_target_pairs={{0,2},{1,3},{2,0},{3,1},{4,6},{5,7},{6,4},{7,5},{8,10},{9,11},{10,... | collective-permute-start | bytes 393224 | tf_op jit(solution)/shard_map/ppermute | solution.py:30
  51.8 0.0 collective-permute-done.13.refs_5_
  51.8 0.4 collective-permute-start.14
  52.2 3.7 %attend.3.refs_1_ = bf16[512,128]{1,0:T(8,128)(2,1)S(1)} custom-call(bf16[512,256]{1,0:T(8,128)(2,1)S(1)} %copy-done.1, bf16[512,256]{1,0:T(8,128)(2,1)} %get-tuple-element.17.refs_1_, bf16[512,256]{1,0:T(8,128)(2,1)S(1)} %collective-permute-done.10.refs_2_, bf16[512,256]{1,0:T(8,128)(2,1)} %collective-permute-done.11.refs_3_, ...), custom_call_target="tpu_custom_call" | custom-call | flops 1342177280 | bytes 1310720 | tf_op jit(solution)/shard_map/attend/pallas_call | solution.py:190
  55.9 2.4 %collective-permute-start.19 = (bf16[512,128]{1,0:T(8,128)(2,1)S(1)}, bf16[512,128]{1,0:T(8,128)(2,1)S(1)}, u32[]{:S(2)}, u32[]{:S(2)}) collective-permute-start(bf16[512,128]{1,0:T(8,128)(2,1)S(1)} %attend.3.refs_1_), channel_id=1, source_target_pairs={{0,3},{1,2},{2,1},{3,0},{4,7},{5,6},{6,5},{7,4},{8,11},{9,10},{10,... | collective-permute-start | bytes 393224 | tf_op jit(solution)/shard_map/ppermute | solution.py:30
  58.3 0.0 collective-permute-done.16.refs_4_
  58.3 2.6 %collective-permute-start.18 = (bf16[512,128]{1,0:T(8,128)(2,1)S(1)}, bf16[512,128]{1,0:T(8,128)(2,1)S(1)}, u32[]{:S(2)}, u32[]{:S(2)}) collective-permute-start(bf16[512,128]{1,0:T(8,128)(2,1)S(1)} %attend.3.refs_1_), channel_id=1, source_target_pairs={{0,2},{1,3},{2,0},{3,1},{4,6},{5,7},{6,4},{7,5},{8,10},{9,11},{10,... | collective-permute-start | bytes 393224 | tf_op jit(solution)/shard_map/ppermute | solution.py:30
  60.9 0.2 assemble.1.w_ref
  61.1 5.6 %collective-permute-done.15.refs_3_ = bf16[512,128]{1,0:T(8,128)(2,1)S(1)} collective-permute-done((bf16[512,128]{1,0:T(8,128)(2,1)S(1)}, bf16[512,128]{1,0:T(8,128)(2,1)S(1)}, u32[]{:S(2)}, u32[]{:S(2)}) %collective-permute-start.15) | collective-permute-done | bytes 131104 | tf_op jit(solution)/shard_map/ppermute | solution.py:30
  66.7 0.0 collective-permute-done.14.refs_2_
  66.7 1.5 %project_first.1.p_ref = f32[512,1280]{1,0:T(8,128)S(1)} custom-call(bf16[4,256,1280]{2,1,0:T(8,128)(2,1)S(1)} %assemble.1.w_ref, bf16[512,128]{1,0:T(8,128)(2,1)S(1)} %get-tuple-element.16.refs_0_, bf16[512,128]{1,0:T(8,128)(2,1)S(1)} %attend.3.refs_1_, bf16[512,128]{1,0:T(8,128)(2,1)S(1)} %collective-permute-done.14.refs_2_, ...), custom_call_target="tpu_custom_call" | custom-call | flops 671088640 | bytes 2621440 | tf_op jit(solution)/shard_map/project_first/pallas_call | solution.py:262
  68.2 0.0 collective-permute-done.19.refs_2_
  68.2 4.2 %collective-permute-done.18.refs_1_ = bf16[512,128]{1,0:T(8,128)(2,1)S(1)} collective-permute-done((bf16[512,128]{1,0:T(8,128)(2,1)S(1)}, bf16[512,128]{1,0:T(8,128)(2,1)S(1)}, u32[]{:S(2)}, u32[]{:S(2)}) %collective-permute-start.18) | collective-permute-done | bytes 131104 | tf_op jit(solution)/shard_map/ppermute | solution.py:30
  72.5 0.0 collective-permute-done.17.refs_0_
  72.5 1.7 %project_last.1 = bf16[512,1280]{1,0:T(8,128)(2,1)} custom-call(bf16[4,256,1280]{2,1,0:T(8,128)(2,1)S(1)} %assemble.1.w_ref, f32[512,1280]{1,0:T(8,128)S(1)} %project_first.1.p_ref, bf16[512,128]{1,0:T(8,128)(2,1)S(1)} %collective-permute-done.17.refs_0_, bf16[512,128]{1,0:T(8,128)(2,1)S(1)} %collective-permute-done.18.refs_1_, ...), custom_call_target="tpu_custom_call" | custom-call | flops 671088640 | bytes 2621440 | tf_op jit(solution)/shard_map/project_last/pallas_call | solution.py:300
  (7 shorter events, 0.0 us)
Async XLA Ops:
  1.7 9.8 %collective-permute-start = (bf16[64,1280]{1,0:T(8,128)(2,1)S(1)}, bf16[64,1280]{1,0:T(8,128)(2,1)S(1)}, u32[]{:S(2)}, u32[]{:S(2)}) collective-permute-start(bf16[64,1280]{1,0:T(8,128)(2,1)S(1)} %get-tuple-element.12), channel_id=1, source_target_pairs={{0,1},{1,0},{2,3},{3,2},{4,5},{5,4},{6,7},{7,6},{8,9},{9,8},{10,11... | collective-permute-start | bytes 491528 | tf_op jit(solution)/shard_map/ppermute | solution.py:30
  4.9 15.0 %collective-permute-start.1 = (bf16[64,1280]{1,0:T(8,128)(2,1)S(1)}, bf16[64,1280]{1,0:T(8,128)(2,1)S(1)}, u32[]{:S(2)}, u32[]{:S(2)}) collective-permute-start(bf16[64,1280]{1,0:T(8,128)(2,1)S(1)} %get-tuple-element.13), channel_id=1, source_target_pairs={{0,2},{1,3},{2,0},{3,1},{4,6},{5,7},{6,4},{7,5},{8,10},{9,11},{10,... | collective-permute-start | bytes 491528 | tf_op jit(solution)/shard_map/ppermute | solution.py:30
  7.4 12.4 %collective-permute-start.2 = (bf16[64,1280]{1,0:T(8,128)(2,1)S(1)}, bf16[64,1280]{1,0:T(8,128)(2,1)S(1)}, u32[]{:S(2)}, u32[]{:S(2)}) collective-permute-start(bf16[64,1280]{1,0:T(8,128)(2,1)S(1)} %get-tuple-element.14), channel_id=1, source_target_pairs={{0,3},{1,2},{2,1},{3,0},{4,7},{5,6},{6,5},{7,4},{8,11},{9,10},{10,... | collective-permute-start | bytes 491528 | tf_op jit(solution)/shard_map/ppermute | solution.py:30
  9.3 18.1 %collective-permute-start.7 = (bf16[528,256]{1,0:T(8,128)(2,1)S(1)}, bf16[528,256]{1,0:T(8,128)(2,1)S(1)}, u32[]{:S(2)}, u32[]{:S(2)}) collective-permute-start(bf16[528,256]{1,0:T(8,128)(2,1)S(1)} %get-tuple-element.15.refs_1_), channel_id=1, source_target_pairs={{8,0},{16,8},{4,12},{24,16},{12,20},{20,28},{9,1},{17,9},{5,13},{2... | collective-permute-start | bytes 811016 | tf_op jit(solution)/shard_map/ppermute | solution.py:44
  19.9 15.4 %collective-permute-start.4 = (bf16[3,64,1280]{2,1,0:T(8,128)(2,1)S(1)}, bf16[3,64,1280]{2,1,0:T(8,128)(2,1)S(1)}, u32[]{:S(2)}, u32[]{:S(2)}) collective-permute-start(bf16[3,64,1280]{2,1,0:T(8,128)(2,1)S(1)} %stacked.1.refs_0_), channel_id=1, source_target_pairs={{0,16},{4,20},{8,24},{12,28},{16,0},{20,4},{24,8},{28,12},{1,17},{... | collective-permute-start | bytes 1474568 | tf_op jit(solution)/shard_map/ppermute | solution.py:38
  21.5 11.3 %collective-permute-start.11 = (bf16[512,256]{1,0:T(8,128)(2,1)}, bf16[512,256]{1,0:T(8,128)(2,1)}, u32[]{:S(2)}, u32[]{:S(2)}) collective-permute-start(bf16[512,256]{1,0:T(8,128)(2,1)} %get-tuple-element.17.refs_1_), channel_id=1, source_target_pairs={{8,0},{16,8},{4,12},{24,16},{12,20},{20,28},{9,1},{17,9},{5,13},{2... | collective-permute-start | bytes 786440 | tf_op jit(solution)/shard_map/ppermute | solution.py:44
  22.8 12.5 %collective-permute-start.8 = (bf16[528,256]{1,0:T(8,128)(2,1)S(1)}, bf16[528,256]{1,0:T(8,128)(2,1)S(1)}, u32[]{:S(2)}, u32[]{:S(2)}) collective-permute-start(bf16[528,256]{1,0:T(8,128)(2,1)S(1)} %get-tuple-element.15.refs_1_), channel_id=1, source_target_pairs={{12,4},{0,8},{20,12},{8,16},{28,20},{16,24},{13,5},{1,9},{21,13},{... | collective-permute-start | bytes 811016 | tf_op jit(solution)/shard_map/ppermute | solution.py:44
  27.3 13.0 %collective-permute-start.6 = (bf16[528,256]{1,0:T(8,128)(2,1)S(1)}, bf16[528,256]{1,0:T(8,128)(2,1)S(1)}, u32[]{:S(2)}, u32[]{:S(2)}) collective-permute-start(bf16[528,256]{1,0:T(8,128)(2,1)S(1)} %get-tuple-element.15.refs_1_), channel_id=1, source_target_pairs={{0,4},{4,0},{8,12},{12,8},{16,20},{20,16},{24,28},{28,24},{1,5},{5... | collective-permute-start | bytes 811016 | tf_op jit(solution)/shard_map/ppermute | solution.py:38
  27.4 12.9 %collective-permute-start.9 = (bf16[528,256]{1,0:T(8,128)(2,1)S(1)}, bf16[528,256]{1,0:T(8,128)(2,1)S(1)}, u32[]{:S(2)}, u32[]{:S(2)}) collective-permute-start(bf16[528,256]{1,0:T(8,128)(2,1)S(1)} %collective-permute-done.7.refs_3_), channel_id=1, source_target_pairs={{0,4},{4,0},{8,12},{12,8},{16,20},{20,16},{24,28},{28,24},{1,5},{5... | collective-permute-start | bytes 811016 | tf_op jit(solution)/shard_map/ppermute | solution.py:38
  32.7 23.2 %collective-permute-start.3 = (bf16[3,64,1280]{2,1,0:T(8,128)(2,1)S(1)}, bf16[3,64,1280]{2,1,0:T(8,128)(2,1)S(1)}, u32[]{:S(2)}, u32[]{:S(2)}) collective-permute-start(bf16[3,64,1280]{2,1,0:T(8,128)(2,1)S(1)} %stacked.1.refs_0_), channel_id=1, source_target_pairs={{0,4},{4,0},{8,12},{12,8},{16,20},{20,16},{24,28},{28,24},{1,5},{5... | collective-permute-start | bytes 1474568 | tf_op jit(solution)/shard_map/ppermute | solution.py:38
  35.3 25.7 %collective-permute-start.5 = (bf16[3,64,1280]{2,1,0:T(8,128)(2,1)S(1)}, bf16[3,64,1280]{2,1,0:T(8,128)(2,1)S(1)}, u32[]{:S(2)}, u32[]{:S(2)}) collective-permute-start(bf16[3,64,1280]{2,1,0:T(8,128)(2,1)S(1)} %collective-permute-done.4.refs_2_), channel_id=1, source_target_pairs={{0,4},{4,0},{8,12},{12,8},{16,20},{20,16},{24,28},{28,24},{1,5},{5... | collective-permute-start | bytes 1474568 | tf_op jit(solution)/shard_map/ppermute | solution.py:38
  35.3 9.3 %collective-permute-start.12 = (bf16[512,256]{1,0:T(8,128)(2,1)}, bf16[512,256]{1,0:T(8,128)(2,1)}, u32[]{:S(2)}, u32[]{:S(2)}) collective-permute-start(bf16[512,256]{1,0:T(8,128)(2,1)} %get-tuple-element.17.refs_1_), channel_id=1, source_target_pairs={{12,4},{0,8},{20,12},{8,16},{28,20},{16,24},{13,5},{1,9},{21,13},{... | collective-permute-start | bytes 786440 | tf_op jit(solution)/shard_map/ppermute | solution.py:44
  40.3 9.3 %collective-permute-start.10 = (bf16[512,256]{1,0:T(8,128)(2,1)}, bf16[512,256]{1,0:T(8,128)(2,1)S(1)}, u32[]{:S(2)}, u32[]{:S(2)}) collective-permute-start(bf16[512,256]{1,0:T(8,128)(2,1)} %get-tuple-element.17.refs_1_), channel_id=1, source_target_pairs={{0,4},{4,0},{8,12},{12,8},{16,20},{20,16},{24,28},{28,24},{1,5},{5... | collective-permute-start | bytes 786440 | tf_op jit(solution)/shard_map/ppermute | solution.py:38
  40.3 11.5 %collective-permute-start.13 = (bf16[512,256]{1,0:T(8,128)(2,1)}, bf16[512,256]{1,0:T(8,128)(2,1)S(1)}, u32[]{:S(2)}, u32[]{:S(2)}) collective-permute-start(bf16[512,256]{1,0:T(8,128)(2,1)} %collective-permute-done.11.refs_3_), channel_id=1, source_target_pairs={{0,4},{4,0},{8,12},{12,8},{16,20},{20,16},{24,28},{28,24},{1,5},{5... | collective-permute-start | bytes 786440 | tf_op jit(solution)/shard_map/ppermute | solution.py:38
  40.9 0.9 %copy-start = (bf16[512,256]{1,0:T(8,128)(2,1)S(1)}, bf16[512,256]{1,0:T(8,128)(2,1)}, u32[]{:S(2)}) copy-start(bf16[512,256]{1,0:T(8,128)(2,1)} %refs_0_.3) | copy-start | bytes 786436
  44.5 7.7 %copy-start.1 = (bf16[512,256]{1,0:T(8,128)(2,1)S(1)}, bf16[512,256]{1,0:T(8,128)(2,1)}, u32[]{:S(2)}) copy-start(bf16[512,256]{1,0:T(8,128)(2,1)} %refs_0_.3) | copy-start | bytes 786436
  44.6 13.7 %collective-permute-start.16 = (bf16[512,128]{1,0:T(8,128)(2,1)S(1)}, bf16[512,128]{1,0:T(8,128)(2,1)S(1)}, u32[]{:S(2)}, u32[]{:S(2)}) collective-permute-start(bf16[512,128]{1,0:T(8,128)(2,1)S(1)} %get-tuple-element.16.refs_0_), channel_id=1, source_target_pairs={{0,3},{1,2},{2,1},{3,0},{4,7},{5,6},{6,5},{7,4},{8,11},{9,10},{10,... | collective-permute-start | bytes 393224 | tf_op jit(solution)/shard_map/ppermute | solution.py:30
  49.7 17.0 %collective-permute-start.15 = (bf16[512,128]{1,0:T(8,128)(2,1)S(1)}, bf16[512,128]{1,0:T(8,128)(2,1)S(1)}, u32[]{:S(2)}, u32[]{:S(2)}) collective-permute-start(bf16[512,128]{1,0:T(8,128)(2,1)S(1)} %get-tuple-element.16.refs_0_), channel_id=1, source_target_pairs={{0,2},{1,3},{2,0},{3,1},{4,6},{5,7},{6,4},{7,5},{8,10},{9,11},{10,... | collective-permute-start | bytes 393224 | tf_op jit(solution)/shard_map/ppermute | solution.py:30
  51.8 14.8 %collective-permute-start.14 = (bf16[512,128]{1,0:T(8,128)(2,1)S(1)}, bf16[512,128]{1,0:T(8,128)(2,1)S(1)}, u32[]{:S(2)}, u32[]{:S(2)}) collective-permute-start(bf16[512,128]{1,0:T(8,128)(2,1)S(1)} %get-tuple-element.16.refs_0_), channel_id=1, source_target_pairs={{0,1},{1,0},{2,3},{3,2},{4,5},{5,4},{6,7},{7,6},{8,9},{9,8},{10,11... | collective-permute-start | bytes 393224 | tf_op jit(solution)/shard_map/ppermute | solution.py:30
  55.9 12.3 %collective-permute-start.19 = (bf16[512,128]{1,0:T(8,128)(2,1)S(1)}, bf16[512,128]{1,0:T(8,128)(2,1)S(1)}, u32[]{:S(2)}, u32[]{:S(2)}) collective-permute-start(bf16[512,128]{1,0:T(8,128)(2,1)S(1)} %attend.3.refs_1_), channel_id=1, source_target_pairs={{0,3},{1,2},{2,1},{3,0},{4,7},{5,6},{6,5},{7,4},{8,11},{9,10},{10,... | collective-permute-start | bytes 393224 | tf_op jit(solution)/shard_map/ppermute | solution.py:30
  58.3 14.2 %collective-permute-start.18 = (bf16[512,128]{1,0:T(8,128)(2,1)S(1)}, bf16[512,128]{1,0:T(8,128)(2,1)S(1)}, u32[]{:S(2)}, u32[]{:S(2)}) collective-permute-start(bf16[512,128]{1,0:T(8,128)(2,1)S(1)} %attend.3.refs_1_), channel_id=1, source_target_pairs={{0,2},{1,3},{2,0},{3,1},{4,6},{5,7},{6,4},{7,5},{8,10},{9,11},{10,... | collective-permute-start | bytes 393224 | tf_op jit(solution)/shard_map/ppermute | solution.py:30
  60.9 11.5 %collective-permute-start.17 = (bf16[512,128]{1,0:T(8,128)(2,1)S(1)}, bf16[512,128]{1,0:T(8,128)(2,1)S(1)}, u32[]{:S(2)}, u32[]{:S(2)}) collective-permute-start(bf16[512,128]{1,0:T(8,128)(2,1)S(1)} %attend.3.refs_1_), channel_id=1, source_target_pairs={{0,1},{1,0},{2,3},{3,2},{4,5},{5,4},{6,7},{7,6},{8,9},{9,8},{10,11... | collective-permute-start | bytes 393224 | tf_op jit(solution)/shard_map/ppermute | solution.py:30

commit v4 on v3

--- a/solution.py
+++ b/solution.py
@@ -273,47 +273,43 @@
     )(weight, *flat)
 
 
-def project_last(weight, partial, others):
-    groups, depth, columns = weight.shape
-    rows, head = others[0][0].shape
-    flat = [array for arrays in others for array in arrays]
-    span = (groups - 1) * (depth - head)
+def project_more(weight, partial, parts, last):
+    _, _, columns = weight.shape
+    rows, head = parts[0][0].shape
     cuts = tiles(columns)
 
     def body(w_ref, p_ref, *refs):
-        ins, (out_ref, left_ref, right_ref, done_ref, sems) = refs[:len(flat)], refs[len(flat):]
-        placed(left_ref, ins, others)
-        for g in range(1, groups):
-            place = (g - 1) * (depth - head)
-            right_ref[place:place + depth - head, :] = w_ref[g, head:, :]
+        ins, (out_ref, *rest) = refs[:len(parts)], refs[len(parts):]
         copies = []
         for number, tile in enumerate(cuts):
-            out = p_ref[:, tile] + jnp.dot(
-                left_ref[...], right_ref[:, tile], preferred_element_type=jnp.float32
-            )
+            out = p_ref[:, tile]
+            for ref, (_, group, row) in zip(ins, parts):
+                out += jnp.dot(
+                    ref[...], w_ref[group, row:row + head, tile], preferred_element_type=jnp.float32
+                )
+            if not last:
+                out_ref[:, tile] = out
+                continue
+            done_ref, sems = rest
             done_ref[:, tile] = out.astype(jnp.bfloat16)
             copies.append(pltpu.make_async_copy(done_ref.at[:, tile], out_ref.at[:, tile], sems.at[number]))
             copies[-1].start()
         for copy in copies:
             copy.wait()
 
-    return pl.pallas_call(
-        body,
-        name="project_last",
-        in_specs=[IN_VMEM] * (2 + len(flat)),
-        out_specs=pl.BlockSpec(memory_space=pltpu.HBM),
-        out_shape=jax.ShapeDtypeStruct((rows, columns), jnp.bfloat16),
-        scratch_shapes=[
-            pltpu.VMEM((rows, span), jnp.bfloat16),
-            pltpu.VMEM((span, columns), jnp.bfloat16),
-            pltpu.VMEM((rows, columns), jnp.bfloat16),
-            pltpu.SemaphoreType.DMA((len(cuts),)),
-        ],
-        compiler_params=pltpu.CompilerParams(vmem_limit_bytes=2 * KERNEL_VMEM),
-        cost_estimate=pl.CostEstimate(
-            flops=rows * groups * depth * columns, bytes_accessed=4 * columns * rows, transcendentals=0
-        ),
-    )(weight, partial, *flat)
+    scratch = [pltpu.VMEM((rows, columns), jnp.bfloat16), pltpu.SemaphoreType.DMA((len(cuts),))]
+    return pl.pallas_call(
+        body,
+        name="project_last" if last else "project_more",
+        in_specs=[IN_VMEM] * (2 + len(parts)),
+        out_specs=IN_HBM if last else IN_VMEM,
+        out_shape=jax.ShapeDtypeStruct((rows, columns), jnp.bfloat16 if last else jnp.float32),
+        scratch_shapes=scratch if last else [],
+        compiler_params=pltpu.CompilerParams(vmem_limit_bytes=KERNEL_VMEM),
+        cost_estimate=pl.CostEstimate(
+            flops=2 * rows * len(parts) * head * columns, bytes_accessed=4 * columns * rows, transcendentals=0
+        ),
+    )(weight, partial, *[part[0] for part in parts])
 
 
 def shards(queries, keys, values, segment_ids, out_weight):
@@ -374,8 +370,19 @@
         own_weight = lax.dynamic_slice(out_weight, (0, me * columns), (out_weight.shape[0], columns))
     weight = assemble(mine.astype(jnp.int32)[None], own_weight, [first, third, second, fourth])
     partial = project_first(weight, own, others[0])
-    rest = [line[distance] for distance in range(groups - 1) for line in others[1:]]
-    return project_last(weight, partial, rest)
+    head = queries.shape[1] // HEAD_DEV
+    parts = [
+        (line[distance - 1][0], distance, index * head)
+        for distance in turns(groups) for index, line in enumerate(others) if index
+    ]
+    final = HEAD_DEV - 1
+    if len(parts) > final:
+        partial = project_more(weight, partial, parts[:-final], False)
+    return project_more(weight, partial, parts[-final:], True)
+
+
+def turns(groups):
+    return [2, 1, 3] if groups == 4 else list(range(1, groups))
 
 
 def solution(mesh):

time: 74.5 us -> 75 us (level)
    pallas_call x1 -> x2, Pallas kernels: 1.69 us -> 2.19 us  [project_more(): pl.pallas_call(body, name='project_last' if last else 'project_more', in_...]
  transfers between devices with their start and end apart: 20 -> 20, of which waited for: 6 -> 7; matrix products, arithmetic and copies ran while one was open for 0% -> 0% of each run, Pallas kernels for 16% -> 17%
where the time goes in v4:
time: 75 us; the launch traced here: 74.7 us
  starting transfers between devices  31.5 us (42%)
  waiting for transfers between devices  26.5 us (35%)
  Pallas kernels  15.4 us (21%)
  local copies, waits for them, and re-layouts  1.04 us (1%)
    ppermute x9, waiting for transfers between devices, to_partner(): lax.ppermute(block, axis, [(i, partner(i, distance, count)) for i in rang...  19.1 us
    ppermute x9, starting transfers between devices, to_partner(): lax.ppermute(block, axis, [(i, partner(i, distance, count)) for i in rang...  16.7 us
    ppermute x4, starting transfers between devices, from_far(): lax.ppermute(block, axis, [(s, d) for s, d in route if 0 <= s < count])  12.2 us
    pallas_call x2, Pallas kernels, attend(): pl.pallas_call(body, name='attend', in_specs=[IN_VMEM] * (1 + count + (no...  6.38 us
    ppermute x4, waiting for transfers between devices, from_far(): lax.ppermute(block, axis, [(s, d) for s, d in route if 0 <= s < count])  4.84 us
    pallas_call x2, Pallas kernels, cut(): pl.pallas_call(body, name='cut', in_specs=[pl.BlockSpec(memory_space=pltp...  3.29 us
    ppermute x7, starting transfers between devices, exchanged(): lax.ppermute(block, axis, [(i, i ^ flip) for i in range(lax.axis_size(axi...  2.66 us
    ppermute x7, waiting for transfers between devices, exchanged(): lax.ppermute(block, axis, [(i, i ^ flip) for i in range(lax.axis_size(axi...  2.53 us
  transfers between devices with their start and end apart: 20, of which 7 were waited for; matrix products, arithmetic and copies ran while one was open for 0% of the time, Pallas kernels for 17%

profile of v4, /device:TPU:0, one launch (start us, length us, event | category | flops | bytes accessed | tf_op | source)
XLA Modules:
  0.0 74.7 jit_solution(14653481506608354370)
XLA Ops:
  0.0 0.1 stack.29.corner_ref
  0.1 1.6 %cut.3 = (bf16[64,1280]{1,0:T(8,128)(2,1)S(1)}, bf16[64,1280]{1,0:T(8,128)(2,1)S(1)}, bf16[64,1280]{1,0:T(8,128)(2,1)S(1)}) custom-call(s32[6]{0:T(128)S(1)} %stack.29.corner_ref, bf16[256,5120]{1,0:T(8,128)(2,1)} %source_ref.3), custom_call_target="tpu_custom_call" | custom-call | flops 1000000000 | bytes 983040 | tf_op jit(solution)/shard_map/cut/pallas_call | solution.py:104
  1.7 3.1 %collective-permute-start = (bf16[64,1280]{1,0:T(8,128)(2,1)S(1)}, bf16[64,1280]{1,0:T(8,128)(2,1)S(1)}, u32[]{:S(2)}, u32[]{:S(2)}) collective-permute-start(bf16[64,1280]{1,0:T(8,128)(2,1)S(1)} %get-tuple-element.12), channel_id=1, source_target_pairs={{0,1},{1,0},{2,3},{3,2},{4,5},{5,4},{6,7},{7,6},{8,9},{9,8},{10,11... | collective-permute-start | bytes 491528 | tf_op jit(solution)/shard_map/ppermute | solution.py:30
  4.9 2.6 %collective-permute-start.1 = (bf16[64,1280]{1,0:T(8,128)(2,1)S(1)}, bf16[64,1280]{1,0:T(8,128)(2,1)S(1)}, u32[]{:S(2)}, u32[]{:S(2)}) collective-permute-start(bf16[64,1280]{1,0:T(8,128)(2,1)S(1)} %get-tuple-element.13), channel_id=1, source_target_pairs={{0,2},{1,3},{2,0},{3,1},{4,6},{5,7},{6,4},{7,5},{8,10},{9,11},{10,... | collective-permute-start | bytes 491528 | tf_op jit(solution)/shard_map/ppermute | solution.py:30
  7.4 0.0 collective-permute-start.2
  7.4 1.9 %pack.1 = (bf16[528,256]{1,0:T(8,128)(2,1)S(1)}, bf16[512,256]{1,0:T(8,128)(2,1)}) custom-call(bf16[512,256]{1,0:T(8,128)(2,1)} %k_ref.1, bf16[512,256]{1,0:T(8,128)(2,1)} %v_ref.1, s32[1,512]{1,0:T(1,128)} %bitcast.7), custom_call_target="tpu_custom_call" | custom-call | flops 1000000000 | bytes 1048576 | tf_op jit(solution)/shard_map/pack/pallas_call | solution.py:74
  9.3 1.3 %collective-permute-start.7 = (bf16[528,256]{1,0:T(8,128)(2,1)S(1)}, bf16[528,256]{1,0:T(8,128)(2,1)S(1)}, u32[]{:S(2)}, u32[]{:S(2)}) collective-permute-start(bf16[528,256]{1,0:T(8,128)(2,1)S(1)} %get-tuple-element.15.refs_1_), channel_id=1, source_target_pairs={{8,0},{16,8},{4,12},{24,16},{12,20},{20,28},{9,1},{17,9},{5,13},{2... | collective-permute-start | bytes 811016 | tf_op jit(solution)/shard_map/ppermute | solution.py:44
  10.6 1.0 %collective-permute-done.refs_0_ = bf16[64,1280]{1,0:T(8,128)(2,1)S(1)} collective-permute-done((bf16[64,1280]{1,0:T(8,128)(2,1)S(1)}, bf16[64,1280]{1,0:T(8,128)(2,1)S(1)}, u32[]{:S(2)}, u32[]{:S(2)}) %collective-permute-start) | collective-permute-done | bytes 163872 | tf_op jit(solution)/shard_map/ppermute | solution.py:30
  11.6 8.3 %collective-permute-done.1.refs_1_ = bf16[64,1280]{1,0:T(8,128)(2,1)S(1)} collective-permute-done((bf16[64,1280]{1,0:T(8,128)(2,1)S(1)}, bf16[64,1280]{1,0:T(8,128)(2,1)S(1)}, u32[]{:S(2)}, u32[]{:S(2)}) %collective-permute-start.1) | collective-permute-done | bytes 163872 | tf_op jit(solution)/shard_map/ppermute | solution.py:30
  19.9 0.0 collective-permute-done.2.refs_2_
  19.9 1.6 %collective-permute-start.4 = (bf16[3,64,1280]{2,1,0:T(8,128)(2,1)S(1)}, bf16[3,64,1280]{2,1,0:T(8,128)(2,1)S(1)}, u32[]{:S(2)}, u32[]{:S(2)}) collective-permute-start(bf16[3,64,1280]{2,1,0:T(8,128)(2,1)S(1)} %stacked.1.refs_0_), channel_id=1, source_target_pairs={{0,16},{4,20},{8,24},{12,28},{16,0},{20,4},{24,8},{28,12},{1,17},{... | collective-permute-start | bytes 1474568 | tf_op jit(solution)/shard_map/ppermute | solution.py:38
  21.5 1.3 %collective-permute-start.11 = (bf16[512,256]{1,0:T(8,128)(2,1)}, bf16[512,256]{1,0:T(8,128)(2,1)}, u32[]{:S(2)}, u32[]{:S(2)}) collective-permute-start(bf16[512,256]{1,0:T(8,128)(2,1)} %get-tuple-element.17.refs_1_), channel_id=1, source_target_pairs={{8,0},{16,8},{4,12},{24,16},{12,20},{20,28},{9,1},{17,9},{5,13},{2... | collective-permute-start | bytes 786440 | tf_op jit(solution)/shard_map/ppermute | solution.py:44
  22.8 4.6 %collective-permute-start.8 = (bf16[528,256]{1,0:T(8,128)(2,1)S(1)}, bf16[528,256]{1,0:T(8,128)(2,1)S(1)}, u32[]{:S(2)}, u32[]{:S(2)}) collective-permute-start(bf16[528,256]{1,0:T(8,128)(2,1)S(1)} %get-tuple-element.15.refs_1_), channel_id=1, source_target_pairs={{12,4},{0,8},{20,12},{8,16},{28,20},{16,24},{13,5},{1,9},{21,13},{... | collective-permute-start | bytes 811016 | tf_op jit(solution)/shard_map/ppermute | solution.py:44
  27.3 0.1 collective-permute-start.6
  27.4 0.0 collective-permute-done.7.refs_3_
  27.4 0.5 collective-permute-start.9
  27.9 4.8 %collective-permute-done.11.refs_3_ = bf16[512,256]{1,0:T(8,128)(2,1)} collective-permute-done((bf16[512,256]{1,0:T(8,128)(2,1)}, bf16[512,256]{1,0:T(8,128)(2,1)}, u32[]{:S(2)}, u32[]{:S(2)}) %collective-permute-start.11) | collective-permute-done | bytes 262176 | tf_op jit(solution)/shard_map/ppermute | solution.py:44
  32.7 0.0 collective-permute-start.3
  32.8 2.5 %collective-permute-done.4.refs_2_ = bf16[3,64,1280]{2,1,0:T(8,128)(2,1)S(1)} collective-permute-done((bf16[3,64,1280]{2,1,0:T(8,128)(2,1)S(1)}, bf16[3,64,1280]{2,1,0:T(8,128)(2,1)S(1)}, u32[]{:S(2)}, u32[]{:S(2)}) %collective-permute-start.4) | collective-permute-done | bytes 491552 | tf_op jit(solution)/shard_map/ppermute | solution.py:38
  35.3 5.1 %collective-permute-start.12 = (bf16[512,256]{1,0:T(8,128)(2,1)}, bf16[512,256]{1,0:T(8,128)(2,1)}, u32[]{:S(2)}, u32[]{:S(2)}) collective-permute-start(bf16[512,256]{1,0:T(8,128)(2,1)} %get-tuple-element.17.refs_1_), channel_id=1, source_target_pairs={{12,4},{0,8},{20,12},{8,16},{28,20},{16,24},{13,5},{1,9},{21,13},{... | collective-permute-start | bytes 786440 | tf_op jit(solution)/shard_map/ppermute | solution.py:44
  40.3 0.0 collective-permute-start.10
  40.3 0.0 collective-permute-done.9.refs_5_
  40.3 0.5 collective-permute-start.13
  40.9 0.1 pad_add_fusion.corner_ref
  40.9 0.9 %copy-done = bf16[512,256]{1,0:T(8,128)(2,1)S(1)} copy-done((bf16[512,256]{1,0:T(8,128)(2,1)S(1)}, bf16[512,256]{1,0:T(8,128)(2,1)}, u32[]{:S(2)}) %copy-start) | copy-done | bytes 262168
  41.9 2.6 %attend.2 = (bf16[512,128]{1,0:T(8,128)(2,1)S(1)}, f32[16,256]{1,0:T(8,128)S(1)}) custom-call(bf16[512,256]{1,0:T(8,128)(2,1)S(1)} %copy-done, bf16[528,256]{1,0:T(8,128)(2,1)S(1)} %get-tuple-element.15.refs_1_, bf16[528,256]{1,0:T(8,128)(2,1)S(1)} %collective-permute-done.6.refs_2_, bf16[528,256]{1,0:T(8,128)(2,1)S(1)} %collective-permute-done.7.refs_3_, ...), custom_call_target="tpu_custom_call" | custom-call | flops 1342177280 | bytes 1310720 | tf_op jit(solution)/shard_map/attend/pallas_call | solution.py:190
  44.5 0.0 copy-start.1
  44.5 0.0 collective-permute-done.12.refs_4_
  44.6 3.4 %collective-permute-start.16 = (bf16[512,128]{1,0:T(8,128)(2,1)S(1)}, bf16[512,128]{1,0:T(8,128)(2,1)S(1)}, u32[]{:S(2)}, u32[]{:S(2)}) collective-permute-start(bf16[512,128]{1,0:T(8,128)(2,1)S(1)} %get-tuple-element.16.refs_0_), channel_id=1, source_target_pairs={{0,3},{1,2},{2,1},{3,0},{4,7},{5,6},{6,5},{7,4},{8,11},{9,10},{10,... | collective-permute-start | bytes 393224 | tf_op jit(solution)/shard_map/ppermute | solution.py:30
  48.0 1.6 %cut.2.own_ref = bf16[256,1280]{1,0:T(8,128)(2,1)S(1)} custom-call(s32[2]{0:T(128)S(1)} %pad_add_fusion.corner_ref, bf16[256,5120]{1,0:T(8,128)(2,1)} %source_ref.3), custom_call_target="tpu_custom_call" | custom-call | flops 1000000000 | bytes 1310720 | tf_op jit(solution)/shard_map/cut/pallas_call | solution.py:104
  49.6 0.0 collective-permute-done.10.refs_2_
  49.7 2.2 %collective-permute-start.15 = (bf16[512,128]{1,0:T(8,128)(2,1)S(1)}, bf16[512,128]{1,0:T(8,128)(2,1)S(1)}, u32[]{:S(2)}, u32[]{:S(2)}) collective-permute-start(bf16[512,128]{1,0:T(8,128)(2,1)S(1)} %get-tuple-element.16.refs_0_), channel_id=1, source_target_pairs={{0,2},{1,3},{2,0},{3,1},{4,6},{5,7},{6,4},{7,5},{8,10},{9,11},{10,... | collective-permute-start | bytes 393224 | tf_op jit(solution)/shard_map/ppermute | solution.py:30
  51.8 0.0 collective-permute-done.13.refs_5_
  51.8 0.4 collective-permute-start.14
  52.2 3.7 %attend.3.refs_1_ = bf16[512,128]{1,0:T(8,128)(2,1)S(1)} custom-call(bf16[512,256]{1,0:T(8,128)(2,1)S(1)} %copy-done.1, bf16[512,256]{1,0:T(8,128)(2,1)} %get-tuple-element.17.refs_1_, bf16[512,256]{1,0:T(8,128)(2,1)S(1)} %collective-permute-done.10.refs_2_, bf16[512,256]{1,0:T(8,128)(2,1)} %collective-permute-done.11.refs_3_, ...), custom_call_target="tpu_custom_call" | custom-call | flops 1342177280 | bytes 1310720 | tf_op jit(solution)/shard_map/attend/pallas_call | solution.py:190
  55.9 2.4 %collective-permute-start.19 = (bf16[512,128]{1,0:T(8,128)(2,1)S(1)}, bf16[512,128]{1,0:T(8,128)(2,1)S(1)}, u32[]{:S(2)}, u32[]{:S(2)}) collective-permute-start(bf16[512,128]{1,0:T(8,128)(2,1)S(1)} %attend.3.refs_1_), channel_id=1, source_target_pairs={{0,3},{1,2},{2,1},{3,0},{4,7},{5,6},{6,5},{7,4},{8,11},{9,10},{10,... | collective-permute-start | bytes 393224 | tf_op jit(solution)/shard_map/ppermute | solution.py:30
  58.3 0.0 collective-permute-done.16.refs_4_
  58.3 1.1 %collective-permute-start.18 = (bf16[512,128]{1,0:T(8,128)(2,1)S(1)}, bf16[512,128]{1,0:T(8,128)(2,1)S(1)}, u32[]{:S(2)}, u32[]{:S(2)}) collective-permute-start(bf16[512,128]{1,0:T(8,128)(2,1)S(1)} %attend.3.refs_1_), channel_id=1, source_target_pairs={{0,1},{1,0},{2,3},{3,2},{4,5},{5,4},{6,7},{7,6},{8,9},{9,8},{10,11... | collective-permute-start | bytes 393224 | tf_op jit(solution)/shard_map/ppermute | solution.py:30
  59.4 0.0 collective-permute-done.5.refs_3_
  59.4 1.5 %collective-permute-start.17 = (bf16[512,128]{1,0:T(8,128)(2,1)S(1)}, bf16[512,128]{1,0:T(8,128)(2,1)S(1)}, u32[]{:S(2)}, u32[]{:S(2)}) collective-permute-start(bf16[512,128]{1,0:T(8,128)(2,1)S(1)} %attend.3.refs_1_), channel_id=1, source_target_pairs={{0,2},{1,3},{2,0},{3,1},{4,6},{5,7},{6,4},{7,5},{8,10},{9,11},{10,... | collective-permute-start | bytes 393224 | tf_op jit(solution)/shard_map/ppermute | solution.py:30
  60.9 0.2 assemble.1.w_ref
  61.1 2.8 %collective-permute-done.15.refs_3_ = bf16[512,128]{1,0:T(8,128)(2,1)S(1)} collective-permute-done((bf16[512,128]{1,0:T(8,128)(2,1)S(1)}, bf16[512,128]{1,0:T(8,128)(2,1)S(1)}, u32[]{:S(2)}, u32[]{:S(2)}) %collective-permute-start.15) | collective-permute-done | bytes 131104 | tf_op jit(solution)/shard_map/ppermute | solution.py:30
  63.9 0.0 collective-permute-done.14.refs_2_
  63.9 1.5 %project_first.1.p_ref = f32[512,1280]{1,0:T(8,128)S(1)} custom-call(bf16[4,256,1280]{2,1,0:T(8,128)(2,1)S(1)} %assemble.1.w_ref, bf16[512,128]{1,0:T(8,128)(2,1)S(1)} %get-tuple-element.16.refs_0_, bf16[512,128]{1,0:T(8,128)(2,1)S(1)} %attend.3.refs_1_, bf16[512,128]{1,0:T(8,128)(2,1)S(1)} %collective-permute-done.14.refs_2_, ...), custom_call_target="tpu_custom_call" | custom-call | flops 671088640 | bytes 2621440 | tf_op jit(solution)/shard_map/project_first/pallas_call | solution.py:262
  65.5 1.4 %collective-permute-done.18.refs_1_ = bf16[512,128]{1,0:T(8,128)(2,1)S(1)} collective-permute-done((bf16[512,128]{1,0:T(8,128)(2,1)S(1)}, bf16[512,128]{1,0:T(8,128)(2,1)S(1)}, u32[]{:S(2)}, u32[]{:S(2)}) %collective-permute-start.18) | collective-permute-done | bytes 131104 | tf_op jit(solution)/shard_map/ppermute | solution.py:30
  66.8 5.7 %collective-permute-done.17.refs_0_ = bf16[512,128]{1,0:T(8,128)(2,1)S(1)} collective-permute-done((bf16[512,128]{1,0:T(8,128)(2,1)S(1)}, bf16[512,128]{1,0:T(8,128)(2,1)S(1)}, u32[]{:S(2)}, u32[]{:S(2)}) %collective-permute-start.17) | collective-permute-done | bytes 131104 | tf_op jit(solution)/shard_map/ppermute | solution.py:30
  72.5 0.8 %project_more.1.p_ref = f32[512,1280]{1,0:T(8,128)S(1)} custom-call(bf16[4,256,1280]{2,1,0:T(8,128)(2,1)S(1)} %assemble.1.w_ref, f32[512,1280]{1,0:T(8,128)S(1)} %project_first.1.p_ref, bf16[512,128]{1,0:T(8,128)(2,1)S(1)} %collective-permute-done.17.refs_0_, bf16[512,128]{1,0:T(8,128)(2,1)S(1)} %collective-permute-done.18.refs_1_), custom_call_target="tpu_custom_call" | custom-call | flops 335544320 | bytes 2621440 | tf_op jit(solution)/shard_map/project_more/pallas_call | solution.py:301
  73.3 1.4 %project_last.1 = bf16[512,1280]{1,0:T(8,128)(2,1)} custom-call(bf16[4,256,1280]{2,1,0:T(8,128)(2,1)S(1)} %assemble.1.w_ref, f32[512,1280]{1,0:T(8,128)S(1)} %project_more.1.p_ref, bf16[512,128]{1,0:T(8,128)(2,1)S(1)} %collective-permute-done.19.refs_0_), custom_call_target="tpu_custom_call" | custom-call | flops 167772160 | bytes 2621440 | tf_op jit(solution)/shard_map/project_last/pallas_call | solution.py:301
  (8 shorter events, 0.0 us)
Async XLA Ops:
  1.7 9.8 %collective-permute-start = (bf16[64,1280]{1,0:T(8,128)(2,1)S(1)}, bf16[64,1280]{1,0:T(8,128)(2,1)S(1)}, u32[]{:S(2)}, u32[]{:S(2)}) collective-permute-start(bf16[64,1280]{1,0:T(8,128)(2,1)S(1)} %get-tuple-element.12), channel_id=1, source_target_pairs={{0,1},{1,0},{2,3},{3,2},{4,5},{5,4},{6,7},{7,6},{8,9},{9,8},{10,11... | collective-permute-start | bytes 491528 | tf_op jit(solution)/shard_map/ppermute | solution.py:30
  4.9 15.0 %collective-permute-start.1 = (bf16[64,1280]{1,0:T(8,128)(2,1)S(1)}, bf16[64,1280]{1,0:T(8,128)(2,1)S(1)}, u32[]{:S(2)}, u32[]{:S(2)}) collective-permute-start(bf16[64,1280]{1,0:T(8,128)(2,1)S(1)} %get-tuple-element.13), channel_id=1, source_target_pairs={{0,2},{1,3},{2,0},{3,1},{4,6},{5,7},{6,4},{7,5},{8,10},{9,11},{10,... | collective-permute-start | bytes 491528 | tf_op jit(solution)/shard_map/ppermute | solution.py:30
  7.4 12.4 %collective-permute-start.2 = (bf16[64,1280]{1,0:T(8,128)(2,1)S(1)}, bf16[64,1280]{1,0:T(8,128)(2,1)S(1)}, u32[]{:S(2)}, u32[]{:S(2)}) collective-permute-start(bf16[64,1280]{1,0:T(8,128)(2,1)S(1)} %get-tuple-element.14), channel_id=1, source_target_pairs={{0,3},{1,2},{2,1},{3,0},{4,7},{5,6},{6,5},{7,4},{8,11},{9,10},{10,... | collective-permute-start | bytes 491528 | tf_op jit(solution)/shard_map/ppermute | solution.py:30
  9.3 18.1 %collective-permute-start.7 = (bf16[528,256]{1,0:T(8,128)(2,1)S(1)}, bf16[528,256]{1,0:T(8,128)(2,1)S(1)}, u32[]{:S(2)}, u32[]{:S(2)}) collective-permute-start(bf16[528,256]{1,0:T(8,128)(2,1)S(1)} %get-tuple-element.15.refs_1_), channel_id=1, source_target_pairs={{8,0},{16,8},{4,12},{24,16},{12,20},{20,28},{9,1},{17,9},{5,13},{2... | collective-permute-start | bytes 811016 | tf_op jit(solution)/shard_map/ppermute | solution.py:44
  19.9 15.4 %collective-permute-start.4 = (bf16[3,64,1280]{2,1,0:T(8,128)(2,1)S(1)}, bf16[3,64,1280]{2,1,0:T(8,128)(2,1)S(1)}, u32[]{:S(2)}, u32[]{:S(2)}) collective-permute-start(bf16[3,64,1280]{2,1,0:T(8,128)(2,1)S(1)} %stacked.1.refs_0_), channel_id=1, source_target_pairs={{0,16},{4,20},{8,24},{12,28},{16,0},{20,4},{24,8},{28,12},{1,17},{... | collective-permute-start | bytes 1474568 | tf_op jit(solution)/shard_map/ppermute | solution.py:38
  21.5 11.3 %collective-permute-start.11 = (bf16[512,256]{1,0:T(8,128)(2,1)}, bf16[512,256]{1,0:T(8,128)(2,1)}, u32[]{:S(2)}, u32[]{:S(2)}) collective-permute-start(bf16[512,256]{1,0:T(8,128)(2,1)} %get-tuple-element.17.refs_1_), channel_id=1, source_target_pairs={{8,0},{16,8},{4,12},{24,16},{12,20},{20,28},{9,1},{17,9},{5,13},{2... | collective-permute-start | bytes 786440 | tf_op jit(solution)/shard_map/ppermute | solution.py:44
  22.8 12.5 %collective-permute-start.8 = (bf16[528,256]{1,0:T(8,128)(2,1)S(1)}, bf16[528,256]{1,0:T(8,128)(2,1)S(1)}, u32[]{:S(2)}, u32[]{:S(2)}) collective-permute-start(bf16[528,256]{1,0:T(8,128)(2,1)S(1)} %get-tuple-element.15.refs_1_), channel_id=1, source_target_pairs={{12,4},{0,8},{20,12},{8,16},{28,20},{16,24},{13,5},{1,9},{21,13},{... | collective-permute-start | bytes 811016 | tf_op jit(solution)/shard_map/ppermute | solution.py:44
  27.3 13.0 %collective-permute-start.6 = (bf16[528,256]{1,0:T(8,128)(2,1)S(1)}, bf16[528,256]{1,0:T(8,128)(2,1)S(1)}, u32[]{:S(2)}, u32[]{:S(2)}) collective-permute-start(bf16[528,256]{1,0:T(8,128)(2,1)S(1)} %get-tuple-element.15.refs_1_), channel_id=1, source_target_pairs={{0,4},{4,0},{8,12},{12,8},{16,20},{20,16},{24,28},{28,24},{1,5},{5... | collective-permute-start | bytes 811016 | tf_op jit(solution)/shard_map/ppermute | solution.py:38
  27.4 12.9 %collective-permute-start.9 = (bf16[528,256]{1,0:T(8,128)(2,1)S(1)}, bf16[528,256]{1,0:T(8,128)(2,1)S(1)}, u32[]{:S(2)}, u32[]{:S(2)}) collective-permute-start(bf16[528,256]{1,0:T(8,128)(2,1)S(1)} %collective-permute-done.7.refs_3_), channel_id=1, source_target_pairs={{0,4},{4,0},{8,12},{12,8},{16,20},{20,16},{24,28},{28,24},{1,5},{5... | collective-permute-start | bytes 811016 | tf_op jit(solution)/shard_map/ppermute | solution.py:38
  32.7 23.2 %collective-permute-start.3 = (bf16[3,64,1280]{2,1,0:T(8,128)(2,1)S(1)}, bf16[3,64,1280]{2,1,0:T(8,128)(2,1)S(1)}, u32[]{:S(2)}, u32[]{:S(2)}) collective-permute-start(bf16[3,64,1280]{2,1,0:T(8,128)(2,1)S(1)} %stacked.1.refs_0_), channel_id=1, source_target_pairs={{0,4},{4,0},{8,12},{12,8},{16,20},{20,16},{24,28},{28,24},{1,5},{5... | collective-permute-start | bytes 1474568 | tf_op jit(solution)/shard_map/ppermute | solution.py:38
  35.3 24.1 %collective-permute-start.5 = (bf16[3,64,1280]{2,1,0:T(8,128)(2,1)S(1)}, bf16[3,64,1280]{2,1,0:T(8,128)(2,1)S(1)}, u32[]{:S(2)}, u32[]{:S(2)}) collective-permute-start(bf16[3,64,1280]{2,1,0:T(8,128)(2,1)S(1)} %collective-permute-done.4.refs_2_), channel_id=1, source_target_pairs={{0,4},{4,0},{8,12},{12,8},{16,20},{20,16},{24,28},{28,24},{1,5},{5... | collective-permute-start | bytes 1474568 | tf_op jit(solution)/shard_map/ppermute | solution.py:38
  35.3 9.3 %collective-permute-start.12 = (bf16[512,256]{1,0:T(8,128)(2,1)}, bf16[512,256]{1,0:T(8,128)(2,1)}, u32[]{:S(2)}, u32[]{:S(2)}) collective-permute-start(bf16[512,256]{1,0:T(8,128)(2,1)} %get-tuple-element.17.refs_1_), channel_id=1, source_target_pairs={{12,4},{0,8},{20,12},{8,16},{28,20},{16,24},{13,5},{1,9},{21,13},{... | collective-permute-start | bytes 786440 | tf_op jit(solution)/shard_map/ppermute | solution.py:44
  40.3 9.3 %collective-permute-start.10 = (bf16[512,256]{1,0:T(8,128)(2,1)}, bf16[512,256]{1,0:T(8,128)(2,1)S(1)}, u32[]{:S(2)}, u32[]{:S(2)}) collective-permute-start(bf16[512,256]{1,0:T(8,128)(2,1)} %get-tuple-element.17.refs_1_), channel_id=1, source_target_pairs={{0,4},{4,0},{8,12},{12,8},{16,20},{20,16},{24,28},{28,24},{1,5},{5... | collective-permute-start | bytes 786440 | tf_op jit(solution)/shard_map/ppermute | solution.py:38
  40.3 11.5 %collective-permute-start.13 = (bf16[512,256]{1,0:T(8,128)(2,1)}, bf16[512,256]{1,0:T(8,128)(2,1)S(1)}, u32[]{:S(2)}, u32[]{:S(2)}) collective-permute-start(bf16[512,256]{1,0:T(8,128)(2,1)} %collective-permute-done.11.refs_3_), channel_id=1, source_target_pairs={{0,4},{4,0},{8,12},{12,8},{16,20},{20,16},{24,28},{28,24},{1,5},{5... | collective-permute-start | bytes 786440 | tf_op jit(solution)/shard_map/ppermute | solution.py:38
  40.9 0.9 %copy-start = (bf16[512,256]{1,0:T(8,128)(2,1)S(1)}, bf16[512,256]{1,0:T(8,128)(2,1)}, u32[]{:S(2)}) copy-start(bf16[512,256]{1,0:T(8,128)(2,1)} %refs_0_.3) | copy-start | bytes 786436
  44.5 7.7 %copy-start.1 = (bf16[512,256]{1,0:T(8,128)(2,1)S(1)}, bf16[512,256]{1,0:T(8,128)(2,1)}, u32[]{:S(2)}) copy-start(bf16[512,256]{1,0:T(8,128)(2,1)} %refs_0_.3) | copy-start | bytes 786436
  44.6 13.7 %collective-permute-start.16 = (bf16[512,128]{1,0:T(8,128)(2,1)S(1)}, bf16[512,128]{1,0:T(8,128)(2,1)S(1)}, u32[]{:S(2)}, u32[]{:S(2)}) collective-permute-start(bf16[512,128]{1,0:T(8,128)(2,1)S(1)} %get-tuple-element.16.refs_0_), channel_id=1, source_target_pairs={{0,3},{1,2},{2,1},{3,0},{4,7},{5,6},{6,5},{7,4},{8,11},{9,10},{10,... | collective-permute-start | bytes 393224 | tf_op jit(solution)/shard_map/ppermute | solution.py:30
  49.7 14.3 %collective-permute-start.15 = (bf16[512,128]{1,0:T(8,128)(2,1)S(1)}, bf16[512,128]{1,0:T(8,128)(2,1)S(1)}, u32[]{:S(2)}, u32[]{:S(2)}) collective-permute-start(bf16[512,128]{1,0:T(8,128)(2,1)S(1)} %get-tuple-element.16.refs_0_), channel_id=1, source_target_pairs={{0,2},{1,3},{2,0},{3,1},{4,6},{5,7},{6,4},{7,5},{8,10},{9,11},{10,... | collective-permute-start | bytes 393224 | tf_op jit(solution)/shard_map/ppermute | solution.py:30
  51.8 12.1 %collective-permute-start.14 = (bf16[512,128]{1,0:T(8,128)(2,1)S(1)}, bf16[512,128]{1,0:T(8,128)(2,1)S(1)}, u32[]{:S(2)}, u32[]{:S(2)}) collective-permute-start(bf16[512,128]{1,0:T(8,128)(2,1)S(1)} %get-tuple-element.16.refs_0_), channel_id=1, source_target_pairs={{0,1},{1,0},{2,3},{3,2},{4,5},{5,4},{6,7},{7,6},{8,9},{9,8},{10,11... | collective-permute-start | bytes 393224 | tf_op jit(solution)/shard_map/ppermute | solution.py:30
  55.9 17.4 %collective-permute-start.19 = (bf16[512,128]{1,0:T(8,128)(2,1)S(1)}, bf16[512,128]{1,0:T(8,128)(2,1)S(1)}, u32[]{:S(2)}, u32[]{:S(2)}) collective-permute-start(bf16[512,128]{1,0:T(8,128)(2,1)S(1)} %attend.3.refs_1_), channel_id=1, source_target_pairs={{0,3},{1,2},{2,1},{3,0},{4,7},{5,6},{6,5},{7,4},{8,11},{9,10},{10,... | collective-permute-start | bytes 393224 | tf_op jit(solution)/shard_map/ppermute | solution.py:30
  58.3 8.5 %collective-permute-start.18 = (bf16[512,128]{1,0:T(8,128)(2,1)S(1)}, bf16[512,128]{1,0:T(8,128)(2,1)S(1)}, u32[]{:S(2)}, u32[]{:S(2)}) collective-permute-start(bf16[512,128]{1,0:T(8,128)(2,1)S(1)} %attend.3.refs_1_), channel_id=1, source_target_pairs={{0,1},{1,0},{2,3},{3,2},{4,5},{5,4},{6,7},{7,6},{8,9},{9,8},{10,11... | collective-permute-start | bytes 393224 | tf_op jit(solution)/shard_map/ppermute | solution.py:30
  59.4 13.1 %collective-permute-start.17 = (bf16[512,128]{1,0:T(8,128)(2,1)S(1)}, bf16[512,128]{1,0:T(8,128)(2,1)S(1)}, u32[]{:S(2)}, u32[]{:S(2)}) collective-permute-start(bf16[512,128]{1,0:T(8,128)(2,1)S(1)} %attend.3.refs_1_), channel_id=1, source_target_pairs={{0,2},{1,3},{2,0},{3,1},{4,6},{5,7},{6,4},{7,5},{8,10},{9,11},{10,... | collective-permute-start | bytes 393224 | tf_op jit(solution)/shard_map/ppermute | solution.py:30

commit v5 on v4

--- a/solution.py
+++ b/solution.py
@@ -44,21 +44,21 @@
     return lax.ppermute(block, axis, [(s, d) for s, d in route if 0 <= s < count])
 
 
-def pack(keys, values, segment_ids):
+def pack(keys, values, segment_ids, heads):
     rows, width = keys.shape
     head = width // HEAD_DEV
     wide = 2 * head
     lines = rows // wide
 
     def body(k_ref, v_ref, s_ref, *refs):
-        messages, (ids_ref, sems) = refs[:HEAD_DEV], refs[HEAD_DEV:]
+        messages, (ids_ref, sems) = refs[:len(heads)], refs[len(heads):]
         copies = [pltpu.make_async_copy(s_ref, ids_ref, sems.at[0])]
-        for index, ref in enumerate(messages):
+        for place, (index, ref) in enumerate(zip(heads, messages)):
             for side, source in enumerate((k_ref, v_ref)):
                 copies.append(pltpu.make_async_copy(
                     source.at[:, index * head:(index + 1) * head],
                     ref.at[:rows, side * head:(side + 1) * head],
-                    sems.at[1 + 2 * index + side],
+                    sems.at[1 + 2 * place + side],
                 ))
         for copy in copies:
             copy.start()
@@ -66,19 +66,20 @@
         marks = (ids_ref[...] + 1).astype(jnp.float32)
         parts = [marks[:, i * wide:(i + 1) * wide] for i in range(lines)]
         parts.append(jnp.zeros((PAD_ROWS - lines, wide), jnp.float32))
-        messages[0][rows:, :] = jnp.concatenate(parts, axis=0).astype(jnp.bfloat16)
+        if 0 in heads:
+            messages[0][rows:, :] = jnp.concatenate(parts, axis=0).astype(jnp.bfloat16)
         for copy in copies[1:]:
             copy.wait()
 
-    shapes = [(rows + PAD_ROWS, wide)] + [(rows, wide)] * (HEAD_DEV - 1)
+    shapes = [(rows if index else rows + PAD_ROWS, wide) for index in heads]
     return pl.pallas_call(
         body,
         name="pack",
         in_specs=[IN_HBM] * 3,
-        out_specs=[IN_VMEM] * HEAD_DEV,
+        out_specs=[IN_VMEM] * len(heads),
         out_shape=[jax.ShapeDtypeStruct(shape, jnp.bfloat16) for shape in shapes],
         scratch_shapes=[
-            pltpu.VMEM((1, rows), jnp.int32), pltpu.SemaphoreType.DMA((1 + 2 * HEAD_DEV,)),
+            pltpu.VMEM((1, rows), jnp.int32), pltpu.SemaphoreType.DMA((1 + 2 * len(heads),)),
         ],
         compiler_params=pltpu.CompilerParams(vmem_limit_bytes=KERNEL_VMEM),
         cost_estimate=pl.CostEstimate(flops=10**9, bytes_accessed=8 * rows * width, transcendentals=0),
@@ -320,7 +321,8 @@
     mine = (place & 1) + 2 * ((place >> 2) & 1)
     part, columns = out_weight.shape[0] // replicas, out_weight.shape[1] // groups
 
-    messages = pack(keys, values, segment_ids)
+    messages = pack(keys, values, segment_ids, [0])
+    messages = [*messages, *pack(keys, values, segment_ids, list(range(1, HEAD_DEV)))]
 
     aligned = columns % LANES == 0
     corners = [

time: 75 us -> 74.2 us (0.989)
  the two profiles are of different devices: /device:TPU:0 before, /device:TPU:4 now
where the time goes in v5:
time: 74.2 us; the launch traced here: 73.9 us
  starting transfers between devices  28.6 us (39%)
  waiting for transfers between devices  27.7 us (37%)
  Pallas kernels  16.3 us (22%)
  local copies, waits for them, and re-layouts  1.04 us (1%)
    ppermute x9, waiting for transfers between devices, to_partner(): lax.ppermute(block, axis, [(i, partner(i, distance, count)) for i in rang...  16.6 us
    ppermute x9, starting transfers between devices, to_partner(): lax.ppermute(block, axis, [(i, partner(i, distance, count)) for i in rang...  14.8 us
    ppermute x4, starting transfers between devices, from_far(): lax.ppermute(block, axis, [(s, d) for s, d in route if 0 <= s < count])  11.8 us
    ppermute x4, waiting for transfers between devices, from_far(): lax.ppermute(block, axis, [(s, d) for s, d in route if 0 <= s < count])  10.5 us
    pallas_call x2, Pallas kernels, attend(): pl.pallas_call(body, name='attend', in_specs=[IN_VMEM] * (1 + count + (no...  6.37 us
    pallas_call x2, Pallas kernels, cut(): pl.pallas_call(body, name='cut', in_specs=[pl.BlockSpec(memory_space=pltp...  3.29 us
    pallas_call x2, Pallas kernels, pack(): pl.pallas_call(body, name='pack', in_specs=[IN_HBM] * 3, out_specs=[IN_VM...  2.72 us
    pallas_call x2, Pallas kernels, project_more(): pl.pallas_call(body, name='project_last' if last else 'project_more', in_...  2.19 us
  transfers between devices with their start and end apart: 20, of which 8 were waited for; matrix products, arithmetic and copies ran while one was open for 0% of the time, Pallas kernels for 18%

profile of v5, /device:TPU:4, one launch (start us, length us, event | category | flops | bytes accessed | tf_op | source)
XLA Modules:
  0.0 73.9 jit_solution(11327183359147886002)
XLA Ops:
  0.0 0.1 stack.29.corner_ref
  0.1 1.6 %cut.3 = (bf16[64,1280]{1,0:T(8,128)(2,1)S(1)}, bf16[64,1280]{1,0:T(8,128)(2,1)S(1)}, bf16[64,1280]{1,0:T(8,128)(2,1)S(1)}) custom-call(s32[6]{0:T(128)S(1)} %stack.29.corner_ref, bf16[256,5120]{1,0:T(8,128)(2,1)} %source_ref.3), custom_call_target="tpu_custom_call" | custom-call | flops 1000000000 | bytes 983040 | tf_op jit(solution)/shard_map/cut/pallas_call | solution.py:105
  1.7 1.6 %collective-permute-start = (bf16[64,1280]{1,0:T(8,128)(2,1)S(1)}, bf16[64,1280]{1,0:T(8,128)(2,1)S(1)}, u32[]{:S(2)}, u32[]{:S(2)}) collective-permute-start(bf16[64,1280]{1,0:T(8,128)(2,1)S(1)} %get-tuple-element.10), channel_id=1, source_target_pairs={{0,1},{1,0},{2,3},{3,2},{4,5},{5,4},{6,7},{7,6},{8,9},{9,8},{10,11... | collective-permute-start | bytes 491528 | tf_op jit(solution)/shard_map/ppermute | solution.py:30
  3.4 2.6 %collective-permute-start.1 = (bf16[64,1280]{1,0:T(8,128)(2,1)S(1)}, bf16[64,1280]{1,0:T(8,128)(2,1)S(1)}, u32[]{:S(2)}, u32[]{:S(2)}) collective-permute-start(bf16[64,1280]{1,0:T(8,128)(2,1)S(1)} %get-tuple-element.11), channel_id=1, source_target_pairs={{0,2},{1,3},{2,0},{3,1},{4,6},{5,7},{6,4},{7,5},{8,10},{9,11},{10,... | collective-permute-start | bytes 491528 | tf_op jit(solution)/shard_map/ppermute | solution.py:30
  6.0 0.2 collective-permute-start.2
  6.2 1.0 %pack.2.refs_1_ = bf16[528,256]{1,0:T(8,128)(2,1)S(1)} custom-call(bf16[512,256]{1,0:T(8,128)(2,1)} %k_ref.3, bf16[512,256]{1,0:T(8,128)(2,1)} %v_ref.3, s32[1,512]{1,0:T(1,128)} %bitcast.7), custom_call_target="tpu_custom_call" | custom-call | flops 1000000000 | bytes 1048576 | tf_op jit(solution)/shard_map/pack/pallas_call | solution.py:75
  7.2 3.3 %collective-permute-start.7 = (bf16[528,256]{1,0:T(8,128)(2,1)S(1)}, bf16[528,256]{1,0:T(8,128)(2,1)S(1)}, u32[]{:S(2)}, u32[]{:S(2)}) collective-permute-start(bf16[528,256]{1,0:T(8,128)(2,1)S(1)} %pack.2.refs_1_), channel_id=1, source_target_pairs={{8,0},{16,8},{4,12},{24,16},{12,20},{20,28},{9,1},{17,9},{5,13},{2... | collective-permute-start | bytes 811016 | tf_op jit(solution)/shard_map/ppermute | solution.py:44
  10.6 0.0 collective-permute-done.refs_0_
  10.6 7.8 %collective-permute-done.1.refs_1_ = bf16[64,1280]{1,0:T(8,128)(2,1)S(1)} collective-permute-done((bf16[64,1280]{1,0:T(8,128)(2,1)S(1)}, bf16[64,1280]{1,0:T(8,128)(2,1)S(1)}, u32[]{:S(2)}, u32[]{:S(2)}) %collective-permute-start.1) | collective-permute-done | bytes 163872 | tf_op jit(solution)/shard_map/ppermute | solution.py:30
  18.4 0.0 collective-permute-done.2.refs_2_
  18.4 0.6 collective-permute-start.4
  19.0 1.7 %pack.3.refs_1_ = bf16[512,256]{1,0:T(8,128)(2,1)} custom-call(bf16[512,256]{1,0:T(8,128)(2,1)} %k_ref.3, bf16[512,256]{1,0:T(8,128)(2,1)} %v_ref.3, s32[1,512]{1,0:T(1,128)} %bitcast.8), custom_call_target="tpu_custom_call" | custom-call | flops 1000000000 | bytes 1048576 | tf_op jit(solution)/shard_map/pack/pallas_call | solution.py:75
  20.7 4.4 %collective-permute-start.11 = (bf16[512,256]{1,0:T(8,128)(2,1)}, bf16[512,256]{1,0:T(8,128)(2,1)}, u32[]{:S(2)}, u32[]{:S(2)}) collective-permute-start(bf16[512,256]{1,0:T(8,128)(2,1)} %pack.3.refs_1_), channel_id=1, source_target_pairs={{8,0},{16,8},{4,12},{24,16},{12,20},{20,28},{9,1},{17,9},{5,13},{2... | collective-permute-start | bytes 786440 | tf_op jit(solution)/shard_map/ppermute | solution.py:44
  25.1 2.2 %collective-permute-start.8 = (bf16[528,256]{1,0:T(8,128)(2,1)S(1)}, bf16[528,256]{1,0:T(8,128)(2,1)S(1)}, u32[]{:S(2)}, u32[]{:S(2)}) collective-permute-start(bf16[528,256]{1,0:T(8,128)(2,1)S(1)} %pack.2.refs_1_), channel_id=1, source_target_pairs={{12,4},{0,8},{20,12},{8,16},{28,20},{16,24},{13,5},{1,9},{21,13},{... | collective-permute-start | bytes 811016 | tf_op jit(solution)/shard_map/ppermute | solution.py:44
  27.2 0.1 collective-permute-start.6
  27.3 0.0 collective-permute-done.7.refs_3_
  27.3 0.5 collective-permute-start.9
  27.8 3.5 %collective-permute-done.11.refs_3_ = bf16[512,256]{1,0:T(8,128)(2,1)} collective-permute-done((bf16[512,256]{1,0:T(8,128)(2,1)}, bf16[512,256]{1,0:T(8,128)(2,1)}, u32[]{:S(2)}, u32[]{:S(2)}) %collective-permute-start.11) | collective-permute-done | bytes 262176 | tf_op jit(solution)/shard_map/ppermute | solution.py:44
  31.3 0.0 collective-permute-start.3
  31.3 0.6 collective-permute-done.4.refs_2_
  31.9 0.0 collective-permute-start.5
  31.9 3.9 %collective-permute-done.8.refs_4_ = bf16[528,256]{1,0:T(8,128)(2,1)S(1)} collective-permute-done((bf16[528,256]{1,0:T(8,128)(2,1)S(1)}, bf16[528,256]{1,0:T(8,128)(2,1)S(1)}, u32[]{:S(2)}, u32[]{:S(2)}) %collective-permute-start.8) | collective-permute-done | bytes 270368 | tf_op jit(solution)/shard_map/ppermute | solution.py:44
  35.7 1.9 %collective-permute-start.12 = (bf16[512,256]{1,0:T(8,128)(2,1)}, bf16[512,256]{1,0:T(8,128)(2,1)}, u32[]{:S(2)}, u32[]{:S(2)}) collective-permute-start(bf16[512,256]{1,0:T(8,128)(2,1)} %pack.3.refs_1_), channel_id=1, source_target_pairs={{12,4},{0,8},{20,12},{8,16},{28,20},{16,24},{13,5},{1,9},{21,13},{... | collective-permute-start | bytes 786440 | tf_op jit(solution)/shard_map/ppermute | solution.py:44
  37.6 0.0 collective-permute-done.6.refs_2_
  37.7 0.8 %collective-permute-start.10 = (bf16[512,256]{1,0:T(8,128)(2,1)}, bf16[512,256]{1,0:T(8,128)(2,1)S(1)}, u32[]{:S(2)}, u32[]{:S(2)}) collective-permute-start(bf16[512,256]{1,0:T(8,128)(2,1)} %pack.3.refs_1_), channel_id=1, source_target_pairs={{0,4},{4,0},{8,12},{12,8},{16,20},{20,16},{24,28},{28,24},{1,5},{5... | collective-permute-start | bytes 786440 | tf_op jit(solution)/shard_map/ppermute | solution.py:38
  38.4 0.1 collective-permute-start.13
  38.5 0.1 pad_add_fusion.corner_ref
  38.6 0.9 %copy-done = bf16[512,256]{1,0:T(8,128)(2,1)S(1)} copy-done((bf16[512,256]{1,0:T(8,128)(2,1)S(1)}, bf16[512,256]{1,0:T(8,128)(2,1)}, u32[]{:S(2)}) %copy-start) | copy-done | bytes 262168
  39.5 2.6 %attend.2 = (bf16[512,128]{1,0:T(8,128)(2,1)S(1)}, f32[16,256]{1,0:T(8,128)S(1)}) custom-call(bf16[512,256]{1,0:T(8,128)(2,1)S(1)} %copy-done, bf16[528,256]{1,0:T(8,128)(2,1)S(1)} %pack.2.refs_1_, bf16[528,256]{1,0:T(8,128)(2,1)S(1)} %collective-permute-done.6.refs_2_, bf16[528,256]{1,0:T(8,128)(2,1)S(1)} %collective-permute-done.7.refs_3_, ...), custom_call_target="tpu_custom_call" | custom-call | flops 1342177280 | bytes 1310720 | tf_op jit(solution)/shard_map/attend/pallas_call | solution.py:191
  42.2 0.0 copy-start.1
  42.2 3.2 %collective-permute-done.12.refs_4_ = bf16[512,256]{1,0:T(8,128)(2,1)} collective-permute-done((bf16[512,256]{1,0:T(8,128)(2,1)}, bf16[512,256]{1,0:T(8,128)(2,1)}, u32[]{:S(2)}, u32[]{:S(2)}) %collective-permute-start.12) | collective-permute-done | bytes 262176 | tf_op jit(solution)/shard_map/ppermute | solution.py:44
  45.4 2.6 %collective-permute-start.16 = (bf16[512,128]{1,0:T(8,128)(2,1)S(1)}, bf16[512,128]{1,0:T(8,128)(2,1)S(1)}, u32[]{:S(2)}, u32[]{:S(2)}) collective-permute-start(bf16[512,128]{1,0:T(8,128)(2,1)S(1)} %get-tuple-element.13.refs_0_), channel_id=1, source_target_pairs={{0,3},{1,2},{2,1},{3,0},{4,7},{5,6},{6,5},{7,4},{8,11},{9,10},{10,... | collective-permute-start | bytes 393224 | tf_op jit(solution)/shard_map/ppermute | solution.py:30
  48.0 1.6 %cut.2.own_ref = bf16[256,1280]{1,0:T(8,128)(2,1)S(1)} custom-call(s32[2]{0:T(128)S(1)} %pad_add_fusion.corner_ref, bf16[256,5120]{1,0:T(8,128)(2,1)} %source_ref.3), custom_call_target="tpu_custom_call" | custom-call | flops 1000000000 | bytes 1310720 | tf_op jit(solution)/shard_map/cut/pallas_call | solution.py:105
  49.6 0.0 collective-permute-done.10.refs_2_
  49.6 3.0 %collective-permute-start.15 = (bf16[512,128]{1,0:T(8,128)(2,1)S(1)}, bf16[512,128]{1,0:T(8,128)(2,1)S(1)}, u32[]{:S(2)}, u32[]{:S(2)}) collective-permute-start(bf16[512,128]{1,0:T(8,128)(2,1)S(1)} %get-tuple-element.13.refs_0_), channel_id=1, source_target_pairs={{0,2},{1,3},{2,0},{3,1},{4,6},{5,7},{6,4},{7,5},{8,10},{9,11},{10,... | collective-permute-start | bytes 393224 | tf_op jit(solution)/shard_map/ppermute | solution.py:30
  52.6 0.4 collective-permute-start.14
  52.9 3.7 %attend.3.refs_1_ = bf16[512,128]{1,0:T(8,128)(2,1)S(1)} custom-call(bf16[512,256]{1,0:T(8,128)(2,1)S(1)} %copy-done.1, bf16[512,256]{1,0:T(8,128)(2,1)} %pack.3.refs_1_, bf16[512,256]{1,0:T(8,128)(2,1)S(1)} %collective-permute-done.10.refs_2_, bf16[512,256]{1,0:T(8,128)(2,1)} %collective-permute-done.11.refs_3_, ...), custom_call_target="tpu_custom_call" | custom-call | flops 1342177280 | bytes 1310720 | tf_op jit(solution)/shard_map/attend/pallas_call | solution.py:191
  56.7 0.0 collective-permute-done.3.refs_1_
  56.7 2.3 %collective-permute-start.19 = (bf16[512,128]{1,0:T(8,128)(2,1)S(1)}, bf16[512,128]{1,0:T(8,128)(2,1)S(1)}, u32[]{:S(2)}, u32[]{:S(2)}) collective-permute-start(bf16[512,128]{1,0:T(8,128)(2,1)S(1)} %attend.3.refs_1_), channel_id=1, source_target_pairs={{0,3},{1,2},{2,1},{3,0},{4,7},{5,6},{6,5},{7,4},{8,11},{9,10},{10,... | collective-permute-start | bytes 393224 | tf_op jit(solution)/shard_map/ppermute | solution.py:30
  59.0 1.1 %collective-permute-start.18 = (bf16[512,128]{1,0:T(8,128)(2,1)S(1)}, bf16[512,128]{1,0:T(8,128)(2,1)S(1)}, u32[]{:S(2)}, u32[]{:S(2)}) collective-permute-start(bf16[512,128]{1,0:T(8,128)(2,1)S(1)} %attend.3.refs_1_), channel_id=1, source_target_pairs={{0,1},{1,0},{2,3},{3,2},{4,5},{5,4},{6,7},{7,6},{8,9},{9,8},{10,11... | collective-permute-start | bytes 393224 | tf_op jit(solution)/shard_map/ppermute | solution.py:30
  60.2 1.0 %collective-permute-start.17 = (bf16[512,128]{1,0:T(8,128)(2,1)S(1)}, bf16[512,128]{1,0:T(8,128)(2,1)S(1)}, u32[]{:S(2)}, u32[]{:S(2)}) collective-permute-start(bf16[512,128]{1,0:T(8,128)(2,1)S(1)} %attend.3.refs_1_), channel_id=1, source_target_pairs={{0,2},{1,3},{2,0},{3,1},{4,6},{5,7},{6,4},{7,5},{8,10},{9,11},{10,... | collective-permute-start | bytes 393224 | tf_op jit(solution)/shard_map/ppermute | solution.py:30
  61.1 0.2 assemble.1.w_ref
  61.3 1.0 %collective-permute-done.15.refs_3_ = bf16[512,128]{1,0:T(8,128)(2,1)S(1)} collective-permute-done((bf16[512,128]{1,0:T(8,128)(2,1)S(1)}, bf16[512,128]{1,0:T(8,128)(2,1)S(1)}, u32[]{:S(2)}, u32[]{:S(2)}) %collective-permute-start.15) | collective-permute-done | bytes 131104 | tf_op jit(solution)/shard_map/ppermute | solution.py:30
  62.3 1.5 %project_first.1.p_ref = f32[512,1280]{1,0:T(8,128)S(1)} custom-call(bf16[4,256,1280]{2,1,0:T(8,128)(2,1)S(1)} %assemble.1.w_ref, bf16[512,128]{1,0:T(8,128)(2,1)S(1)} %get-tuple-element.13.refs_0_, bf16[512,128]{1,0:T(8,128)(2,1)S(1)} %attend.3.refs_1_, bf16[512,128]{1,0:T(8,128)(2,1)S(1)} %collective-permute-done.14.refs_2_, ...), custom_call_target="tpu_custom_call" | custom-call | flops 671088640 | bytes 2621440 | tf_op jit(solution)/shard_map/project_first/pallas_call | solution.py:263
  63.8 2.2 %collective-permute-done.18.refs_1_ = bf16[512,128]{1,0:T(8,128)(2,1)S(1)} collective-permute-done((bf16[512,128]{1,0:T(8,128)(2,1)S(1)}, bf16[512,128]{1,0:T(8,128)(2,1)S(1)}, u32[]{:S(2)}, u32[]{:S(2)}) %collective-permute-start.18) | collective-permute-done | bytes 131104 | tf_op jit(solution)/shard_map/ppermute | solution.py:30
  66.1 5.6 %collective-permute-done.17.refs_0_ = bf16[512,128]{1,0:T(8,128)(2,1)S(1)} collective-permute-done((bf16[512,128]{1,0:T(8,128)(2,1)S(1)}, bf16[512,128]{1,0:T(8,128)(2,1)S(1)}, u32[]{:S(2)}, u32[]{:S(2)}) %collective-permute-start.17) | collective-permute-done | bytes 131104 | tf_op jit(solution)/shard_map/ppermute | solution.py:30
  71.7 0.8 %project_more.1.p_ref = f32[512,1280]{1,0:T(8,128)S(1)} custom-call(bf16[4,256,1280]{2,1,0:T(8,128)(2,1)S(1)} %assemble.1.w_ref, f32[512,1280]{1,0:T(8,128)S(1)} %project_first.1.p_ref, bf16[512,128]{1,0:T(8,128)(2,1)S(1)} %collective-permute-done.17.refs_0_, bf16[512,128]{1,0:T(8,128)(2,1)S(1)} %collective-permute-done.18.refs_1_), custom_call_target="tpu_custom_call" | custom-call | flops 335544320 | bytes 2621440 | tf_op jit(solution)/shard_map/project_more/pallas_call | solution.py:302
  72.5 1.4 %project_last.1 = bf16[512,1280]{1,0:T(8,128)(2,1)} custom-call(bf16[4,256,1280]{2,1,0:T(8,128)(2,1)S(1)} %assemble.1.w_ref, f32[512,1280]{1,0:T(8,128)S(1)} %project_more.1.p_ref, bf16[512,128]{1,0:T(8,128)(2,1)S(1)} %collective-permute-done.19.refs_0_), custom_call_target="tpu_custom_call" | custom-call | flops 167772160 | bytes 2621440 | tf_op jit(solution)/shard_map/project_last/pallas_call | solution.py:302
  (9 shorter events, 0.1 us)
Async XLA Ops:
  1.7 8.8 %collective-permute-start = (bf16[64,1280]{1,0:T(8,128)(2,1)S(1)}, bf16[64,1280]{1,0:T(8,128)(2,1)S(1)}, u32[]{:S(2)}, u32[]{:S(2)}) collective-permute-start(bf16[64,1280]{1,0:T(8,128)(2,1)S(1)} %get-tuple-element.10), channel_id=1, source_target_pairs={{0,1},{1,0},{2,3},{3,2},{4,5},{5,4},{6,7},{7,6},{8,9},{9,8},{10,11... | collective-permute-start | bytes 491528 | tf_op jit(solution)/shard_map/ppermute | solution.py:30
  3.4 15.0 %collective-permute-start.1 = (bf16[64,1280]{1,0:T(8,128)(2,1)S(1)}, bf16[64,1280]{1,0:T(8,128)(2,1)S(1)}, u32[]{:S(2)}, u32[]{:S(2)}) collective-permute-start(bf16[64,1280]{1,0:T(8,128)(2,1)S(1)} %get-tuple-element.11), channel_id=1, source_target_pairs={{0,2},{1,3},{2,0},{3,1},{4,6},{5,7},{6,4},{7,5},{8,10},{9,11},{10,... | collective-permute-start | bytes 491528 | tf_op jit(solution)/shard_map/ppermute | solution.py:30
  6.0 12.4 %collective-permute-start.2 = (bf16[64,1280]{1,0:T(8,128)(2,1)S(1)}, bf16[64,1280]{1,0:T(8,128)(2,1)S(1)}, u32[]{:S(2)}, u32[]{:S(2)}) collective-permute-start(bf16[64,1280]{1,0:T(8,128)(2,1)S(1)} %get-tuple-element.12), channel_id=1, source_target_pairs={{0,3},{1,2},{2,1},{3,0},{4,7},{5,6},{6,5},{7,4},{8,11},{9,10},{10,... | collective-permute-start | bytes 491528 | tf_op jit(solution)/shard_map/ppermute | solution.py:30
  7.2 20.1 %collective-permute-start.7 = (bf16[528,256]{1,0:T(8,128)(2,1)S(1)}, bf16[528,256]{1,0:T(8,128)(2,1)S(1)}, u32[]{:S(2)}, u32[]{:S(2)}) collective-permute-start(bf16[528,256]{1,0:T(8,128)(2,1)S(1)} %pack.2.refs_1_), channel_id=1, source_target_pairs={{8,0},{16,8},{4,12},{24,16},{12,20},{20,28},{9,1},{17,9},{5,13},{2... | collective-permute-start | bytes 811016 | tf_op jit(solution)/shard_map/ppermute | solution.py:44
  18.4 13.4 %collective-permute-start.4 = (bf16[3,64,1280]{2,1,0:T(8,128)(2,1)S(1)}, bf16[3,64,1280]{2,1,0:T(8,128)(2,1)S(1)}, u32[]{:S(2)}, u32[]{:S(2)}) collective-permute-start(bf16[3,64,1280]{2,1,0:T(8,128)(2,1)S(1)} %stacked.1.refs_0_), channel_id=1, source_target_pairs={{0,16},{4,20},{8,24},{12,28},{16,0},{20,4},{24,8},{28,12},{1,17},{... | collective-permute-start | bytes 1474568 | tf_op jit(solution)/shard_map/ppermute | solution.py:38
  20.7 10.6 %collective-permute-start.11 = (bf16[512,256]{1,0:T(8,128)(2,1)}, bf16[512,256]{1,0:T(8,128)(2,1)}, u32[]{:S(2)}, u32[]{:S(2)}) collective-permute-start(bf16[512,256]{1,0:T(8,128)(2,1)} %pack.3.refs_1_), channel_id=1, source_target_pairs={{8,0},{16,8},{4,12},{24,16},{12,20},{20,28},{9,1},{17,9},{5,13},{2... | collective-permute-start | bytes 786440 | tf_op jit(solution)/shard_map/ppermute | solution.py:44
  25.1 10.6 %collective-permute-start.8 = (bf16[528,256]{1,0:T(8,128)(2,1)S(1)}, bf16[528,256]{1,0:T(8,128)(2,1)S(1)}, u32[]{:S(2)}, u32[]{:S(2)}) collective-permute-start(bf16[528,256]{1,0:T(8,128)(2,1)S(1)} %pack.2.refs_1_), channel_id=1, source_target_pairs={{12,4},{0,8},{20,12},{8,16},{28,20},{16,24},{13,5},{1,9},{21,13},{... | collective-permute-start | bytes 811016 | tf_op jit(solution)/shard_map/ppermute | solution.py:44
  27.2 10.4 %collective-permute-start.6 = (bf16[528,256]{1,0:T(8,128)(2,1)S(1)}, bf16[528,256]{1,0:T(8,128)(2,1)S(1)}, u32[]{:S(2)}, u32[]{:S(2)}) collective-permute-start(bf16[528,256]{1,0:T(8,128)(2,1)S(1)} %pack.2.refs_1_), channel_id=1, source_target_pairs={{0,4},{4,0},{8,12},{12,8},{16,20},{20,16},{24,28},{28,24},{1,5},{5... | collective-permute-start | bytes 811016 | tf_op jit(solution)/shard_map/ppermute | solution.py:38
  27.3 11.1 %collective-permute-start.9 = (bf16[528,256]{1,0:T(8,128)(2,1)S(1)}, bf16[528,256]{1,0:T(8,128)(2,1)S(1)}, u32[]{:S(2)}, u32[]{:S(2)}) collective-permute-start(bf16[528,256]{1,0:T(8,128)(2,1)S(1)} %collective-permute-done.7.refs_3_), channel_id=1, source_target_pairs={{0,4},{4,0},{8,12},{12,8},{16,20},{20,16},{24,28},{28,24},{1,5},{5... | collective-permute-start | bytes 811016 | tf_op jit(solution)/shard_map/ppermute | solution.py:38
  31.3 25.4 %collective-permute-start.3 = (bf16[3,64,1280]{2,1,0:T(8,128)(2,1)S(1)}, bf16[3,64,1280]{2,1,0:T(8,128)(2,1)S(1)}, u32[]{:S(2)}, u32[]{:S(2)}) collective-permute-start(bf16[3,64,1280]{2,1,0:T(8,128)(2,1)S(1)} %stacked.1.refs_0_), channel_id=1, source_target_pairs={{0,4},{4,0},{8,12},{12,8},{16,20},{20,16},{24,28},{28,24},{1,5},{5... | collective-permute-start | bytes 1474568 | tf_op jit(solution)/shard_map/ppermute | solution.py:38
  31.9 28.3 %collective-permute-start.5 = (bf16[3,64,1280]{2,1,0:T(8,128)(2,1)S(1)}, bf16[3,64,1280]{2,1,0:T(8,128)(2,1)S(1)}, u32[]{:S(2)}, u32[]{:S(2)}) collective-permute-start(bf16[3,64,1280]{2,1,0:T(8,128)(2,1)S(1)} %collective-permute-done.4.refs_2_), channel_id=1, source_target_pairs={{0,4},{4,0},{8,12},{12,8},{16,20},{20,16},{24,28},{28,24},{1,5},{5... | collective-permute-start | bytes 1474568 | tf_op jit(solution)/shard_map/ppermute | solution.py:38
  35.7 9.7 %collective-permute-start.12 = (bf16[512,256]{1,0:T(8,128)(2,1)}, bf16[512,256]{1,0:T(8,128)(2,1)}, u32[]{:S(2)}, u32[]{:S(2)}) collective-permute-start(bf16[512,256]{1,0:T(8,128)(2,1)} %pack.3.refs_1_), channel_id=1, source_target_pairs={{12,4},{0,8},{20,12},{8,16},{28,20},{16,24},{13,5},{1,9},{21,13},{... | collective-permute-start | bytes 786440 | tf_op jit(solution)/shard_map/ppermute | solution.py:44
  37.7 12.0 %collective-permute-start.10 = (bf16[512,256]{1,0:T(8,128)(2,1)}, bf16[512,256]{1,0:T(8,128)(2,1)S(1)}, u32[]{:S(2)}, u32[]{:S(2)}) collective-permute-start(bf16[512,256]{1,0:T(8,128)(2,1)} %pack.3.refs_1_), channel_id=1, source_target_pairs={{0,4},{4,0},{8,12},{12,8},{16,20},{20,16},{24,28},{28,24},{1,5},{5... | collective-permute-start | bytes 786440 | tf_op jit(solution)/shard_map/ppermute | solution.py:38
  38.4 14.2 %collective-permute-start.13 = (bf16[512,256]{1,0:T(8,128)(2,1)}, bf16[512,256]{1,0:T(8,128)(2,1)S(1)}, u32[]{:S(2)}, u32[]{:S(2)}) collective-permute-start(bf16[512,256]{1,0:T(8,128)(2,1)} %collective-permute-done.11.refs_3_), channel_id=1, source_target_pairs={{0,4},{4,0},{8,12},{12,8},{16,20},{20,16},{24,28},{28,24},{1,5},{5... | collective-permute-start | bytes 786440 | tf_op jit(solution)/shard_map/ppermute | solution.py:38
  38.6 0.9 %copy-start = (bf16[512,256]{1,0:T(8,128)(2,1)S(1)}, bf16[512,256]{1,0:T(8,128)(2,1)}, u32[]{:S(2)}) copy-start(bf16[512,256]{1,0:T(8,128)(2,1)} %refs_0_.3) | copy-start | bytes 786436
  42.2 10.8 %copy-start.1 = (bf16[512,256]{1,0:T(8,128)(2,1)S(1)}, bf16[512,256]{1,0:T(8,128)(2,1)}, u32[]{:S(2)}) copy-start(bf16[512,256]{1,0:T(8,128)(2,1)} %refs_0_.3) | copy-start | bytes 786436
  45.4 13.7 %collective-permute-start.16 = (bf16[512,128]{1,0:T(8,128)(2,1)S(1)}, bf16[512,128]{1,0:T(8,128)(2,1)S(1)}, u32[]{:S(2)}, u32[]{:S(2)}) collective-permute-start(bf16[512,128]{1,0:T(8,128)(2,1)S(1)} %get-tuple-element.13.refs_0_), channel_id=1, source_target_pairs={{0,3},{1,2},{2,1},{3,0},{4,7},{5,6},{6,5},{7,4},{8,11},{9,10},{10,... | collective-permute-start | bytes 393224 | tf_op jit(solution)/shard_map/ppermute | solution.py:30
  49.6 12.7 %collective-permute-start.15 = (bf16[512,128]{1,0:T(8,128)(2,1)S(1)}, bf16[512,128]{1,0:T(8,128)(2,1)S(1)}, u32[]{:S(2)}, u32[]{:S(2)}) collective-permute-start(bf16[512,128]{1,0:T(8,128)(2,1)S(1)} %get-tuple-element.13.refs_0_), channel_id=1, source_target_pairs={{0,2},{1,3},{2,0},{3,1},{4,6},{5,7},{6,4},{7,5},{8,10},{9,11},{10,... | collective-permute-start | bytes 393224 | tf_op jit(solution)/shard_map/ppermute | solution.py:30
  52.6 9.7 %collective-permute-start.14 = (bf16[512,128]{1,0:T(8,128)(2,1)S(1)}, bf16[512,128]{1,0:T(8,128)(2,1)S(1)}, u32[]{:S(2)}, u32[]{:S(2)}) collective-permute-start(bf16[512,128]{1,0:T(8,128)(2,1)S(1)} %get-tuple-element.13.refs_0_), channel_id=1, source_target_pairs={{0,1},{1,0},{2,3},{3,2},{4,5},{5,4},{6,7},{7,6},{8,9},{9,8},{10,11... | collective-permute-start | bytes 393224 | tf_op jit(solution)/shard_map/ppermute | solution.py:30
  56.7 15.8 %collective-permute-start.19 = (bf16[512,128]{1,0:T(8,128)(2,1)S(1)}, bf16[512,128]{1,0:T(8,128)(2,1)S(1)}, u32[]{:S(2)}, u32[]{:S(2)}) collective-permute-start(bf16[512,128]{1,0:T(8,128)(2,1)S(1)} %attend.3.refs_1_), channel_id=1, source_target_pairs={{0,3},{1,2},{2,1},{3,0},{4,7},{5,6},{6,5},{7,4},{8,11},{9,10},{10,... | collective-permute-start | bytes 393224 | tf_op jit(solution)/shard_map/ppermute | solution.py:30
  59.0 7.0 %collective-permute-start.18 = (bf16[512,128]{1,0:T(8,128)(2,1)S(1)}, bf16[512,128]{1,0:T(8,128)(2,1)S(1)}, u32[]{:S(2)}, u32[]{:S(2)}) collective-permute-start(bf16[512,128]{1,0:T(8,128)(2,1)S(1)} %attend.3.refs_1_), channel_id=1, source_target_pairs={{0,1},{1,0},{2,3},{3,2},{4,5},{5,4},{6,7},{7,6},{8,9},{9,8},{10,11... | collective-permute-start | bytes 393224 | tf_op jit(solution)/shard_map/ppermute | solution.py:30
  60.2 11.5 %collective-permute-start.17 = (bf16[512,128]{1,0:T(8,128)(2,1)S(1)}, bf16[512,128]{1,0:T(8,128)(2,1)S(1)}, u32[]{:S(2)}, u32[]{:S(2)}) collective-permute-start(bf16[512,128]{1,0:T(8,128)(2,1)S(1)} %attend.3.refs_1_), channel_id=1, source_target_pairs={{0,2},{1,3},{2,0},{3,1},{4,6},{5,7},{6,4},{7,5},{8,10},{9,11},{10,... | collective-permute-start | bytes 393224 | tf_op jit(solution)/shard_map/ppermute | solution.py:30
